TPU v7x, 1024 devices: a whole 4x4x32 slice. The times are simulated.
1024 devices in a mesh: gx: 32 (over z_lo, core), gy: 8 (over z_hi, x), gz: 4 (over y).
Axes of the slice: x: 4, y: 4, z: 32 (z_hi: 2, z_lo: 16; z = z_hi * 16 + z_lo), core: 2. Of those that a mesh axis runs over, the one named last changes fastest.
Arguments:
- conserved_state: float32 [6, 128, 64, 480], P(None, 'gx', 'gy', 'gz'), as said below
Outputs:
- updated_state: float32 [6, 128, 64, 480], P(None, 'gx', 'gy', 'gz')
- next_timestep: float32 [], replicated
Inputs may be any that keep to these rules, and one draw needn't show every extreme that they name: `conserved_state`: component 0 is density within 0.5 to 3, components 1 to 3 are density times velocities each within -1 to 1, component 4 is total energy with pressure within 0.5 to 6, component 5 is density times a tracer fraction within 0 to 1.
All inputs are finite; a program needn't handle non-finite values.
Results may differ from a plain program's by a relative error of at most 0.0003.
Values sent between devices are 32-bit elements; how exact they have to be, the bound alone decides.
No kernel may reach another device: no remote copies, remote signals or barrier semaphores. Data moves between devices by JAX's collectives and lax.ppermute only.
A program may use at most 32 MiB of HBM per device.

v0:
```python
import functools

import jax
import jax.numpy as jnp
from jax import lax
from jax.sharding import Mesh
from jax.sharding import PartitionSpec as P

GHOST = 4
GX_GY_GZ = ("gx_0", "gx_1", "gy_0", "gy_1", "gz")
GY = ("gy_0", "gy_1")
GX = ("gx_0", "gx_1")


adiabatic = 5.0 / 3.0
courant = 0.3


def over_axes(array, axes):
    return functools.reduce(lax.pmax, axes, array)


def padded_2(block, sides, width):
    for axis, dim in sides:
        count = lax.axis_size(axis)
        forward = [(i, i + 1) for i in range(count - 1)]
        forward.append((count - 1, 0))
        backward = [(target, source) for source, target in forward]
        low = lax.ppermute(
            lax.slice_in_dim(block, block.shape[dim] - width, None, axis=dim), axis, forward
        )
        high = lax.ppermute(lax.slice_in_dim(block, 0, width, axis=dim), axis, backward)
        block = jnp.concatenate([low, block, high], axis=dim)
    return block


def window(values, axis_number, start, length):
    return lax.slice_in_dim(values, start, start + length, axis=axis_number)


def primitive_of(conserved_list):
    density = conserved_list[0]
    inverse = 1.0 / density
    velocity = [conserved_list[component] * inverse for component in (1, 2, 3)]
    kinetic = 0.5 * (
        conserved_list[1] * velocity[0]
        + conserved_list[2] * velocity[1]
        + conserved_list[3] * velocity[2]
    )
    pressure = (adiabatic - 1.0) * (conserved_list[4] - kinetic)
    return [density, velocity[0], velocity[1], velocity[2], pressure, conserved_list[5] * inverse]


def conserved_of(primitive):
    density = primitive[0]
    momenta = [density * primitive[component] for component in (1, 2, 3)]
    kinetic = 0.5 * (
        momenta[0] * primitive[1] + momenta[1] * primitive[2] + momenta[2] * primitive[3]
    )
    energy = primitive[4] / (adiabatic - 1.0) + kinetic
    return [density, momenta[0], momenta[1], momenta[2], energy, density * primitive[5]]


def fastest_signal(conserved_list):
    primitive = primitive_of(conserved_list)
    sound = jnp.sqrt(adiabatic * primitive[4] / primitive[0])
    speeds = jnp.maximum(
        jnp.maximum(jnp.abs(primitive[1]), jnp.abs(primitive[2])), jnp.abs(primitive[3])
    )
    return jnp.max(speeds + sound)


def parabola(centre, sweep_axis):
    extent = centre.shape[sweep_axis]
    count = extent - 5

    def offset_cells(offset):
        return window(centre, sweep_axis, 3 + offset, count)

    before_one = offset_cells(-1)
    middle = offset_cells(0)
    edge = (
        37.0 * (before_one + middle)
        - 8.0 * (offset_cells(-2) + offset_cells(1))
        + (offset_cells(-3) + offset_cells(2))
    ) / 60.0
    edge = jnp.clip(edge, jnp.minimum(before_one, middle), jnp.maximum(before_one, middle))
    lower = window(edge, sweep_axis, 0, count - 1)
    upper = window(edge, sweep_axis, 1, count - 1)
    inner = window(centre, sweep_axis, 3, count - 1)
    flatten = (upper - inner) * (inner - lower) <= 0.0
    spread = upper - lower
    skewed = spread * (inner - 0.5 * (lower + upper))
    limit = spread * spread / 6.0
    new_lower = jnp.where(
        flatten, inner, jnp.where(skewed > limit, 3.0 * inner - 2.0 * upper, lower)
    )
    new_upper = jnp.where(
        flatten, inner, jnp.where(skewed < -limit, 3.0 * inner - 2.0 * lower, upper)
    )
    return (new_lower, new_upper)


def traced_faces(primitive, sweep_axis, time_step):
    normal = 1 + sweep_axis
    extent = primitive[0].shape[sweep_axis]
    edges = [parabola(item, sweep_axis) for item in primitive]
    slopes = [pair[1] - pair[0] for pair in edges]
    inner = [window(item, sweep_axis, 3, extent - 6) for item in primitive]
    normal_vel = inner[normal]
    density = inner[0]
    rates = [-(normal_vel * slopes[0] + density * slopes[normal])]
    for component in (1, 2, 3):
        if component == normal:
            rates.append(-(normal_vel * slopes[normal] + slopes[4] / density))
        else:
            rates.append(-normal_vel * slopes[component])
    rates.append(-(adiabatic * inner[4] * slopes[normal] + normal_vel * slopes[4]))
    rates.append(-normal_vel * slopes[5])
    lower_faces = [
        edges[component][0] + 0.5 * time_step * rates[component] for component in range(6)
    ]
    upper_faces = [
        edges[component][1] + 0.5 * time_step * rates[component] for component in range(6)
    ]
    return (lower_faces, upper_faces)


def physical_flux(primitive, conserved_list, normal):
    normal_vel = primitive[normal]
    result = [item * normal_vel for item in conserved_list]
    result[normal] = result[normal] + primitive[4]
    result[4] = result[4] + primitive[4] * normal_vel
    return result


def star_state(primitive, conserved_list, outer_speed, middle_speed, normal):
    mass_rate = primitive[0] * (outer_speed - primitive[normal])
    factor = mass_rate / (outer_speed - middle_speed)
    result = [factor * primitive[component] for component in range(6)]
    result[0] = factor
    result[normal] = factor * middle_speed
    result[4] = factor * (
        conserved_list[4] / primitive[0]
        + (middle_speed - primitive[normal]) * (middle_speed + primitive[4] / mass_rate)
    )
    return result


def hllc_flux(left, right, sweep_axis):
    normal = 1 + sweep_axis
    sound_left = jnp.sqrt(adiabatic * left[4] / left[0])
    sound_right = jnp.sqrt(adiabatic * right[4] / right[0])
    low_speed = jnp.minimum(left[normal] - sound_left, right[normal] - sound_right)
    high_speed = jnp.maximum(left[normal] + sound_left, right[normal] + sound_right)
    mass_left = left[0] * (low_speed - left[normal])
    mass_right = right[0] * (high_speed - right[normal])
    middle = (right[4] - left[4] + mass_left * left[normal] - mass_right * right[normal]) / (
        mass_left - mass_right
    )
    left_state = conserved_of(left)
    right_state = conserved_of(right)
    flux_left = physical_flux(left, left_state, normal)
    flux_right = physical_flux(right, right_state, normal)
    star_left = star_state(left, left_state, low_speed, middle, normal)
    star_right = star_state(right, right_state, high_speed, middle, normal)
    result = []
    for component in range(6):
        left_star_flux = flux_left[component] + low_speed * (
            star_left[component] - left_state[component]
        )
        right_star_flux = flux_right[component] + high_speed * (
            star_right[component] - right_state[component]
        )
        chosen = jnp.where(high_speed > 0.0, right_star_flux, flux_right[component])
        chosen = jnp.where(middle >= 0.0, left_star_flux, chosen)
        chosen = jnp.where(low_speed >= 0.0, flux_left[component], chosen)
        result.append(chosen)
    return result


def face_fluxes(lower_faces, upper_faces, sweep_axis):
    extent = lower_faces[0].shape[sweep_axis]
    from_below = [window(item, sweep_axis, 0, extent - 1) for item in upper_faces]
    from_above = [window(item, sweep_axis, 1, extent - 1) for item in lower_faces]
    return hllc_flux(from_below, from_above, sweep_axis)


def hydro_step(padded, time_step):
    conserved_list = [padded[component] for component in range(6)]
    extents = padded.shape[1:]
    owned = [extent - 2 * GHOST for extent in extents]
    primitive = primitive_of(conserved_list)
    faces = [traced_faces(primitive, sweep_axis, time_step) for sweep_axis in range(3)]
    predicted = [
        face_fluxes(faces[sweep_axis][0], faces[sweep_axis][1], sweep_axis)
        for sweep_axis in range(3)
    ]
    final_fluxes = []
    for sweep_axis in range(3):
        lower_faces, upper_faces = faces[sweep_axis]
        lower_state = conserved_of(lower_faces)
        upper_state = conserved_of(upper_faces)
        for other_axis in range(3):
            if other_axis != sweep_axis:
                for component in range(6):
                    lower_state[component] = window(
                        lower_state[component], other_axis, GHOST, owned[other_axis]
                    )
                    upper_state[component] = window(
                        upper_state[component], other_axis, GHOST, owned[other_axis]
                    )
        for other_axis in range(3):
            if other_axis != sweep_axis:
                for component in range(6):
                    flux_other = predicted[other_axis][component]
                    divergence = (
                        0.5
                        * time_step
                        * (
                            window(flux_other, other_axis, 1, owned[other_axis])
                            - window(flux_other, other_axis, 0, owned[other_axis])
                        )
                    )
                    for third_axis in range(3):
                        if third_axis == sweep_axis:
                            divergence = window(divergence, third_axis, 3, extents[third_axis] - 6)
                        elif third_axis != other_axis:
                            divergence = window(divergence, third_axis, GHOST, owned[third_axis])
                    lower_state[component] = lower_state[component] - divergence
                    upper_state[component] = upper_state[component] - divergence
        lower_prim = primitive_of(lower_state)
        upper_prim = primitive_of(upper_state)
        final_fluxes.append(face_fluxes(lower_prim, upper_prim, sweep_axis))
    updated = []
    for component in range(6):
        total = conserved_list[component][GHOST:-GHOST, GHOST:-GHOST, GHOST:-GHOST]
        for sweep_axis in range(3):
            flux_here = final_fluxes[sweep_axis][component]
            total = total - time_step * (
                window(flux_here, sweep_axis, 1, owned[sweep_axis])
                - window(flux_here, sweep_axis, 0, owned[sweep_axis])
            )
        updated.append(total)
    return jnp.stack(updated)


def body(conserved_state):
    own_cells = [conserved_state[component] for component in range(6)]
    signal_now = over_axes(fastest_signal(own_cells), GX_GY_GZ)
    time_step = courant / signal_now
    padded = padded_2(conserved_state, (("gz", 3),), GHOST)
    padded = padded_2(padded, ((GY, 2),), GHOST)
    padded = padded_2(padded, ((GX, 1),), GHOST)
    updated = hydro_step(padded, time_step)
    new_cells = [updated[component] for component in range(6)]
    signal_next = over_axes(fastest_signal(new_cells), GX_GY_GZ)
    return (updated, courant / signal_next)


def solution(mesh):
    finer = Mesh(
        mesh.devices.reshape(16, 2, 2, 4, mesh.shape["gz"]), ("gx_0", "gx_1", "gy_0", "gy_1", "gz")
    )
    in_specs = (P(None, GX, GY, "gz"),)
    out_specs = (P(None, GX, GY, "gz"), P())
    return jax.shard_map(body, mesh=finer, in_specs=in_specs, out_specs=out_specs, check_vma=False)
```

profile of v0, /device:TPU:1, one launch (start us, length us, event | category | flops | bytes accessed | tf_op | source)
XLA Modules:
  0.0 367.3 jit_solution(1305983094790338408)
XLA Ops:
  0.6 1.1 fusion.428
  1.8 4.0 %collective-permute-start = (f32[6,4,8,4]{3,2,1,0:T(8,128)S(1)}, f32[6,4,8,4]{3,2,1,0:T(8,128)S(1)}, u32[]{:S(2)}, u32[]{:S(2)}) collective-permute-start(f32[6,4,8,4]{3,2,1,0:T(8,128)S(1)} %get-tuple-element.267), channel_id=1, source_target_pairs={{0,1},{1,2},{2,3},{3,0},{4,5},{5,6},{6,7},{7,4},{8,9},{9,10},{10,1... | collective-permute-start | bytes 9224 | tf_op jit(solution)/shard_map/ppermute | solution.py:29
  5.8 3.4 collective-permute-start.1
  9.2 1.9 collective-permute-done.1
  11.2 0.1 pad_maximum_fusion.2
  11.3 3.1 collective-permute-start.2
  14.4 29.7 %collective-permute-start.3 = (f32[6,4,4,128]{3,2,1,0:T(4,128)S(1)}, f32[6,4,4,128]{3,2,1,0:T(4,128)S(1)}, u32[]{:S(2)}, u32[]{:S(2)}) collective-permute-start(f32[6,4,4,128]{3,2,1,0:T(4,128)S(1)} %get-tuple-element.266), channel_id=1, source_target_pairs={{4,0},{8,4},{12,8},{16,12},{20,16},{24,20},{28,24},{0,28},{5,1},{9... | collective-permute-start | bytes 147464 | tf_op jit(solution)/shard_map/ppermute | solution.py:32
  44.1 1.1 collective-permute-done.3
  45.3 0.2 pad_maximum_fusion.1
  45.5 9.9 %collective-permute-start.5 = (f32[6,4,16,128]{3,2,1,0:T(8,128)S(1)}, f32[6,4,16,128]{3,2,1,0:T(8,128)S(1)}, u32[]{:S(2)}, u32[]{:S(2)}) collective-permute-start(f32[6,4,16,128]{3,2,1,0:T(8,128)S(1)} %pad_maximum_fusion.1), channel_id=1, source_target_pairs={{32,0},{64,32},{96,64},{128,96},{160,128},{192,160},{224,192},{256... | collective-permute-start | bytes 589832 | tf_op jit(solution)/shard_map/ppermute | solution.py:32
  55.4 1.9 collective-permute-start.4
  57.3 0.6 fusion.341
  58.0 107.9 %pmax.70 = f32[]{:T(128)} all-reduce(f32[]{:T(128)} %fusion.341), channel_id=1, replica_groups=mesh['gx_0'=16,'gx_1'=2,'gy_0'=2,'gy_1'=4,'gz'=4] {'gx_0'}, use_global_device_ids=true, to_apply=%region_1.0 | all-reduce | flops 1 | bytes 8 | tf_op jit(solution)/shard_map/pmax | solution.py:20
  165.9 3.1 pmax.71
  169.0 22.7 %pmax.72 = f32[]{:T(128)} all-reduce(f32[]{:T(128)} %pmax.71), channel_id=1, replica_groups=mesh['gx_0'=16,'gx_1'=2,'gy_0'=2,'gy_1'=4,'gz'=4] {'gy_0'}, use_global_device_ids=true, to_apply=%region_3.0 | all-reduce | flops 1 | bytes 8 | tf_op jit(solution)/shard_map/pmax | solution.py:20
  191.7 19.1 %pmax.73 = f32[]{:T(128)} all-reduce(f32[]{:T(128)} %pmax.72), channel_id=1, replica_groups=mesh['gx_0'=16,'gx_1'=2,'gy_0'=2,'gy_1'=4,'gz'=4] {'gy_1'}, use_global_device_ids=true, to_apply=%region_4.0 | all-reduce | flops 1 | bytes 8 | tf_op jit(solution)/shard_map/pmax | solution.py:20
  210.8 9.2 %pmax.74 = f32[]{:T(128)} all-reduce(f32[]{:T(128)} %pmax.73), channel_id=1, replica_groups=mesh['gx_0'=16,'gx_1'=2,'gy_0'=2,'gy_1'=4,'gz'=4] {'gz'}, use_global_device_ids=true, to_apply=%region_5.0 | all-reduce | flops 1 | bytes 8 | tf_op jit(solution)/shard_map/pmax | solution.py:20
  220.7 0.2 pad_maximum_fusion
  221.1 0.2 fusion.75
  221.4 0.2 fusion.168
  221.6 0.2 fusion.385
  222.2 0.1 fusion.188
  222.5 0.2 fusion.63
  222.7 0.1 fusion.87
  222.8 0.3 fusion.28
  223.2 0.1 fusion.34
  223.3 0.3 fusion.57
  223.6 0.1 fusion.81
  223.8 0.1 fusion.389
  223.9 0.1 fusion.184
  224.0 0.1 fusion.182
  224.3 0.4 fusion.129
  224.7 0.3 fusion.410
  225.0 0.2 fusion.416
  225.2 0.2 fusion.419
  225.5 0.3 fusion.23
  225.9 0.3 fusion.19
  226.2 0.4 fusion.11
  227.2 0.3 fusion.397
  227.5 0.2 fusion.403
  227.7 0.3 fusion.401
  228.0 0.2 fusion.423
  228.5 0.1 broadcast_divide_fusion.2
  228.7 0.1 fusion.367
  228.8 0.1 fusion.366
  229.0 0.2 fusion.213
  229.2 0.1 fusion.205
  229.4 0.3 fusion.21
  229.6 0.3 fusion.9
  230.0 0.3 fusion.13
  230.9 0.1 fusion.360
  231.1 0.1 fusion.361
  231.2 0.1 fusion.253
  231.6 0.1 fusion.355
  231.7 0.2 fusion.279
  231.8 0.1 fusion.271
  232.0 0.1 fusion.269
  232.1 0.7 add_reduce_fusion
  232.8 80.9 %pmax.75 = f32[]{:T(128)} all-reduce(f32[]{:T(128)} %get-tuple-element.2), channel_id=1, replica_groups=mesh['gx_0'=16,'gx_1'=2,'gy_0'=2,'gy_1'=4,'gz'=4] {'gx_0'}, use_global_device_ids=true, to_apply=%region_7.8 | all-reduce | flops 1 | bytes 8 | tf_op jit(solution)/shard_map/pmax | solution.py:20
  313.7 15.1 %pmax.76 = f32[]{:T(128)} all-reduce(f32[]{:T(128)} %pmax.75), channel_id=1, replica_groups=mesh['gx_0'=16,'gx_1'=2,'gy_0'=2,'gy_1'=4,'gz'=4] {'gx_1'}, use_global_device_ids=true, to_apply=%region_8.9 | all-reduce | flops 1 | bytes 8 | tf_op jit(solution)/shard_map/pmax | solution.py:20
  328.8 22.7 %pmax.77 = f32[]{:T(128)} all-reduce(f32[]{:T(128)} %pmax.76), channel_id=1, replica_groups=mesh['gx_0'=16,'gx_1'=2,'gy_0'=2,'gy_1'=4,'gz'=4] {'gy_0'}, use_global_device_ids=true, to_apply=%region_9.10 | all-reduce | flops 1 | bytes 8 | tf_op jit(solution)/shard_map/pmax | solution.py:20
  351.5 6.6 %pmax.78 = f32[]{:T(128)} all-reduce(f32[]{:T(128)} %pmax.77), channel_id=1, replica_groups=mesh['gx_0'=16,'gx_1'=2,'gy_0'=2,'gy_1'=4,'gz'=4] {'gy_1'}, use_global_device_ids=true, to_apply=%region_10.11 | all-reduce | flops 1 | bytes 8 | tf_op jit(solution)/shard_map/pmax | solution.py:20
  358.1 6.6 %pmax.79 = f32[]{:T(128)} all-reduce(f32[]{:T(128)} %pmax.78), channel_id=1, replica_groups=mesh['gx_0'=16,'gx_1'=2,'gy_0'=2,'gy_1'=4,'gz'=4] {'gz'}, use_global_device_ids=true, to_apply=%region_11.12 | all-reduce | flops 1 | bytes 8 | tf_op jit(solution)/shard_map/pmax | solution.py:20
  365.6 0.6 copy-done.1
  (74 shorter events, 3.2 us)
Async XLA Ops:
  0.6 10.5 %copy-start = (f32[6,4,8,120]{3,2,1,0:T(8,128)S(1)}, f32[6,4,8,120]{3,2,1,0:T(8,128)}, u32[]{:S(2)}) copy-start(f32[6,4,8,120]{3,2,1,0:T(8,128)} %param.1) | copy-start | bytes 276484
  1.8 7.5 %collective-permute-start = (f32[6,4,8,4]{3,2,1,0:T(8,128)S(1)}, f32[6,4,8,4]{3,2,1,0:T(8,128)S(1)}, u32[]{:S(2)}, u32[]{:S(2)}) collective-permute-start(f32[6,4,8,4]{3,2,1,0:T(8,128)S(1)} %get-tuple-element.267), channel_id=1, source_target_pairs={{0,1},{1,2},{2,3},{3,0},{4,5},{5,6},{6,7},{7,4},{8,9},{9,10},{10,1... | collective-permute-start | bytes 9224 | tf_op jit(solution)/shard_map/ppermute | solution.py:29
  5.8 5.4 %collective-permute-start.1 = (f32[6,4,8,4]{3,2,1,0:T(8,128)S(1)}, f32[6,4,8,4]{3,2,1,0:T(8,128)S(1)}, u32[]{:S(2)}, u32[]{:S(2)}) collective-permute-start(f32[6,4,8,4]{3,2,1,0:T(8,128)S(1)} %get-tuple-element.268), channel_id=1, source_target_pairs={{1,0},{2,1},{3,2},{0,3},{5,4},{6,5},{7,6},{4,7},{9,8},{10,9},{11,1... | collective-permute-start | bytes 9224 | tf_op jit(solution)/shard_map/ppermute | solution.py:32
  11.3 32.8 %collective-permute-start.2 = (f32[6,4,4,128]{3,2,1,0:T(4,128)S(1)}, f32[6,4,4,128]{3,2,1,0:T(4,128)S(1)}, u32[]{:S(2)}, u32[]{:S(2)}) collective-permute-start(f32[6,4,4,128]{3,2,1,0:T(4,128)S(1)} %get-tuple-element.265), channel_id=1, source_target_pairs={{0,4},{4,8},{8,12},{12,16},{16,20},{20,24},{24,28},{28,0},{1,5},{5... | collective-permute-start | bytes 147464 | tf_op jit(solution)/shard_map/ppermute | solution.py:29
  14.4 30.9 %collective-permute-start.3 = (f32[6,4,4,128]{3,2,1,0:T(4,128)S(1)}, f32[6,4,4,128]{3,2,1,0:T(4,128)S(1)}, u32[]{:S(2)}, u32[]{:S(2)}) collective-permute-start(f32[6,4,4,128]{3,2,1,0:T(4,128)S(1)} %get-tuple-element.266), channel_id=1, source_target_pairs={{4,0},{8,4},{12,8},{16,12},{20,16},{24,20},{28,24},{0,28},{5,1},{9... | collective-permute-start | bytes 147464 | tf_op jit(solution)/shard_map/ppermute | solution.py:32
  45.5 175.2 %collective-permute-start.5 = (f32[6,4,16,128]{3,2,1,0:T(8,128)S(1)}, f32[6,4,16,128]{3,2,1,0:T(8,128)S(1)}, u32[]{:S(2)}, u32[]{:S(2)}) collective-permute-start(f32[6,4,16,128]{3,2,1,0:T(8,128)S(1)} %pad_maximum_fusion.1), channel_id=1, source_target_pairs={{32,0},{64,32},{96,64},{128,96},{160,128},{192,160},{224,192},{256... | collective-permute-start | bytes 589832 | tf_op jit(solution)/shard_map/ppermute | solution.py:32
  55.4 165.3 %collective-permute-start.4 = (f32[6,4,16,128]{3,2,1,0:T(8,128)S(1)}, f32[6,4,16,128]{3,2,1,0:T(8,128)S(1)}, u32[]{:S(2)}, u32[]{:S(2)}) collective-permute-start(f32[6,4,16,128]{3,2,1,0:T(8,128)S(1)} %pad_maximum_fusion.1), channel_id=1, source_target_pairs={{0,32},{32,64},{64,96},{96,128},{128,160},{160,192},{192,224},{224... | collective-permute-start | bytes 589832 | tf_op jit(solution)/shard_map/ppermute | solution.py:29
  365.6 0.6 copy-start.1
where the time goes:
time: 372 us; the launch traced here: 367 us
  blocking collectives  294 us (79%)
  starting transfers between devices  52 us (14%)
  other arithmetic  11.3 us (3%)
  between operations  3.87 us (1%)
    pmax x10, blocking collectives, over_axes(): return functools.reduce(lax.pmax, axes, array)  294 us
    ppermute x3, starting transfers between devices, padded_2(): lax.ppermute(lax.slice_in_dim(block, 0, width, axis=dim), axis, backward)  43 us
    ppermute x3, starting transfers between devices, padded_2(): lax.ppermute(lax.slice_in_dim(block, block.shape[dim] - width, None, axis...  9.06 us
  transfers between devices with their start and end apart: 6, of which 3 were waited for; matrix products, arithmetic and copies ran while one was open for 0% of the time, Pallas kernels for 0%

commit v1 on v0

--- a/solution.py
+++ b/solution.py
@@ -1,5 +1,3 @@
-import functools
-
 import jax
 import jax.numpy as jnp
 from jax import lax
@@ -7,31 +5,47 @@
 from jax.sharding import PartitionSpec as P
 
 GHOST = 4
-GX_GY_GZ = ("gx_0", "gx_1", "gy_0", "gy_1", "gz")
-GY = ("gy_0", "gy_1")
-GX = ("gx_0", "gx_1")
-
+ALL = ("zl", "c", "zh", "x", "y")
+PLANE = ("c", "x", "y")
+COLUMN = ("zl", "zh")
+GX = ("zl", "c")
+GY = ("zh", "x")
+GZ = ("y",)
 
 adiabatic = 5.0 / 3.0
 courant = 0.3
 
 
-def over_axes(array, axes):
-    return functools.reduce(lax.pmax, axes, array)
-
-
-def padded_2(block, sides, width):
-    for axis, dim in sides:
-        count = lax.axis_size(axis)
-        forward = [(i, i + 1) for i in range(count - 1)]
-        forward.append((count - 1, 0))
-        backward = [(target, source) for source, target in forward]
-        low = lax.ppermute(
-            lax.slice_in_dim(block, block.shape[dim] - width, None, axis=dim), axis, forward
-        )
-        high = lax.ppermute(lax.slice_in_dim(block, 0, width, axis=dim), axis, backward)
-        block = jnp.concatenate([low, block, high], axis=dim)
-    return block
+def over_all(value):
+    for axes in (PLANE, COLUMN):
+        count = lax.axis_size(axes)
+        everyone = lax.all_to_all(jnp.broadcast_to(value, (count,)), axes, 0, 0, tiled=True)
+        value = jnp.max(everyone)
+    return value
+
+
+def swaps(count):
+    even = [(i, i ^ 1) for i in range(count)]
+    odd = [(i, (i + 1) % count if i % 2 else (i - 1) % count) for i in range(count)]
+    return even, odd
+
+
+def exchange(block, axes, parity, dim, width):
+    even, odd = swaps(lax.axis_size(axes))
+    first = lax.slice_in_dim(block, 0, width, axis=dim)
+    last = lax.slice_in_dim(block, block.shape[dim] - width, None, axis=dim)
+    if block.shape[dim] == width:
+        to_even, to_odd = block, block
+    else:
+        to_even, to_odd = jnp.where(parity, first, last), jnp.where(parity, last, first)
+    by_even = lax.ppermute(to_even, axes, even)
+    by_odd = lax.ppermute(to_odd, axes, odd)
+    return jnp.where(parity, by_even, by_odd), jnp.where(parity, by_odd, by_even)
+
+
+def padded(block, axes, parity, dim, width):
+    low, high = exchange(block, axes, parity, dim, width)
+    return jnp.concatenate([low, block, high], axis=dim)
 
 
 def window(values, axis_number, start, length):
@@ -247,21 +261,20 @@
 
 def body(conserved_state):
     own_cells = [conserved_state[component] for component in range(6)]
-    signal_now = over_axes(fastest_signal(own_cells), GX_GY_GZ)
+    signal_now = over_all(fastest_signal(own_cells))
     time_step = courant / signal_now
-    padded = padded_2(conserved_state, (("gz", 3),), GHOST)
-    padded = padded_2(padded, ((GY, 2),), GHOST)
-    padded = padded_2(padded, ((GX, 1),), GHOST)
-    updated = hydro_step(padded, time_step)
+    block = padded(conserved_state, GZ, lax.axis_index("y") % 2 == 1, 3, GHOST)
+    block = padded(block, GY, lax.axis_index("x") % 2 == 1, 2, GHOST)
+    block = padded(block, GX, lax.axis_index("c") == 1, 1, GHOST)
+    updated = hydro_step(block, time_step)
     new_cells = [updated[component] for component in range(6)]
-    signal_next = over_axes(fastest_signal(new_cells), GX_GY_GZ)
+    signal_next = over_all(fastest_signal(new_cells))
     return (updated, courant / signal_next)
 
 
 def solution(mesh):
-    finer = Mesh(
-        mesh.devices.reshape(16, 2, 2, 4, mesh.shape["gz"]), ("gx_0", "gx_1", "gy_0", "gy_1", "gz")
-    )
-    in_specs = (P(None, GX, GY, "gz"),)
-    out_specs = (P(None, GX, GY, "gz"), P())
-    return jax.shard_map(body, mesh=finer, in_specs=in_specs, out_specs=out_specs, check_vma=False)
+    finer = Mesh(mesh.devices.reshape(16, 2, 2, 4, 4), ALL)
+    spec = P(None, GX, GY, GZ)
+    return jax.shard_map(
+        body, mesh=finer, in_specs=(spec,), out_specs=(spec, P()), check_vma=False
+    )

time: 372 us -> 176 us (0.47); the launches traced: 367 us -> 176 us
  blocking collectives: 294 us -> 12 us
  waiting for transfers between devices: 3.15 us -> 52.5 us
  starting transfers between devices: 52 us -> 86.6 us
    pmax x10 -> x0, blocking collectives: 294 us -> none  [over_axes(): return functools.reduce(lax.pmax, axes, array)]
    all_to_all x0 -> x3, waiting for transfers between devices: none -> 47.8 us  [over_all(): lax.all_to_all(jnp.broadcast_to(value, (count,)), axes, 0, 0, tiled=True)]
    all_to_all x0 -> x3, starting transfers between devices: none -> 23.9 us  [over_all(): lax.all_to_all(jnp.broadcast_to(value, (count,)), axes, 0, 0, tiled=True)]
    all_to_all x0 -> x1, blocking collectives: none -> 12 us  [over_all(): lax.all_to_all(jnp.broadcast_to(value, (count,)), axes, 0, 0, tiled=True)]
    ppermute x6, starting transfers between devices: 52 us -> 62.7 us  [the longest x3 39.4 us: exchange(): by_odd = lax.ppermute(to_odd, axes, odd)]
    broadcast_in_dim x0 -> x4, local copies, waits for them, and re-layouts: none -> 4.42 us  [over_all(): jnp.broadcast_to(value, (count,))]
  transfers between devices with their start and end apart: 6 -> 9, of which waited for: 3 -> 5; matrix products, arithmetic and copies ran while one was open for 0% -> 2% of each run, Pallas kernels for 0% -> 0%
where the time goes in v1:
time: 176 us
  starting transfers between devices  86.6 us (49%)
  waiting for transfers between devices  52.5 us (30%)
  other arithmetic  14.9 us (8%)
  blocking collectives  12 us (7%)
  local copies, waits for them, and re-layouts  5.73 us (3%)
  between operations  3.98 us (2%)
    all_to_all x3, waiting for transfers between devices, over_all(): lax.all_to_all(jnp.broadcast_to(value, (count,)), axes, 0, 0, tiled=True)  47.8 us
    ppermute x3, starting transfers between devices, exchange(): by_odd = lax.ppermute(to_odd, axes, odd)  39.4 us
    all_to_all x3, starting transfers between devices, over_all(): lax.all_to_all(jnp.broadcast_to(value, (count,)), axes, 0, 0, tiled=True)  23.9 us
    ppermute x3, starting transfers between devices, exchange(): by_even = lax.ppermute(to_even, axes, even)  23.4 us
    all_to_all x1, blocking collectives, over_all(): lax.all_to_all(jnp.broadcast_to(value, (count,)), axes, 0, 0, tiled=True)  12 us
    ppermute x3, waiting for transfers between devices, exchange(): by_odd = lax.ppermute(to_odd, axes, odd)  4.69 us
    broadcast_in_dim x4, local copies, waits for them, and re-layouts, over_all(): jnp.broadcast_to(value, (count,))  4.42 us
  transfers between devices with their start and end apart: 9, of which 5 were waited for; matrix products, arithmetic and copies ran while one was open for 2% of the time, Pallas kernels for 0%

profile of v1, /device:TPU:1, one launch (start us, length us, event | category | flops | bytes accessed | tf_op | source)
XLA Modules:
  0.0 175.6 jit_solution(4607836759497759554)
XLA Ops:
  0.6 1.1 slice_select_fusion.1
  1.7 4.0 %collective-permute-start = (f32[6,4,8,4]{3,2,1,0:T(8,128)S(1)}, f32[6,4,8,4]{3,2,1,0:T(8,128)S(1)}, u32[]{:S(2)}, u32[]{:S(2)}) collective-permute-start(f32[6,4,8,4]{3,2,1,0:T(8,128)S(1)} %get-tuple-element.273), channel_id=1, source_target_pairs={{0,1},{1,0},{2,3},{3,2},{4,5},{5,4},{6,7},{7,6},{8,9},{9,8},{10,11... | collective-permute-start | bytes 9224 | tf_op jit(solution)/shard_map/ppermute | solution.py:41
  5.7 3.8 %collective-permute-start.1 = (f32[6,4,8,4]{3,2,1,0:T(8,128)S(1)}, f32[6,4,8,4]{3,2,1,0:T(8,128)S(1)}, u32[]{:S(2)}, u32[]{:S(2)}) collective-permute-start(f32[6,4,8,4]{3,2,1,0:T(8,128)S(1)} %get-tuple-element.274), channel_id=1, source_target_pairs={{0,3},{1,2},{2,1},{3,0},{4,7},{5,6},{6,5},{7,4},{8,11},{9,10},{10,... | collective-permute-start | bytes 9224 | tf_op jit(solution)/shard_map/ppermute | solution.py:42
  9.6 2.7 %collective-permute-done.1 = f32[6,4,8,4]{3,2,1,0:T(8,128)S(1)} collective-permute-done((f32[6,4,8,4]{3,2,1,0:T(8,128)S(1)}, f32[6,4,8,4]{3,2,1,0:T(8,128)S(1)}, u32[]{:S(2)}, u32[]{:S(2)}) %collective-permute-start.1) | collective-permute-done | bytes 3104 | tf_op jit(solution)/shard_map/ppermute | solution.py:42
  12.3 0.1 pad_maximum_fusion.2
  12.5 3.1 %collective-permute-start.2 = (f32[6,4,4,128]{3,2,1,0:T(4,128)S(1)}, f32[6,4,4,128]{3,2,1,0:T(4,128)S(1)}, u32[]{:S(2)}, u32[]{:S(2)}) collective-permute-start(f32[6,4,4,128]{3,2,1,0:T(4,128)S(1)} %get-tuple-element.271), channel_id=1, source_target_pairs={{0,4},{4,0},{8,12},{12,8},{16,20},{20,16},{24,28},{28,24},{1,5},{5... | collective-permute-start | bytes 147464 | tf_op jit(solution)/shard_map/ppermute | solution.py:41
  15.6 30.2 %collective-permute-start.3 = (f32[6,4,4,128]{3,2,1,0:T(4,128)S(1)}, f32[6,4,4,128]{3,2,1,0:T(4,128)S(1)}, u32[]{:S(2)}, u32[]{:S(2)}) collective-permute-start(f32[6,4,4,128]{3,2,1,0:T(4,128)S(1)} %get-tuple-element.272), channel_id=1, source_target_pairs={{0,28},{4,8},{8,4},{12,16},{16,12},{20,24},{24,20},{28,0},{1,29},{... | collective-permute-start | bytes 147464 | tf_op jit(solution)/shard_map/ppermute | solution.py:42
  45.9 2.0 %collective-permute-done.3 = f32[6,4,4,128]{3,2,1,0:T(4,128)S(1)} collective-permute-done((f32[6,4,4,128]{3,2,1,0:T(4,128)S(1)}, f32[6,4,4,128]{3,2,1,0:T(4,128)S(1)}, u32[]{:S(2)}, u32[]{:S(2)}) %collective-permute-start.3) | collective-permute-done | bytes 49184 | tf_op jit(solution)/shard_map/ppermute | solution.py:42
  47.8 0.2 pad_maximum_fusion.1
  48.0 5.3 %collective-permute-start.5 = (f32[6,4,16,128]{3,2,1,0:T(8,128)S(1)}, f32[6,4,16,128]{3,2,1,0:T(8,128)S(1)}, u32[]{:S(2)}, u32[]{:S(2)}) collective-permute-start(f32[6,4,16,128]{3,2,1,0:T(8,128)S(1)} %pad_maximum_fusion.1), channel_id=1, source_target_pairs={{0,992},{32,64},{64,32},{96,128},{128,96},{160,192},{192,160},{224... | collective-permute-start | bytes 589832 | tf_op jit(solution)/shard_map/ppermute | solution.py:42
  53.3 16.2 %collective-permute-start.4 = (f32[6,4,16,128]{3,2,1,0:T(8,128)S(1)}, f32[6,4,16,128]{3,2,1,0:T(8,128)S(1)}, u32[]{:S(2)}, u32[]{:S(2)}) collective-permute-start(f32[6,4,16,128]{3,2,1,0:T(8,128)S(1)} %pad_maximum_fusion.1), channel_id=1, source_target_pairs={{0,32},{32,0},{64,96},{96,64},{128,160},{160,128},{192,224},{224,1... | collective-permute-start | bytes 589832 | tf_op jit(solution)/shard_map/ppermute | solution.py:41
  69.6 0.6 fusion.341
  70.2 0.7 broadcast_in_dim.12
  70.9 12.0 %all_to_all.24 = f32[32,1,1]{2,1,0:T(1,128)S(1)} all-to-all(f32[32,1,1]{2,1,0:T(1,128)S(1)} %broadcast_in_dim.12), channel_id=1, replica_groups=mesh['zl'=16,'c'=2,'zh'=2,'x'=4,'y'=4] {'c','x','y'}, dimensions={0} | all-to-all | bytes 256 | tf_op jit(solution)/shard_map/all_to_all | solution.py:22
  82.8 0.6 reduce_max.55
  83.4 1.3 broadcast_in_dim.13
  84.7 14.3 %all-to-all-start.1 = ((f32[32,1,1]{2,1,0:T(1,128)}), f32[32,1,1]{2,1,0:T(1,128)S(1)}, u32[]{:S(2)}, u32[]{:S(2)}) async-start(f32[32,1,1]{2,1,0:T(1,128)} %broadcast_in_dim.13), calls=%async_computation.1 | async-start | bytes 32768 | tf_op jit(solution)/shard_map/all_to_all | solution.py:22
  99.0 20.6 %all-to-all-done.1 = f32[32,1,1]{2,1,0:T(1,128)S(1)} async-done(((f32[32,1,1]{2,1,0:T(1,128)}), f32[32,1,1]{2,1,0:T(1,128)S(1)}, u32[]{:S(2)}, u32[]{:S(2)}) %all-to-all-start.1) | async-done | bytes 160 | tf_op jit(solution)/shard_map/all_to_all | solution.py:22
  119.6 0.6 reduce_max.56
  121.0 0.2 fusion.168
  121.2 0.2 pad_maximum_fusion
  121.5 0.2 fusion.75
  121.9 0.2 fusion.385
  122.5 0.1 fusion.188
  122.8 0.2 fusion.63
  123.0 0.1 fusion.87
  123.1 0.3 fusion.28
  123.5 0.1 fusion.34
  123.6 0.3 fusion.57
  123.9 0.1 fusion.81
  124.3 0.1 fusion.182
  124.6 0.4 fusion.129
  125.0 0.3 fusion.410
  125.3 0.2 fusion.416
  125.5 0.2 fusion.419
  125.8 0.3 fusion.23
  126.2 0.3 fusion.19
  126.5 0.4 fusion.11
  127.5 0.3 fusion.397
  127.8 0.2 fusion.403
  128.0 0.3 fusion.401
  128.3 0.2 fusion.423
  128.8 0.1 broadcast_divide_fusion.2
  129.0 0.1 fusion.367
  129.1 0.1 fusion.366
  129.3 0.2 fusion.213
  129.5 0.1 fusion.205
  129.7 0.2 fusion.21
  129.9 0.3 fusion.9
  130.3 0.3 fusion.13
  131.2 0.1 fusion.360
  131.4 0.1 fusion.361
  131.5 0.1 fusion.253
  132.0 0.2 fusion.279
  132.1 0.1 fusion.271
  132.4 0.7 add_reduce_fusion
  133.1 1.3 broadcast_in_dim.14
  134.4 5.8 %all-to-all-start.2 = ((f32[32,1,1]{2,1,0:T(1,128)}), f32[32,1,1]{2,1,0:T(1,128)S(1)}, u32[]{:S(2)}, u32[]{:S(2)}) async-start(f32[32,1,1]{2,1,0:T(1,128)} %broadcast_in_dim.14), calls=%async_computation.2 | async-start | bytes 32768 | tf_op jit(solution)/shard_map/all_to_all | solution.py:22
  140.2 6.7 %all-to-all-done.2 = f32[32,1,1]{2,1,0:T(1,128)S(1)} async-done(((f32[32,1,1]{2,1,0:T(1,128)}), f32[32,1,1]{2,1,0:T(1,128)S(1)}, u32[]{:S(2)}, u32[]{:S(2)}) %all-to-all-start.2) | async-done | bytes 160 | tf_op jit(solution)/shard_map/all_to_all | solution.py:22
  146.9 0.6 reduce_max.58
  147.5 1.3 broadcast_in_dim.15
  148.8 3.8 %all-to-all-start.3 = ((f32[32,1,1]{2,1,0:T(1,128)}), f32[32,1,1]{2,1,0:T(1,128)S(1)}, u32[]{:S(2)}, u32[]{:S(2)}) async-start(f32[32,1,1]{2,1,0:T(1,128)} %broadcast_in_dim.15), calls=%async_computation.3 | async-start | bytes 32768 | tf_op jit(solution)/shard_map/all_to_all | solution.py:22
  152.7 20.5 %all-to-all-done.3 = f32[32,1,1]{2,1,0:T(1,128)S(1)} async-done(((f32[32,1,1]{2,1,0:T(1,128)}), f32[32,1,1]{2,1,0:T(1,128)S(1)}, u32[]{:S(2)}, u32[]{:S(2)}) %all-to-all-start.3) | async-done | bytes 160 | tf_op jit(solution)/shard_map/all_to_all | solution.py:22
  173.2 0.6 reduce_max.59
  (82 shorter events, 3.6 us)
Async XLA Ops:
  1.7 7.9 %collective-permute-start = (f32[6,4,8,4]{3,2,1,0:T(8,128)S(1)}, f32[6,4,8,4]{3,2,1,0:T(8,128)S(1)}, u32[]{:S(2)}, u32[]{:S(2)}) collective-permute-start(f32[6,4,8,4]{3,2,1,0:T(8,128)S(1)} %get-tuple-element.273), channel_id=1, source_target_pairs={{0,1},{1,0},{2,3},{3,2},{4,5},{5,4},{6,7},{7,6},{8,9},{9,8},{10,11... | collective-permute-start | bytes 9224 | tf_op jit(solution)/shard_map/ppermute | solution.py:41
  5.7 6.6 %collective-permute-start.1 = (f32[6,4,8,4]{3,2,1,0:T(8,128)S(1)}, f32[6,4,8,4]{3,2,1,0:T(8,128)S(1)}, u32[]{:S(2)}, u32[]{:S(2)}) collective-permute-start(f32[6,4,8,4]{3,2,1,0:T(8,128)S(1)} %get-tuple-element.274), channel_id=1, source_target_pairs={{0,3},{1,2},{2,1},{3,0},{4,7},{5,6},{6,5},{7,4},{8,11},{9,10},{10,... | collective-permute-start | bytes 9224 | tf_op jit(solution)/shard_map/ppermute | solution.py:42
  9.6 2.8 %copy-start = (f32[6,4,8,120]{3,2,1,0:T(8,128)S(1)}, f32[6,4,8,120]{3,2,1,0:T(8,128)}, u32[]{:S(2)}) copy-start(f32[6,4,8,120]{3,2,1,0:T(8,128)} %param.1) | copy-start | bytes 276484
  12.5 33.4 %collective-permute-start.2 = (f32[6,4,4,128]{3,2,1,0:T(4,128)S(1)}, f32[6,4,4,128]{3,2,1,0:T(4,128)S(1)}, u32[]{:S(2)}, u32[]{:S(2)}) collective-permute-start(f32[6,4,4,128]{3,2,1,0:T(4,128)S(1)} %get-tuple-element.271), channel_id=1, source_target_pairs={{0,4},{4,0},{8,12},{12,8},{16,20},{20,16},{24,28},{28,24},{1,5},{5... | collective-permute-start | bytes 147464 | tf_op jit(solution)/shard_map/ppermute | solution.py:41
  15.6 32.2 %collective-permute-start.3 = (f32[6,4,4,128]{3,2,1,0:T(4,128)S(1)}, f32[6,4,4,128]{3,2,1,0:T(4,128)S(1)}, u32[]{:S(2)}, u32[]{:S(2)}) collective-permute-start(f32[6,4,4,128]{3,2,1,0:T(4,128)S(1)} %get-tuple-element.272), channel_id=1, source_target_pairs={{0,28},{4,8},{8,4},{12,16},{16,12},{20,24},{24,20},{28,0},{1,29},{... | collective-permute-start | bytes 147464 | tf_op jit(solution)/shard_map/ppermute | solution.py:42
  48.0 73.0 %collective-permute-start.5 = (f32[6,4,16,128]{3,2,1,0:T(8,128)S(1)}, f32[6,4,16,128]{3,2,1,0:T(8,128)S(1)}, u32[]{:S(2)}, u32[]{:S(2)}) collective-permute-start(f32[6,4,16,128]{3,2,1,0:T(8,128)S(1)} %pad_maximum_fusion.1), channel_id=1, source_target_pairs={{0,992},{32,64},{64,32},{96,128},{128,96},{160,192},{192,160},{224... | collective-permute-start | bytes 589832 | tf_op jit(solution)/shard_map/ppermute | solution.py:42
  53.3 67.6 %collective-permute-start.4 = (f32[6,4,16,128]{3,2,1,0:T(8,128)S(1)}, f32[6,4,16,128]{3,2,1,0:T(8,128)S(1)}, u32[]{:S(2)}, u32[]{:S(2)}) collective-permute-start(f32[6,4,16,128]{3,2,1,0:T(8,128)S(1)} %pad_maximum_fusion.1), channel_id=1, source_target_pairs={{0,32},{32,0},{64,96},{96,64},{128,160},{160,128},{192,224},{224,1... | collective-permute-start | bytes 589832 | tf_op jit(solution)/shard_map/ppermute | solution.py:41
  84.7 34.9 %all-to-all-start.1 = ((f32[32,1,1]{2,1,0:T(1,128)}), f32[32,1,1]{2,1,0:T(1,128)S(1)}, u32[]{:S(2)}, u32[]{:S(2)}) async-start(f32[32,1,1]{2,1,0:T(1,128)} %broadcast_in_dim.13), calls=%async_computation.1 | async-start | bytes 32768 | tf_op jit(solution)/shard_map/all_to_all | solution.py:22
  134.4 12.5 %all-to-all-start.2 = ((f32[32,1,1]{2,1,0:T(1,128)}), f32[32,1,1]{2,1,0:T(1,128)S(1)}, u32[]{:S(2)}, u32[]{:S(2)}) async-start(f32[32,1,1]{2,1,0:T(1,128)} %broadcast_in_dim.14), calls=%async_computation.2 | async-start | bytes 32768 | tf_op jit(solution)/shard_map/all_to_all | solution.py:22
  148.8 24.3 %all-to-all-start.3 = ((f32[32,1,1]{2,1,0:T(1,128)}), f32[32,1,1]{2,1,0:T(1,128)S(1)}, u32[]{:S(2)}, u32[]{:S(2)}) async-start(f32[32,1,1]{2,1,0:T(1,128)} %broadcast_in_dim.15), calls=%async_computation.3 | async-start | bytes 32768 | tf_op jit(solution)/shard_map/all_to_all | solution.py:22
  152.7 21.8 %copy-start.1 = (f32[6,4,8,120]{3,2,1,0:T(8,128)}, f32[6,4,8,120]{3,2,1,0:T(8,128)S(1)}, u32[]{:S(2)}) copy-start(f32[6,4,8,120]{3,2,1,0:T(8,128)S(1)} %fusion.283) | copy-start | bytes 276484

commit v2 on v1

--- a/solution.py
+++ b/solution.py
@@ -16,12 +16,11 @@
 courant = 0.3
 
 
-def over_all(value):
-    for axes in (PLANE, COLUMN):
-        count = lax.axis_size(axes)
-        everyone = lax.all_to_all(jnp.broadcast_to(value, (count,)), axes, 0, 0, tiled=True)
-        value = jnp.max(everyone)
-    return value
+def over_group(value, axes):
+    everyone = lax.all_to_all(
+        jnp.broadcast_to(value, (lax.axis_size(axes),)), axes, 0, 0, tiled=True
+    )
+    return jnp.max(everyone)
 
 
 def swaps(count):
@@ -30,7 +29,7 @@
     return even, odd
 
 
-def exchange(block, axes, parity, dim, width):
+def padded(block, axes, parity, dim, width):
     even, odd = swaps(lax.axis_size(axes))
     first = lax.slice_in_dim(block, 0, width, axis=dim)
     last = lax.slice_in_dim(block, block.shape[dim] - width, None, axis=dim)
@@ -38,13 +37,9 @@
         to_even, to_odd = block, block
     else:
         to_even, to_odd = jnp.where(parity, first, last), jnp.where(parity, last, first)
+    by_odd = lax.ppermute(to_odd, axes, odd)
     by_even = lax.ppermute(to_even, axes, even)
-    by_odd = lax.ppermute(to_odd, axes, odd)
-    return jnp.where(parity, by_even, by_odd), jnp.where(parity, by_odd, by_even)
-
-
-def padded(block, axes, parity, dim, width):
-    low, high = exchange(block, axes, parity, dim, width)
+    low, high = jnp.where(parity, by_even, by_odd), jnp.where(parity, by_odd, by_even)
     return jnp.concatenate([low, block, high], axis=dim)
 
 
@@ -259,22 +254,24 @@
     return jnp.stack(updated)
 
 
-def body(conserved_state):
+def step(conserved_state):
     own_cells = [conserved_state[component] for component in range(6)]
-    signal_now = over_all(fastest_signal(own_cells))
+    signal_now = fastest_signal(own_cells)
+    block = padded(conserved_state, GZ, lax.axis_index("y") % 2 == 1, 3, GHOST)
+    signal_now = over_group(signal_now, PLANE)
+    block = padded(block, GY, lax.axis_index("x") % 2 == 1, 2, GHOST)
+    signal_now = over_group(signal_now, COLUMN)
+    block = padded(block, GX, lax.axis_index("c") == 1, 1, GHOST)
     time_step = courant / signal_now
-    block = padded(conserved_state, GZ, lax.axis_index("y") % 2 == 1, 3, GHOST)
-    block = padded(block, GY, lax.axis_index("x") % 2 == 1, 2, GHOST)
-    block = padded(block, GX, lax.axis_index("c") == 1, 1, GHOST)
     updated = hydro_step(block, time_step)
     new_cells = [updated[component] for component in range(6)]
-    signal_next = over_all(fastest_signal(new_cells))
+    signal_next = fastest_signal(new_cells)
+    signal_next = over_group(signal_next, PLANE)
+    signal_next = over_group(signal_next, COLUMN)
     return (updated, courant / signal_next)
 
 
 def solution(mesh):
     finer = Mesh(mesh.devices.reshape(16, 2, 2, 4, 4), ALL)
     spec = P(None, GX, GY, GZ)
-    return jax.shard_map(
-        body, mesh=finer, in_specs=(spec,), out_specs=(spec, P()), check_vma=False
-    )
+    return jax.shard_map(step, mesh=finer, in_specs=(spec,), out_specs=(spec, P()), check_vma=False)

time: 176 us -> 176 us (level)
  no operation moved by 1% of the time
where the time goes in v2:
time: 176 us
  starting transfers between devices  86.6 us (49%)
  waiting for transfers between devices  52.5 us (30%)
  other arithmetic  14.9 us (8%)
  blocking collectives  12 us (7%)
  local copies, waits for them, and re-layouts  5.73 us (3%)
  between operations  3.98 us (2%)
    all_to_all x3, waiting for transfers between devices, over_group(): lax.all_to_all(jnp.broadcast_to(value, (lax.axis_size(axes),)), axes, 0,...  47.8 us
    ppermute x3, starting transfers between devices, padded(): by_odd = lax.ppermute(to_odd, axes, odd)  39.4 us
    all_to_all x3, starting transfers between devices, over_group(): lax.all_to_all(jnp.broadcast_to(value, (lax.axis_size(axes),)), axes, 0,...  23.9 us
    ppermute x3, starting transfers between devices, padded(): by_even = lax.ppermute(to_even, axes, even)  23.4 us
    all_to_all x1, blocking collectives, over_group(): lax.all_to_all(jnp.broadcast_to(value, (lax.axis_size(axes),)), axes, 0,...  12 us
    ppermute x3, waiting for transfers between devices, padded(): by_odd = lax.ppermute(to_odd, axes, odd)  4.69 us
    broadcast_in_dim x4, local copies, waits for them, and re-layouts, over_group(): jnp.broadcast_to(value, (lax.axis_size(axes),))  4.42 us
  transfers between devices with their start and end apart: 9, of which 5 were waited for; matrix products, arithmetic and copies ran while one was open for 2% of the time, Pallas kernels for 0%

profile of v2, /device:TPU:1, one launch (start us, length us, event | category | flops | bytes accessed | tf_op | source)
XLA Modules:
  0.0 175.6 jit_solution(4607836759497759554)
XLA Ops:
  0.6 1.1 slice_select_fusion.1
  1.7 4.0 %collective-permute-start = (f32[6,4,8,4]{3,2,1,0:T(8,128)S(1)}, f32[6,4,8,4]{3,2,1,0:T(8,128)S(1)}, u32[]{:S(2)}, u32[]{:S(2)}) collective-permute-start(f32[6,4,8,4]{3,2,1,0:T(8,128)S(1)} %get-tuple-element.273), channel_id=1, source_target_pairs={{0,1},{1,0},{2,3},{3,2},{4,5},{5,4},{6,7},{7,6},{8,9},{9,8},{10,11... | collective-permute-start | bytes 9224 | tf_op jit(solution)/shard_map/ppermute | solution.py:41
  5.7 3.8 %collective-permute-start.1 = (f32[6,4,8,4]{3,2,1,0:T(8,128)S(1)}, f32[6,4,8,4]{3,2,1,0:T(8,128)S(1)}, u32[]{:S(2)}, u32[]{:S(2)}) collective-permute-start(f32[6,4,8,4]{3,2,1,0:T(8,128)S(1)} %get-tuple-element.274), channel_id=1, source_target_pairs={{0,3},{1,2},{2,1},{3,0},{4,7},{5,6},{6,5},{7,4},{8,11},{9,10},{10,... | collective-permute-start | bytes 9224 | tf_op jit(solution)/shard_map/ppermute | solution.py:40
  9.6 2.7 %collective-permute-done.1 = f32[6,4,8,4]{3,2,1,0:T(8,128)S(1)} collective-permute-done((f32[6,4,8,4]{3,2,1,0:T(8,128)S(1)}, f32[6,4,8,4]{3,2,1,0:T(8,128)S(1)}, u32[]{:S(2)}, u32[]{:S(2)}) %collective-permute-start.1) | collective-permute-done | bytes 3104 | tf_op jit(solution)/shard_map/ppermute | solution.py:40
  12.3 0.1 pad_maximum_fusion.2
  12.5 3.1 %collective-permute-start.2 = (f32[6,4,4,128]{3,2,1,0:T(4,128)S(1)}, f32[6,4,4,128]{3,2,1,0:T(4,128)S(1)}, u32[]{:S(2)}, u32[]{:S(2)}) collective-permute-start(f32[6,4,4,128]{3,2,1,0:T(4,128)S(1)} %get-tuple-element.271), channel_id=1, source_target_pairs={{0,4},{4,0},{8,12},{12,8},{16,20},{20,16},{24,28},{28,24},{1,5},{5... | collective-permute-start | bytes 147464 | tf_op jit(solution)/shard_map/ppermute | solution.py:41
  15.6 30.2 %collective-permute-start.3 = (f32[6,4,4,128]{3,2,1,0:T(4,128)S(1)}, f32[6,4,4,128]{3,2,1,0:T(4,128)S(1)}, u32[]{:S(2)}, u32[]{:S(2)}) collective-permute-start(f32[6,4,4,128]{3,2,1,0:T(4,128)S(1)} %get-tuple-element.272), channel_id=1, source_target_pairs={{0,28},{4,8},{8,4},{12,16},{16,12},{20,24},{24,20},{28,0},{1,29},{... | collective-permute-start | bytes 147464 | tf_op jit(solution)/shard_map/ppermute | solution.py:40
  45.9 2.0 %collective-permute-done.3 = f32[6,4,4,128]{3,2,1,0:T(4,128)S(1)} collective-permute-done((f32[6,4,4,128]{3,2,1,0:T(4,128)S(1)}, f32[6,4,4,128]{3,2,1,0:T(4,128)S(1)}, u32[]{:S(2)}, u32[]{:S(2)}) %collective-permute-start.3) | collective-permute-done | bytes 49184 | tf_op jit(solution)/shard_map/ppermute | solution.py:40
  47.8 0.2 pad_maximum_fusion.1
  48.0 5.3 %collective-permute-start.5 = (f32[6,4,16,128]{3,2,1,0:T(8,128)S(1)}, f32[6,4,16,128]{3,2,1,0:T(8,128)S(1)}, u32[]{:S(2)}, u32[]{:S(2)}) collective-permute-start(f32[6,4,16,128]{3,2,1,0:T(8,128)S(1)} %pad_maximum_fusion.1), channel_id=1, source_target_pairs={{0,992},{32,64},{64,32},{96,128},{128,96},{160,192},{192,160},{224... | collective-permute-start | bytes 589832 | tf_op jit(solution)/shard_map/ppermute | solution.py:40
  53.3 16.2 %collective-permute-start.4 = (f32[6,4,16,128]{3,2,1,0:T(8,128)S(1)}, f32[6,4,16,128]{3,2,1,0:T(8,128)S(1)}, u32[]{:S(2)}, u32[]{:S(2)}) collective-permute-start(f32[6,4,16,128]{3,2,1,0:T(8,128)S(1)} %pad_maximum_fusion.1), channel_id=1, source_target_pairs={{0,32},{32,0},{64,96},{96,64},{128,160},{160,128},{192,224},{224,1... | collective-permute-start | bytes 589832 | tf_op jit(solution)/shard_map/ppermute | solution.py:41
  69.6 0.6 fusion.341
  70.2 0.7 broadcast_in_dim.12
  70.9 12.0 %all_to_all.24 = f32[32,1,1]{2,1,0:T(1,128)S(1)} all-to-all(f32[32,1,1]{2,1,0:T(1,128)S(1)} %broadcast_in_dim.12), channel_id=1, replica_groups=mesh['zl'=16,'c'=2,'zh'=2,'x'=4,'y'=4] {'c','x','y'}, dimensions={0} | all-to-all | bytes 256 | tf_op jit(solution)/shard_map/all_to_all | solution.py:20
  82.8 0.6 reduce_max.55
  83.4 1.3 broadcast_in_dim.13
  84.7 14.3 %all-to-all-start.1 = ((f32[32,1,1]{2,1,0:T(1,128)}), f32[32,1,1]{2,1,0:T(1,128)S(1)}, u32[]{:S(2)}, u32[]{:S(2)}) async-start(f32[32,1,1]{2,1,0:T(1,128)} %broadcast_in_dim.13), calls=%async_computation.1 | async-start | bytes 32768 | tf_op jit(solution)/shard_map/all_to_all | solution.py:20
  99.0 20.6 %all-to-all-done.1 = f32[32,1,1]{2,1,0:T(1,128)S(1)} async-done(((f32[32,1,1]{2,1,0:T(1,128)}), f32[32,1,1]{2,1,0:T(1,128)S(1)}, u32[]{:S(2)}, u32[]{:S(2)}) %all-to-all-start.1) | async-done | bytes 160 | tf_op jit(solution)/shard_map/all_to_all | solution.py:20
  119.6 0.6 reduce_max.56
  121.0 0.2 fusion.168
  121.2 0.2 pad_maximum_fusion
  121.5 0.2 fusion.75
  121.9 0.2 fusion.385
  122.5 0.1 fusion.188
  122.8 0.2 fusion.63
  123.0 0.1 fusion.87
  123.1 0.3 fusion.28
  123.5 0.1 fusion.34
  123.6 0.3 fusion.57
  123.9 0.1 fusion.81
  124.3 0.1 fusion.182
  124.6 0.4 fusion.129
  125.0 0.3 fusion.410
  125.3 0.2 fusion.416
  125.5 0.2 fusion.419
  125.8 0.3 fusion.23
  126.2 0.3 fusion.19
  126.5 0.4 fusion.11
  127.5 0.3 fusion.397
  127.8 0.2 fusion.403
  128.0 0.3 fusion.401
  128.3 0.2 fusion.423
  128.8 0.1 broadcast_divide_fusion.2
  129.0 0.1 fusion.367
  129.1 0.1 fusion.366
  129.3 0.2 fusion.213
  129.5 0.1 fusion.205
  129.7 0.2 fusion.21
  129.9 0.3 fusion.9
  130.3 0.3 fusion.13
  131.2 0.1 fusion.360
  131.4 0.1 fusion.361
  131.5 0.1 fusion.253
  132.0 0.2 fusion.279
  132.1 0.1 fusion.271
  132.4 0.7 add_reduce_fusion
  133.1 1.3 broadcast_in_dim.14
  134.4 5.8 %all-to-all-start.2 = ((f32[32,1,1]{2,1,0:T(1,128)}), f32[32,1,1]{2,1,0:T(1,128)S(1)}, u32[]{:S(2)}, u32[]{:S(2)}) async-start(f32[32,1,1]{2,1,0:T(1,128)} %broadcast_in_dim.14), calls=%async_computation.2 | async-start | bytes 32768 | tf_op jit(solution)/shard_map/all_to_all | solution.py:20
  140.2 6.7 %all-to-all-done.2 = f32[32,1,1]{2,1,0:T(1,128)S(1)} async-done(((f32[32,1,1]{2,1,0:T(1,128)}), f32[32,1,1]{2,1,0:T(1,128)S(1)}, u32[]{:S(2)}, u32[]{:S(2)}) %all-to-all-start.2) | async-done | bytes 160 | tf_op jit(solution)/shard_map/all_to_all | solution.py:20
  146.9 0.6 reduce_max.58
  147.5 1.3 broadcast_in_dim.15
  148.8 3.8 %all-to-all-start.3 = ((f32[32,1,1]{2,1,0:T(1,128)}), f32[32,1,1]{2,1,0:T(1,128)S(1)}, u32[]{:S(2)}, u32[]{:S(2)}) async-start(f32[32,1,1]{2,1,0:T(1,128)} %broadcast_in_dim.15), calls=%async_computation.3 | async-start | bytes 32768 | tf_op jit(solution)/shard_map/all_to_all | solution.py:20
  152.7 20.5 %all-to-all-done.3 = f32[32,1,1]{2,1,0:T(1,128)S(1)} async-done(((f32[32,1,1]{2,1,0:T(1,128)}), f32[32,1,1]{2,1,0:T(1,128)S(1)}, u32[]{:S(2)}, u32[]{:S(2)}) %all-to-all-start.3) | async-done | bytes 160 | tf_op jit(solution)/shard_map/all_to_all | solution.py:20
  173.2 0.6 reduce_max.59
  (82 shorter events, 3.6 us)
Async XLA Ops:
  1.7 7.9 %collective-permute-start = (f32[6,4,8,4]{3,2,1,0:T(8,128)S(1)}, f32[6,4,8,4]{3,2,1,0:T(8,128)S(1)}, u32[]{:S(2)}, u32[]{:S(2)}) collective-permute-start(f32[6,4,8,4]{3,2,1,0:T(8,128)S(1)} %get-tuple-element.273), channel_id=1, source_target_pairs={{0,1},{1,0},{2,3},{3,2},{4,5},{5,4},{6,7},{7,6},{8,9},{9,8},{10,11... | collective-permute-start | bytes 9224 | tf_op jit(solution)/shard_map/ppermute | solution.py:41
  5.7 6.6 %collective-permute-start.1 = (f32[6,4,8,4]{3,2,1,0:T(8,128)S(1)}, f32[6,4,8,4]{3,2,1,0:T(8,128)S(1)}, u32[]{:S(2)}, u32[]{:S(2)}) collective-permute-start(f32[6,4,8,4]{3,2,1,0:T(8,128)S(1)} %get-tuple-element.274), channel_id=1, source_target_pairs={{0,3},{1,2},{2,1},{3,0},{4,7},{5,6},{6,5},{7,4},{8,11},{9,10},{10,... | collective-permute-start | bytes 9224 | tf_op jit(solution)/shard_map/ppermute | solution.py:40
  9.6 2.8 %copy-start = (f32[6,4,8,120]{3,2,1,0:T(8,128)S(1)}, f32[6,4,8,120]{3,2,1,0:T(8,128)}, u32[]{:S(2)}) copy-start(f32[6,4,8,120]{3,2,1,0:T(8,128)} %param.1) | copy-start | bytes 276484
  12.5 33.4 %collective-permute-start.2 = (f32[6,4,4,128]{3,2,1,0:T(4,128)S(1)}, f32[6,4,4,128]{3,2,1,0:T(4,128)S(1)}, u32[]{:S(2)}, u32[]{:S(2)}) collective-permute-start(f32[6,4,4,128]{3,2,1,0:T(4,128)S(1)} %get-tuple-element.271), channel_id=1, source_target_pairs={{0,4},{4,0},{8,12},{12,8},{16,20},{20,16},{24,28},{28,24},{1,5},{5... | collective-permute-start | bytes 147464 | tf_op jit(solution)/shard_map/ppermute | solution.py:41
  15.6 32.2 %collective-permute-start.3 = (f32[6,4,4,128]{3,2,1,0:T(4,128)S(1)}, f32[6,4,4,128]{3,2,1,0:T(4,128)S(1)}, u32[]{:S(2)}, u32[]{:S(2)}) collective-permute-start(f32[6,4,4,128]{3,2,1,0:T(4,128)S(1)} %get-tuple-element.272), channel_id=1, source_target_pairs={{0,28},{4,8},{8,4},{12,16},{16,12},{20,24},{24,20},{28,0},{1,29},{... | collective-permute-start | bytes 147464 | tf_op jit(solution)/shard_map/ppermute | solution.py:40
  48.0 73.0 %collective-permute-start.5 = (f32[6,4,16,128]{3,2,1,0:T(8,128)S(1)}, f32[6,4,16,128]{3,2,1,0:T(8,128)S(1)}, u32[]{:S(2)}, u32[]{:S(2)}) collective-permute-start(f32[6,4,16,128]{3,2,1,0:T(8,128)S(1)} %pad_maximum_fusion.1), channel_id=1, source_target_pairs={{0,992},{32,64},{64,32},{96,128},{128,96},{160,192},{192,160},{224... | collective-permute-start | bytes 589832 | tf_op jit(solution)/shard_map/ppermute | solution.py:40
  53.3 67.6 %collective-permute-start.4 = (f32[6,4,16,128]{3,2,1,0:T(8,128)S(1)}, f32[6,4,16,128]{3,2,1,0:T(8,128)S(1)}, u32[]{:S(2)}, u32[]{:S(2)}) collective-permute-start(f32[6,4,16,128]{3,2,1,0:T(8,128)S(1)} %pad_maximum_fusion.1), channel_id=1, source_target_pairs={{0,32},{32,0},{64,96},{96,64},{128,160},{160,128},{192,224},{224,1... | collective-permute-start | bytes 589832 | tf_op jit(solution)/shard_map/ppermute | solution.py:41
  84.7 34.9 %all-to-all-start.1 = ((f32[32,1,1]{2,1,0:T(1,128)}), f32[32,1,1]{2,1,0:T(1,128)S(1)}, u32[]{:S(2)}, u32[]{:S(2)}) async-start(f32[32,1,1]{2,1,0:T(1,128)} %broadcast_in_dim.13), calls=%async_computation.1 | async-start | bytes 32768 | tf_op jit(solution)/shard_map/all_to_all | solution.py:20
  134.4 12.5 %all-to-all-start.2 = ((f32[32,1,1]{2,1,0:T(1,128)}), f32[32,1,1]{2,1,0:T(1,128)S(1)}, u32[]{:S(2)}, u32[]{:S(2)}) async-start(f32[32,1,1]{2,1,0:T(1,128)} %broadcast_in_dim.14), calls=%async_computation.2 | async-start | bytes 32768 | tf_op jit(solution)/shard_map/all_to_all | solution.py:20
  148.8 24.3 %all-to-all-start.3 = ((f32[32,1,1]{2,1,0:T(1,128)}), f32[32,1,1]{2,1,0:T(1,128)S(1)}, u32[]{:S(2)}, u32[]{:S(2)}) async-start(f32[32,1,1]{2,1,0:T(1,128)} %broadcast_in_dim.15), calls=%async_computation.3 | async-start | bytes 32768 | tf_op jit(solution)/shard_map/all_to_all | solution.py:20
  152.7 21.8 %copy-start.1 = (f32[6,4,8,120]{3,2,1,0:T(8,128)}, f32[6,4,8,120]{3,2,1,0:T(8,128)S(1)}, u32[]{:S(2)}) copy-start(f32[6,4,8,120]{3,2,1,0:T(8,128)S(1)} %fusion.283) | copy-start | bytes 276484

commit v3 on v2

v3 whole, which is shorter than its diff:
```python
import jax
import jax.numpy as jnp
from jax import lax
from jax.experimental import pallas as pl
from jax.experimental.pallas import tpu as pltpu
from jax.sharding import Mesh
from jax.sharding import PartitionSpec as P

GHOST = 4
ALL = ("zl", "c", "zh", "x", "y")
PLANE = ("c", "x", "y")
COLUMN = ("zl", "zh")
GX = ("zl", "c")
GY = ("zh", "x")
GZ = ("y",)

adiabatic = 5.0 / 3.0
courant = 0.3


def over_group(value, axes):
    everyone = lax.all_to_all(
        jnp.broadcast_to(value, (lax.axis_size(axes),)), axes, 0, 0, tiled=True
    )
    return jnp.max(everyone)


def swaps(count):
    even = [(i, i ^ 1) for i in range(count)]
    odd = [(i, (i + 1) % count if i % 2 else (i - 1) % count) for i in range(count)]
    return even, odd


def ghosts(block, axes, parity, dim, width):
    even, odd = swaps(lax.axis_size(axes))
    first = lax.slice_in_dim(block, 0, width, axis=dim)
    last = lax.slice_in_dim(block, block.shape[dim] - width, None, axis=dim)
    if block.shape[dim] == width:
        to_even, to_odd = block, block
    else:
        to_even, to_odd = jnp.where(parity, first, last), jnp.where(parity, last, first)
    by_odd = lax.ppermute(to_odd, axes, odd)
    by_even = lax.ppermute(to_even, axes, even)
    return jnp.where(parity, by_even, by_odd), jnp.where(parity, by_odd, by_even)


def padded(block, axes, parity, dim, width):
    low, high = ghosts(block, axes, parity, dim, width)
    return jnp.concatenate([block, high, low], axis=dim)


def roll(value, shift, axis):
    return pltpu.roll(value, shift % value.shape[axis], axis)


def primitive_of(conserved):
    density, energy = conserved[0], conserved[4]
    inverse = 1.0 / density
    speed = [conserved[component] * inverse for component in (1, 2, 3)]
    kinetic = 0.5 * (conserved[1] * speed[0] + conserved[2] * speed[1] + conserved[3] * speed[2])
    return [density, *speed, (adiabatic - 1.0) * (energy - kinetic), conserved[5] * inverse]


def conserved_of(primitive):
    density = primitive[0]
    momenta = [density * primitive[component] for component in (1, 2, 3)]
    kinetic = 0.5 * (
        momenta[0] * primitive[1] + momenta[1] * primitive[2] + momenta[2] * primitive[3]
    )
    energy = primitive[4] * (1.0 / (adiabatic - 1.0)) + kinetic
    return [density, *momenta, energy, density * primitive[5]]


def fastest_signal(conserved):
    primitive = primitive_of(conserved)
    sound = jnp.sqrt(adiabatic * primitive[4] / primitive[0])
    speeds = jnp.maximum(
        jnp.maximum(jnp.abs(primitive[1]), jnp.abs(primitive[2])), jnp.abs(primitive[3])
    )
    return speeds + sound


def edge_of(q3, q2, q1, q, a1, a2):
    edge = (37.0 / 60.0) * (q1 + q) - (8.0 / 60.0) * (q2 + a1) + (1.0 / 60.0) * (q3 + a2)
    return jnp.clip(edge, jnp.minimum(q1, q), jnp.maximum(q1, q))


def limited(q, lower, upper):
    above, below = upper - q, q - lower
    spread = upper - lower
    skewed = spread * (0.5 * (below - above))
    limit = spread * spread * (1.0 / 6.0)
    flat = above * below <= 0.0
    new_lower = jnp.where(flat, q, jnp.where(skewed > limit, q - 2.0 * above, lower))
    new_upper = jnp.where(flat, q, jnp.where(skewed < -limit, q + 2.0 * below, upper))
    return new_lower, new_upper


def traced(primitive, edges, normal, half_step):
    slopes = [upper - lower for lower, upper in edges]
    density, speed, pressure = primitive[0], primitive[normal], primitive[4]
    rates = [-(speed * slopes[component]) for component in range(6)]
    rates[0] = rates[0] - density * slopes[normal]
    rates[normal] = rates[normal] - slopes[4] / density
    rates[4] = rates[4] - adiabatic * pressure * slopes[normal]
    moves = [half_step * rate for rate in rates]
    lower = [edges[component][0] + moves[component] for component in range(6)]
    upper = [edges[component][1] + moves[component] for component in range(6)]
    return lower, upper


def hllc_flux(left, right, normal):
    ratio_left, ratio_right = left[4] / left[0], right[4] / right[0]
    sound_left, sound_right = jnp.sqrt(adiabatic * ratio_left), jnp.sqrt(adiabatic * ratio_right)
    low = jnp.minimum(left[normal] - sound_left, right[normal] - sound_right)
    high = jnp.maximum(left[normal] + sound_left, right[normal] + sound_right)
    mass_left = left[0] * (low - left[normal])
    mass_right = right[0] * (high - right[normal])
    middle = (right[4] - left[4] + mass_left * left[normal] - mass_right * right[normal]) / (
        mass_left - mass_right
    )
    from_left = middle >= 0.0
    side = [jnp.where(from_left, left[component], right[component]) for component in range(6)]
    ratio = jnp.where(from_left, ratio_left, ratio_right)
    mass = jnp.where(from_left, mass_left, mass_right)
    outer = jnp.where(from_left, low, high)
    weight = jnp.where(from_left, jnp.minimum(low, 0.0), jnp.maximum(high, 0.0))
    speed, pressure = side[normal], side[4]
    state = conserved_of(side)
    flux = [item * speed for item in state]
    flux[normal] = flux[normal] + pressure
    flux[4] = flux[4] + pressure * speed
    factor = mass / (outer - middle)
    star = [factor * item for item in side]
    star[0] = factor
    star[normal] = factor * middle
    half_square = 0.5 * (side[1] * side[1] + side[2] * side[2] + side[3] * side[3])
    specific = ratio * (1.0 / (adiabatic - 1.0)) + half_square
    star[4] = factor * (specific + (middle - speed) * (middle + pressure / mass))
    return [flux[c] + weight * (star[c] - state[c]) for c in range(6)]


def kernel(step_ref, low_ref, own_ref, high_ref, out_ref, signal_ref, prim, lower, upper, fluxes, gx):
    step = step_ref[0]
    half = 0.5 * step
    for source, start in ((low_ref, 0), (own_ref, 4), (high_ref, 8)):
        for layer in range(4):
            values = primitive_of([source[c, layer] for c in range(6)])
            for c in range(6):
                prim[c, start + layer] = values[c]

    def faces(index, carry):
        own = [prim[c, index + 3] for c in range(6)]
        edges = []
        for c in range(6):
            q = [prim[c, index + k] for k in range(7)]
            edges.append(
                limited(own[c], edge_of(*q[0:6]), edge_of(*q[1:7]))
            )
        for axis in range(3):
            if axis:
                edges = []
                for c in range(6):
                    q = own[c]
                    near = [roll(q, k, axis - 1) for k in (3, 2, 1)]
                    far = [roll(q, -k, axis - 1) for k in (1, 2)]
                    edge = edge_of(*near, q, *far)
                    edges.append(limited(q, edge, roll(edge, -1, axis - 1)))
            low_face, high_face = traced(own, edges, 1 + axis, half)
            for c in range(6):
                lower[axis, c, index] = low_face[c]
                upper[axis, c, index] = high_face[c]
        return carry

    lax.fori_loop(0, 6, faces, 0)

    def predicted(index, carry):
        for axis in (1, 2):
            left = [roll(upper[axis, c, index], 1, axis - 1) for c in range(6)]
            flux = hllc_flux(left, [lower[axis, c, index] for c in range(6)], 1 + axis)
            for c in range(6):
                fluxes[axis, c, index] = half * (roll(flux[c], -1, axis - 1) - flux[c])
        return carry

    lax.fori_loop(0, 6, predicted, 0)

    def predicted_first(index, carry):
        flux = hllc_flux(
            [upper[0, c, index] for c in range(6)], [lower[0, c, index + 1] for c in range(6)], 1
        )
        for c in range(6):
            fluxes[0, c, index] = flux[c]
        return carry

    lax.fori_loop(0, 5, predicted_first, 0)

    def corrected(states, changes):
        state = conserved_of(states)
        return primitive_of([state[c] - changes[c] for c in range(6)])

    def final_first(index, carry):
        change = [fluxes[1, c, index + 1, 0:8] + fluxes[2, c, index + 1, 0:8] for c in range(6)]
        before = [carry[c] for c in range(6)]
        right = corrected([lower[0, c, index + 1, 0:8] for c in range(6)], change)
        flux = hllc_flux(before, right, 1)
        for c in range(6):
            gx[c, index] = flux[c]
        return tuple(corrected([upper[0, c, index + 1, 0:8] for c in range(6)], change))

    change = [fluxes[1, c, 0, 0:8] + fluxes[2, c, 0, 0:8] for c in range(6)]
    first = tuple(corrected([upper[0, c, 0, 0:8] for c in range(6)], change))
    lax.fori_loop(0, 5, final_first, first)

    lanes = lax.broadcasted_iota(jnp.int32, (8, 128), 1) < 120

    def final(index, fastest):
        here = index + 1
        total = [own_ref[c, index, 0:8] - step * (gx[c, index + 1] - gx[c, index]) for c in range(6)]
        ahead = [half * (fluxes[0, c, here] - fluxes[0, c, index]) for c in range(6)]
        change = [ahead[c] + fluxes[2, c, here] for c in range(6)]
        left = corrected([upper[1, c, here] for c in range(6)], change)
        right = corrected([lower[1, c, here] for c in range(6)], change)
        flux = hllc_flux([roll(item, 1, 0) for item in left], right, 2)
        total = [total[c] - step * (roll(flux[c], -1, 0)[0:8] - flux[c][0:8]) for c in range(6)]
        change = [ahead[c][0:8] + fluxes[1, c, here, 0:8] for c in range(6)]
        left = corrected([upper[2, c, here, 0:8] for c in range(6)], change)
        right = corrected([lower[2, c, here, 0:8] for c in range(6)], change)
        flux = hllc_flux([roll(item, 1, 1) for item in left], right, 3)
        total = [total[c] - step * (roll(flux[c], -1, 1) - flux[c]) for c in range(6)]
        for c in range(6):
            out_ref[c, index] = total[c][:, 0:120]
        return jnp.maximum(fastest, jnp.where(lanes, fastest_signal(total), 0.0))

    fastest = lax.fori_loop(0, 4, final, jnp.zeros((8, 128), jnp.float32))
    signal_ref[0] = jnp.max(fastest)


def hydro_step(low, own, high, time_step):
    vmem = pl.BlockSpec(memory_space=pltpu.VMEM)
    smem = pl.BlockSpec(memory_space=pltpu.SMEM)
    return pl.pallas_call(
        kernel,
        in_specs=[smem, vmem, vmem, vmem],
        out_specs=[vmem, smem],
        out_shape=[
            jax.ShapeDtypeStruct((6, 4, 8, 120), jnp.float32),
            jax.ShapeDtypeStruct((1,), jnp.float32),
        ],
        scratch_shapes=[
            pltpu.VMEM((6, 12, 16, 128), jnp.float32),
            pltpu.VMEM((3, 6, 6, 16, 128), jnp.float32),
            pltpu.VMEM((3, 6, 6, 16, 128), jnp.float32),
            pltpu.VMEM((3, 6, 6, 16, 128), jnp.float32),
            pltpu.VMEM((6, 5, 8, 128), jnp.float32),
        ],
        name="hydro",
    )(time_step.reshape(1), low, own, high)


def step(conserved_state):
    signal_now = jnp.max(fastest_signal([conserved_state[component] for component in range(6)]))
    block = padded(conserved_state, GZ, lax.axis_index("y") % 2 == 1, 3, GHOST)
    signal_now = over_group(signal_now, PLANE)
    block = padded(block, GY, lax.axis_index("x") % 2 == 1, 2, GHOST)
    block, signal_now = lax.optimization_barrier((block, signal_now))
    signal_now = over_group(signal_now, COLUMN)
    low, high = ghosts(block, GX, lax.axis_index("c") == 1, 1, GHOST)
    updated, signal_next = hydro_step(low, block, high, courant / signal_now)
    signal_next = over_group(signal_next[0], PLANE)
    signal_next = over_group(signal_next, COLUMN)
    return (updated, courant / signal_next)


def solution(mesh):
    finer = Mesh(mesh.devices.reshape(16, 2, 2, 4, 4), ALL)
    spec = P(None, GX, GY, GZ)
    return jax.shard_map(step, mesh=finer, in_specs=(spec,), out_specs=(spec, P()), check_vma=False)
```

time: 176 us -> 155 us (0.88)
  blocking collectives: 12 us -> 48 us
  waiting for transfers between devices: 52.5 us -> 24 us
  starting transfers between devices: 86.6 us -> 64 us
  other arithmetic: 14.9 us -> 5.29 us
  Pallas kernels: 0 us -> 6.44 us
  local copies, waits for them, and re-layouts: 5.73 us -> 3.27 us
    all_to_all x1 -> x3, blocking collectives: 12 us -> 48 us  [over_group(): lax.all_to_all(jnp.broadcast_to(value, (lax.axis_size(axes),)), axes, 0,...]
    all_to_all x3 -> x1, waiting for transfers between devices: 47.8 us -> 20.6 us  [over_group(): lax.all_to_all(jnp.broadcast_to(value, (lax.axis_size(axes),)), axes, 0,...]
    all_to_all x3 -> x1, starting transfers between devices: 23.9 us -> 12.5 us  [over_group(): lax.all_to_all(jnp.broadcast_to(value, (lax.axis_size(axes),)), axes, 0,...]
    ppermute x6, starting transfers between devices: 62.7 us -> 51.5 us  [the longest x3 39.6 us: ghosts(): by_odd = lax.ppermute(to_odd, axes, odd)]
    pallas_call x0 -> x1, Pallas kernels: none -> 6.44 us  [hydro_step(): pl.pallas_call(kernel, in_specs=[smem, vmem, vmem, vmem], out_specs=[vmem...]
    mul x37 -> x0, other arithmetic: 3.44 us -> none  [the longest x10 1.82 us: conserved_of(): momenta = [density * primitive[component] for component in (1, 2, 3)]]
    select_n x23 -> x5, other arithmetic: 4.31 us -> 1.89 us  [the longest x2 1.08 us: ghosts(): jnp.where(parity, last, first)]
    min x11 -> x0, other arithmetic: 1.79 us -> none  [parabola(): jnp.clip(edge, jnp.minimum(before_one, middle), jnp.maximum(before_one, m...]
  transfers between devices with their start and end apart: 9 -> 7, of which waited for: 5 -> 2; matrix products, arithmetic and copies ran while one was open for 2% -> 2% of each run, Pallas kernels for 0% -> 0%
where the time goes in v3:
time: 155 us; the launch traced here: 154 us
  starting transfers between devices  64 us (41%)
  blocking collectives  48 us (31%)
  waiting for transfers between devices  24 us (15%)
  Pallas kernels  6.44 us (4%)
  other arithmetic  5.29 us (3%)
  between operations  3.34 us (2%)
  local copies, waits for them, and re-layouts  3.27 us (2%)
    all_to_all x3, blocking collectives, over_group(): lax.all_to_all(jnp.broadcast_to(value, (lax.axis_size(axes),)), axes, 0,...  48 us
    ppermute x3, starting transfers between devices, ghosts(): by_odd = lax.ppermute(to_odd, axes, odd)  39.6 us
    all_to_all x1, waiting for transfers between devices, over_group(): lax.all_to_all(jnp.broadcast_to(value, (lax.axis_size(axes),)), axes, 0,...  20.6 us
    all_to_all x1, starting transfers between devices, over_group(): lax.all_to_all(jnp.broadcast_to(value, (lax.axis_size(axes),)), axes, 0,...  12.5 us
    ppermute x3, starting transfers between devices, ghosts(): by_even = lax.ppermute(to_even, axes, even)  11.9 us
    pallas_call x1, Pallas kernels, hydro_step(): pl.pallas_call(kernel, in_specs=[smem, vmem, vmem, vmem], out_specs=[vmem...  6.44 us
    ppermute x3, waiting for transfers between devices, ghosts(): by_even = lax.ppermute(to_even, axes, even)  3.37 us
    broadcast_in_dim x4, local copies, waits for them, and re-layouts, over_group(): jnp.broadcast_to(value, (lax.axis_size(axes),))  3.26 us
  transfers between devices with their start and end apart: 7, of which 2 were waited for; matrix products, arithmetic and copies ran while one was open for 2% of the time, Pallas kernels for 0%

profile of v3, /device:TPU:1, one launch (start us, length us, event | category | flops | bytes accessed | tf_op | source)
XLA Modules:
  0.0 154.3 jit_solution(17856352732847826274)
XLA Ops:
  0.6 1.1 slice_select_fusion.1
  1.7 5.5 %collective-permute-start = (f32[6,4,8,4]{3,2,1,0:T(8,128)S(1)}, f32[6,4,8,4]{3,2,1,0:T(8,128)S(1)}, u32[]{:S(2)}, u32[]{:S(2)}) collective-permute-start(f32[6,4,8,4]{3,2,1,0:T(8,128)S(1)} %get-tuple-element.18), channel_id=1, source_target_pairs={{0,3},{1,2},{2,1},{3,0},{4,7},{5,6},{6,5},{7,4},{8,11},{9,10},{10,... | collective-permute-start | bytes 9224 | tf_op jit(solution)/shard_map/ppermute | solution.py:42
  7.2 1.9 %collective-permute-start.1 = (f32[6,4,8,4]{3,2,1,0:T(8,128)S(1)}, f32[6,4,8,4]{3,2,1,0:T(8,128)S(1)}, u32[]{:S(2)}, u32[]{:S(2)}) collective-permute-start(f32[6,4,8,4]{3,2,1,0:T(8,128)S(1)} %get-tuple-element.19), channel_id=1, source_target_pairs={{0,1},{1,0},{2,3},{3,2},{4,5},{5,4},{6,7},{7,6},{8,9},{9,8},{10,11... | collective-permute-start | bytes 9224 | tf_op jit(solution)/shard_map/ppermute | solution.py:43
  9.1 0.0 copy-start
  9.1 0.0 collective-permute-done
  9.2 3.4 %collective-permute-done.1 = f32[6,4,8,4]{3,2,1,0:T(8,128)S(1)} collective-permute-done((f32[6,4,8,4]{3,2,1,0:T(8,128)S(1)}, f32[6,4,8,4]{3,2,1,0:T(8,128)S(1)}, u32[]{:S(2)}, u32[]{:S(2)}) %collective-permute-start.1) | collective-permute-done | bytes 3104 | tf_op jit(solution)/shard_map/ppermute | solution.py:43
  12.6 0.0 copy-done
  12.6 0.1 pad_maximum_fusion.1
  12.7 30.9 %collective-permute-start.2 = (f32[6,4,4,128]{3,2,1,0:T(4,128)S(1)}, f32[6,4,4,128]{3,2,1,0:T(4,128)S(1)}, u32[]{:S(2)}, u32[]{:S(2)}) collective-permute-start(f32[6,4,4,128]{3,2,1,0:T(4,128)S(1)} %get-tuple-element.16), channel_id=1, source_target_pairs={{0,28},{4,8},{8,4},{12,16},{16,12},{20,24},{24,20},{28,0},{1,29},{... | collective-permute-start | bytes 147464 | tf_op jit(solution)/shard_map/ppermute | solution.py:42
  43.6 1.9 %collective-permute-start.3 = (f32[6,4,4,128]{3,2,1,0:T(4,128)S(1)}, f32[6,4,4,128]{3,2,1,0:T(4,128)S(1)}, u32[]{:S(2)}, u32[]{:S(2)}) collective-permute-start(f32[6,4,4,128]{3,2,1,0:T(4,128)S(1)} %get-tuple-element.17), channel_id=1, source_target_pairs={{0,4},{4,0},{8,12},{12,8},{16,20},{20,16},{24,28},{28,24},{1,5},{5... | collective-permute-start | bytes 147464 | tf_op jit(solution)/shard_map/ppermute | solution.py:43
  45.5 0.6 fusion.7
  46.2 0.7 broadcast_in_dim.12
  46.8 12.6 %all_to_all.24 = f32[32,1,1]{2,1,0:T(1,128)S(1)} all-to-all(f32[32,1,1]{2,1,0:T(1,128)S(1)} %broadcast_in_dim.12), channel_id=1, replica_groups=mesh['zl'=16,'c'=2,'zh'=2,'x'=4,'y'=4] {'c','x','y'}, dimensions={0} | all-to-all | bytes 256 | tf_op jit(solution)/shard_map/all_to_all | solution.py:22
  59.4 0.6 reduce_max.46
  60.1 0.0 collective-permute-done.2
  60.1 0.0 collective-permute-done.3
  60.1 0.1 pad_maximum_fusion.own_ref
  60.2 0.0 copy-start.1
  60.2 3.2 %collective-permute-start.5 = (f32[6,4,16,128]{3,2,1,0:T(8,128)S(1)}, f32[6,4,16,128]{3,2,1,0:T(8,128)S(1)}, u32[]{:S(2)}, u32[]{:S(2)}) collective-permute-start(f32[6,4,16,128]{3,2,1,0:T(8,128)S(1)} %pad_maximum_fusion.own_ref), channel_id=1, source_target_pairs={{0,992},{32,64},{64,32},{96,128},{128,96},{160,192},{192,160},{224... | collective-permute-start | bytes 589832 | tf_op jit(solution)/shard_map/ppermute | solution.py:42
  63.5 8.1 %collective-permute-start.4 = (f32[6,4,16,128]{3,2,1,0:T(8,128)S(1)}, f32[6,4,16,128]{3,2,1,0:T(8,128)S(1)}, u32[]{:S(2)}, u32[]{:S(2)}) collective-permute-start(f32[6,4,16,128]{3,2,1,0:T(8,128)S(1)} %pad_maximum_fusion.own_ref), channel_id=1, source_target_pairs={{0,32},{32,0},{64,96},{96,64},{128,160},{160,128},{192,224},{224,1... | collective-permute-start | bytes 589832 | tf_op jit(solution)/shard_map/ppermute | solution.py:43
  71.5 1.3 broadcast_in_dim.13
  72.8 12.5 %all-to-all-start.1 = ((f32[32,1,1]{2,1,0:T(1,128)}), f32[32,1,1]{2,1,0:T(1,128)S(1)}, u32[]{:S(2)}, u32[]{:S(2)}) async-start(f32[32,1,1]{2,1,0:T(1,128)} %broadcast_in_dim.13), calls=%async_computation.1 | async-start | bytes 32768 | tf_op jit(solution)/shard_map/all_to_all | solution.py:22
  85.3 20.6 %all-to-all-done.1 = f32[32,1,1]{2,1,0:T(1,128)S(1)} async-done(((f32[32,1,1]{2,1,0:T(1,128)}), f32[32,1,1]{2,1,0:T(1,128)S(1)}, u32[]{:S(2)}, u32[]{:S(2)}) %all-to-all-start.1) | async-done | bytes 160 | tf_op jit(solution)/shard_map/all_to_all | solution.py:22
  105.9 0.6 reduce_max.47
  107.2 0.0 collective-permute-done.5
  107.2 0.0 collective-permute-done.4
  107.2 0.8 broadcast_select_fusion
  108.0 0.0 copy-done.1
  108.0 6.4 %hydro.1 = (f32[6,4,8,120]{3,2,1,0:T(8,128)}, f32[1]{0:T(128)}) custom-call(f32[1]{0:T(128)} %bitcast.5.step_ref, f32[6,4,16,128]{3,2,1,0:T(8,128)} %get-tuple-element.11.low_ref, f32[6,4,16,128]{3,2,1,0:T(8,128)} %copy-done.1, f32[6,4,16,128]{3,2,1,0:T(8,128)} %get-tuple-element.10.high_ref), custom_call_target="tpu_custom_call" | custom-call | tf_op jit(solution)/shard_map/hydro/pallas_call | solution.py:241
  114.5 0.7 broadcast_in_dim.14
  115.2 11.9 %all_to_all.25 = f32[32,1,1]{2,1,0:T(1,128)S(1)} all-to-all(f32[32,1,1]{2,1,0:T(1,128)S(1)} %broadcast_in_dim.14), channel_id=1, replica_groups=mesh['zl'=16,'c'=2,'zh'=2,'x'=4,'y'=4] {'c','x','y'}, dimensions={0} | all-to-all | bytes 256 | tf_op jit(solution)/shard_map/all_to_all | solution.py:22
  127.0 0.6 reduce_max.48
  127.7 0.7 broadcast_in_dim.15
  128.3 23.5 %all_to_all.26 = f32[32,1,1]{2,1,0:T(1,128)S(1)} all-to-all(f32[32,1,1]{2,1,0:T(1,128)S(1)} %broadcast_in_dim.15), channel_id=1, replica_groups=mesh['zl'=16,'c'=2,'zh'=2,'x'=4,'y'=4] {'zl','zh'}, dimensions={0} | all-to-all | bytes 256 | tf_op jit(solution)/shard_map/all_to_all | solution.py:22
  151.9 0.6 reduce_max.49
  (3 shorter events, 0.0 us)
Async XLA Ops:
  1.7 7.5 %collective-permute-start = (f32[6,4,8,4]{3,2,1,0:T(8,128)S(1)}, f32[6,4,8,4]{3,2,1,0:T(8,128)S(1)}, u32[]{:S(2)}, u32[]{:S(2)}) collective-permute-start(f32[6,4,8,4]{3,2,1,0:T(8,128)S(1)} %get-tuple-element.18), channel_id=1, source_target_pairs={{0,3},{1,2},{2,1},{3,0},{4,7},{5,6},{6,5},{7,4},{8,11},{9,10},{10,... | collective-permute-start | bytes 9224 | tf_op jit(solution)/shard_map/ppermute | solution.py:42
  7.2 5.4 %collective-permute-start.1 = (f32[6,4,8,4]{3,2,1,0:T(8,128)S(1)}, f32[6,4,8,4]{3,2,1,0:T(8,128)S(1)}, u32[]{:S(2)}, u32[]{:S(2)}) collective-permute-start(f32[6,4,8,4]{3,2,1,0:T(8,128)S(1)} %get-tuple-element.19), channel_id=1, source_target_pairs={{0,1},{1,0},{2,3},{3,2},{4,5},{5,4},{6,7},{7,6},{8,9},{9,8},{10,11... | collective-permute-start | bytes 9224 | tf_op jit(solution)/shard_map/ppermute | solution.py:43
  9.1 3.4 %copy-start = (f32[6,4,8,120]{3,2,1,0:T(8,128)S(1)}, f32[6,4,8,120]{3,2,1,0:T(8,128)}, u32[]{:S(2)}) copy-start(f32[6,4,8,120]{3,2,1,0:T(8,128)} %param.1) | copy-start | bytes 276484
  12.7 47.3 %collective-permute-start.2 = (f32[6,4,4,128]{3,2,1,0:T(4,128)S(1)}, f32[6,4,4,128]{3,2,1,0:T(4,128)S(1)}, u32[]{:S(2)}, u32[]{:S(2)}) collective-permute-start(f32[6,4,4,128]{3,2,1,0:T(4,128)S(1)} %get-tuple-element.16), channel_id=1, source_target_pairs={{0,28},{4,8},{8,4},{12,16},{16,12},{20,24},{24,20},{28,0},{1,29},{... | collective-permute-start | bytes 147464 | tf_op jit(solution)/shard_map/ppermute | solution.py:42
  43.6 16.4 %collective-permute-start.3 = (f32[6,4,4,128]{3,2,1,0:T(4,128)S(1)}, f32[6,4,4,128]{3,2,1,0:T(4,128)S(1)}, u32[]{:S(2)}, u32[]{:S(2)}) collective-permute-start(f32[6,4,4,128]{3,2,1,0:T(4,128)S(1)} %get-tuple-element.17), channel_id=1, source_target_pairs={{0,4},{4,0},{8,12},{12,8},{16,20},{20,16},{24,28},{28,24},{1,5},{5... | collective-permute-start | bytes 147464 | tf_op jit(solution)/shard_map/ppermute | solution.py:43
  60.2 47.8 %copy-start.1 = (f32[6,4,16,128]{3,2,1,0:T(8,128)}, f32[6,4,16,128]{3,2,1,0:T(8,128)S(1)}, u32[]{:S(2)}) copy-start(f32[6,4,16,128]{3,2,1,0:T(8,128)S(1)} %pad_maximum_fusion.own_ref) | copy-start | bytes 589828
  60.2 47.0 %collective-permute-start.5 = (f32[6,4,16,128]{3,2,1,0:T(8,128)S(1)}, f32[6,4,16,128]{3,2,1,0:T(8,128)S(1)}, u32[]{:S(2)}, u32[]{:S(2)}) collective-permute-start(f32[6,4,16,128]{3,2,1,0:T(8,128)S(1)} %pad_maximum_fusion.own_ref), channel_id=1, source_target_pairs={{0,992},{32,64},{64,32},{96,128},{128,96},{160,192},{192,160},{224... | collective-permute-start | bytes 589832 | tf_op jit(solution)/shard_map/ppermute | solution.py:42
  63.5 43.8 %collective-permute-start.4 = (f32[6,4,16,128]{3,2,1,0:T(8,128)S(1)}, f32[6,4,16,128]{3,2,1,0:T(8,128)S(1)}, u32[]{:S(2)}, u32[]{:S(2)}) collective-permute-start(f32[6,4,16,128]{3,2,1,0:T(8,128)S(1)} %pad_maximum_fusion.own_ref), channel_id=1, source_target_pairs={{0,32},{32,0},{64,96},{96,64},{128,160},{160,128},{192,224},{224,1... | collective-permute-start | bytes 589832 | tf_op jit(solution)/shard_map/ppermute | solution.py:43
  72.8 33.1 %all-to-all-start.1 = ((f32[32,1,1]{2,1,0:T(1,128)}), f32[32,1,1]{2,1,0:T(1,128)S(1)}, u32[]{:S(2)}, u32[]{:S(2)}) async-start(f32[32,1,1]{2,1,0:T(1,128)} %broadcast_in_dim.13), calls=%async_computation.1 | async-start | bytes 32768 | tf_op jit(solution)/shard_map/all_to_all | solution.py:22

commit v4 on v3

--- a/solution.py
+++ b/solution.py
@@ -21,6 +21,22 @@
 def over_group(value, axes):
     everyone = lax.all_to_all(
         jnp.broadcast_to(value, (lax.axis_size(axes),)), axes, 0, 0, tiled=True
+    )
+    return jnp.max(everyone)
+
+
+def over_column(value, first):
+    halves, rows = lax.axis_size("zh"), lax.axis_size("zl")
+    deep = halves * rows
+    order = [(first + step) % deep for step in range(deep)]
+    columns, width = lax.axis_size("c"), lax.axis_size(("x", "y"))
+    groups = [
+        [(((z % rows) * columns + c) * halves + z // rows) * width + place for z in order]
+        for c in range(columns)
+        for place in range(width)
+    ]
+    everyone = lax.all_to_all(
+        jnp.broadcast_to(value, (deep,)), ALL, 0, 0, axis_index_groups=groups, tiled=True
     )
     return jnp.max(everyone)
 
@@ -262,8 +278,8 @@
     block = padded(conserved_state, GZ, lax.axis_index("y") % 2 == 1, 3, GHOST)
     signal_now = over_group(signal_now, PLANE)
     block = padded(block, GY, lax.axis_index("x") % 2 == 1, 2, GHOST)
-    block, signal_now = lax.optimization_barrier((block, signal_now))
-    signal_now = over_group(signal_now, COLUMN)
+    block, _ = lax.optimization_barrier((block, signal_now))
+    signal_now = over_column(signal_now, 20)
     low, high = ghosts(block, GX, lax.axis_index("c") == 1, 1, GHOST)
     updated, signal_next = hydro_step(low, block, high, courant / signal_now)
     signal_next = over_group(signal_next[0], PLANE)

time: 155 us -> 159 us (1.026)
  blocking collectives: 48 us -> 62.1 us
  waiting for transfers between devices: 24 us -> 10.1 us
  starting transfers between devices: 64 us -> 67.9 us
    all_to_all x3, blocking collectives: 48 us -> 62.1 us  [over_group(): lax.all_to_all(jnp.broadcast_to(value, (lax.axis_size(axes),)), axes, 0,...]
    all_to_all x1, waiting for transfers between devices: 20.6 us -> 6.7 us  [over_column(): lax.all_to_all(jnp.broadcast_to(value, (deep,)), ALL, 0, 0, axis_index_gr...]
    all_to_all x1, starting transfers between devices: 12.5 us -> 16.4 us  [over_column(): lax.all_to_all(jnp.broadcast_to(value, (deep,)), ALL, 0, 0, axis_index_gr...]
    broadcast_in_dim x4 -> x3, local copies, waits for them, and re-layouts: 3.26 us -> 1.99 us  [over_group(): jnp.broadcast_to(value, (lax.axis_size(axes),))]
where the time goes in v4:
time: 159 us; the launch traced here: 158 us
  starting transfers between devices  67.9 us (43%)
  blocking collectives  62.1 us (39%)
  waiting for transfers between devices  10.1 us (6%)
  Pallas kernels  6.44 us (4%)
  other arithmetic  5.29 us (3%)
  between operations  3.34 us (2%)
  local copies, waits for them, and re-layouts  3.27 us (2%)
    all_to_all x3, blocking collectives, over_group(): lax.all_to_all(jnp.broadcast_to(value, (lax.axis_size(axes),)), axes, 0,...  62.1 us
    ppermute x3, starting transfers between devices, ghosts(): by_odd = lax.ppermute(to_odd, axes, odd)  39.6 us
    all_to_all x1, starting transfers between devices, over_column(): lax.all_to_all(jnp.broadcast_to(value, (deep,)), ALL, 0, 0, axis_index_gr...  16.4 us
    ppermute x3, starting transfers between devices, ghosts(): by_even = lax.ppermute(to_even, axes, even)  11.9 us
    all_to_all x1, waiting for transfers between devices, over_column(): lax.all_to_all(jnp.broadcast_to(value, (deep,)), ALL, 0, 0, axis_index_gr...  6.7 us
    pallas_call x1, Pallas kernels, hydro_step(): pl.pallas_call(kernel, in_specs=[smem, vmem, vmem, vmem], out_specs=[vmem...  6.44 us
    ppermute x3, waiting for transfers between devices, ghosts(): by_even = lax.ppermute(to_even, axes, even)  3.37 us
  transfers between devices with their start and end apart: 7, of which 2 were waited for; matrix products, arithmetic and copies ran while one was open for 2% of the time, Pallas kernels for 0%

profile of v4, /device:TPU:1, one launch (start us, length us, event | category | flops | bytes accessed | tf_op | source)
XLA Modules:
  0.0 158.5 jit_solution(1282376813140576032)
XLA Ops:
  0.6 1.1 slice_select_fusion.1
  1.7 5.5 %collective-permute-start = (f32[6,4,8,4]{3,2,1,0:T(8,128)S(1)}, f32[6,4,8,4]{3,2,1,0:T(8,128)S(1)}, u32[]{:S(2)}, u32[]{:S(2)}) collective-permute-start(f32[6,4,8,4]{3,2,1,0:T(8,128)S(1)} %get-tuple-element.16), channel_id=1, source_target_pairs={{0,3},{1,2},{2,1},{3,0},{4,7},{5,6},{6,5},{7,4},{8,11},{9,10},{10,... | collective-permute-start | bytes 9224 | tf_op jit(solution)/shard_map/ppermute | solution.py:58
  7.2 1.9 %collective-permute-start.1 = (f32[6,4,8,4]{3,2,1,0:T(8,128)S(1)}, f32[6,4,8,4]{3,2,1,0:T(8,128)S(1)}, u32[]{:S(2)}, u32[]{:S(2)}) collective-permute-start(f32[6,4,8,4]{3,2,1,0:T(8,128)S(1)} %get-tuple-element.17), channel_id=1, source_target_pairs={{0,1},{1,0},{2,3},{3,2},{4,5},{5,4},{6,7},{7,6},{8,9},{9,8},{10,11... | collective-permute-start | bytes 9224 | tf_op jit(solution)/shard_map/ppermute | solution.py:59
  9.1 0.0 copy-start
  9.1 0.0 collective-permute-done
  9.2 3.4 %collective-permute-done.1 = f32[6,4,8,4]{3,2,1,0:T(8,128)S(1)} collective-permute-done((f32[6,4,8,4]{3,2,1,0:T(8,128)S(1)}, f32[6,4,8,4]{3,2,1,0:T(8,128)S(1)}, u32[]{:S(2)}, u32[]{:S(2)}) %collective-permute-start.1) | collective-permute-done | bytes 3104 | tf_op jit(solution)/shard_map/ppermute | solution.py:59
  12.6 0.0 copy-done
  12.6 0.1 pad_maximum_fusion.1
  12.7 30.9 %collective-permute-start.2 = (f32[6,4,4,128]{3,2,1,0:T(4,128)S(1)}, f32[6,4,4,128]{3,2,1,0:T(4,128)S(1)}, u32[]{:S(2)}, u32[]{:S(2)}) collective-permute-start(f32[6,4,4,128]{3,2,1,0:T(4,128)S(1)} %get-tuple-element.14), channel_id=1, source_target_pairs={{0,28},{4,8},{8,4},{12,16},{16,12},{20,24},{24,20},{28,0},{1,29},{... | collective-permute-start | bytes 147464 | tf_op jit(solution)/shard_map/ppermute | solution.py:58
  43.6 1.9 %collective-permute-start.3 = (f32[6,4,4,128]{3,2,1,0:T(4,128)S(1)}, f32[6,4,4,128]{3,2,1,0:T(4,128)S(1)}, u32[]{:S(2)}, u32[]{:S(2)}) collective-permute-start(f32[6,4,4,128]{3,2,1,0:T(4,128)S(1)} %get-tuple-element.15), channel_id=1, source_target_pairs={{0,4},{4,0},{8,12},{12,8},{16,20},{20,16},{24,28},{28,24},{1,5},{5... | collective-permute-start | bytes 147464 | tf_op jit(solution)/shard_map/ppermute | solution.py:59
  45.5 0.6 fusion.7
  46.2 0.7 broadcast_in_dim.12
  46.8 12.6 %all_to_all.24 = f32[32,1,1]{2,1,0:T(1,128)S(1)} all-to-all(f32[32,1,1]{2,1,0:T(1,128)S(1)} %broadcast_in_dim.12), channel_id=1, replica_groups=mesh['zl'=16,'c'=2,'zh'=2,'x'=4,'y'=4] {'c','x','y'}, dimensions={0} | all-to-all | bytes 256 | tf_op jit(solution)/shard_map/all_to_all | solution.py:22
  59.4 0.6 reduce_max.46
  60.1 0.0 collective-permute-done.2
  60.1 0.0 collective-permute-done.3
  60.1 0.1 pad_maximum_fusion.own_ref
  60.2 0.0 copy-start.1
  60.2 3.2 %collective-permute-start.5 = (f32[6,4,16,128]{3,2,1,0:T(8,128)S(1)}, f32[6,4,16,128]{3,2,1,0:T(8,128)S(1)}, u32[]{:S(2)}, u32[]{:S(2)}) collective-permute-start(f32[6,4,16,128]{3,2,1,0:T(8,128)S(1)} %pad_maximum_fusion.own_ref), channel_id=1, source_target_pairs={{0,992},{32,64},{64,32},{96,128},{128,96},{160,192},{192,160},{224... | collective-permute-start | bytes 589832 | tf_op jit(solution)/shard_map/ppermute | solution.py:58
  63.5 8.1 %collective-permute-start.4 = (f32[6,4,16,128]{3,2,1,0:T(8,128)S(1)}, f32[6,4,16,128]{3,2,1,0:T(8,128)S(1)}, u32[]{:S(2)}, u32[]{:S(2)}) collective-permute-start(f32[6,4,16,128]{3,2,1,0:T(8,128)S(1)} %pad_maximum_fusion.own_ref), channel_id=1, source_target_pairs={{0,32},{32,0},{64,96},{96,64},{128,160},{160,128},{192,224},{224,1... | collective-permute-start | bytes 589832 | tf_op jit(solution)/shard_map/ppermute | solution.py:59
  71.5 1.3 broadcast_in_dim.13
  72.8 16.4 %all-to-all-start.1 = ((f32[32,1,1]{2,1,0:T(1,128)}), f32[32,1,1]{2,1,0:T(1,128)S(1)}, u32[]{:S(2)}, u32[]{:S(2)}) async-start(f32[32,1,1]{2,1,0:T(1,128)} %broadcast_in_dim.13), calls=%async_computation.1 | async-start | bytes 32768 | tf_op jit(solution)/shard_map/all_to_all | solution.py:38
  89.2 6.7 %all-to-all-done.1 = f32[32,1,1]{2,1,0:T(1,128)S(1)} async-done(((f32[32,1,1]{2,1,0:T(1,128)}), f32[32,1,1]{2,1,0:T(1,128)S(1)}, u32[]{:S(2)}, u32[]{:S(2)}) %all-to-all-start.1) | async-done | bytes 160 | tf_op jit(solution)/shard_map/all_to_all | solution.py:38
  95.9 0.6 reduce_max.47
  97.3 0.0 collective-permute-done.5
  97.3 0.0 collective-permute-done.4
  97.3 0.8 broadcast_select_fusion
  98.1 0.0 copy-done.1
  98.1 6.4 %hydro.1 = (f32[6,4,8,120]{3,2,1,0:T(8,128)}, f32[1]{0:T(128)}) custom-call(f32[1]{0:T(128)} %bitcast.5.step_ref, f32[6,4,16,128]{3,2,1,0:T(8,128)} %get-tuple-element.9.low_ref, f32[6,4,16,128]{3,2,1,0:T(8,128)} %copy-done.1, f32[6,4,16,128]{3,2,1,0:T(8,128)} %get-tuple-element.8.high_ref), custom_call_target="tpu_custom_call" | custom-call | tf_op jit(solution)/shard_map/hydro/pallas_call | solution.py:257
  104.5 0.7 broadcast_in_dim.14
  105.2 12.6 %all_to_all.25 = f32[32,1,1]{2,1,0:T(1,128)S(1)} all-to-all(f32[32,1,1]{2,1,0:T(1,128)S(1)} %broadcast_in_dim.14), channel_id=1, replica_groups=mesh['zl'=16,'c'=2,'zh'=2,'x'=4,'y'=4] {'c','x','y'}, dimensions={0} | all-to-all | bytes 256 | tf_op jit(solution)/shard_map/all_to_all | solution.py:22
  117.8 0.6 reduce_max.48
  118.5 0.7 broadcast_in_dim.15
  119.1 36.9 %all_to_all.26 = f32[32,1,1]{2,1,0:T(1,128)S(1)} all-to-all(f32[32,1,1]{2,1,0:T(1,128)S(1)} %broadcast_in_dim.15), channel_id=1, replica_groups=mesh['zl'=16,'c'=2,'zh'=2,'x'=4,'y'=4] {'zl','zh'}, dimensions={0} | all-to-all | bytes 256 | tf_op jit(solution)/shard_map/all_to_all | solution.py:22
  156.0 0.6 reduce_max.49
  (3 shorter events, 0.0 us)
Async XLA Ops:
  1.7 7.5 %collective-permute-start = (f32[6,4,8,4]{3,2,1,0:T(8,128)S(1)}, f32[6,4,8,4]{3,2,1,0:T(8,128)S(1)}, u32[]{:S(2)}, u32[]{:S(2)}) collective-permute-start(f32[6,4,8,4]{3,2,1,0:T(8,128)S(1)} %get-tuple-element.16), channel_id=1, source_target_pairs={{0,3},{1,2},{2,1},{3,0},{4,7},{5,6},{6,5},{7,4},{8,11},{9,10},{10,... | collective-permute-start | bytes 9224 | tf_op jit(solution)/shard_map/ppermute | solution.py:58
  7.2 5.4 %collective-permute-start.1 = (f32[6,4,8,4]{3,2,1,0:T(8,128)S(1)}, f32[6,4,8,4]{3,2,1,0:T(8,128)S(1)}, u32[]{:S(2)}, u32[]{:S(2)}) collective-permute-start(f32[6,4,8,4]{3,2,1,0:T(8,128)S(1)} %get-tuple-element.17), channel_id=1, source_target_pairs={{0,1},{1,0},{2,3},{3,2},{4,5},{5,4},{6,7},{7,6},{8,9},{9,8},{10,11... | collective-permute-start | bytes 9224 | tf_op jit(solution)/shard_map/ppermute | solution.py:59
  9.1 3.4 %copy-start = (f32[6,4,8,120]{3,2,1,0:T(8,128)S(1)}, f32[6,4,8,120]{3,2,1,0:T(8,128)}, u32[]{:S(2)}) copy-start(f32[6,4,8,120]{3,2,1,0:T(8,128)} %param.1) | copy-start | bytes 276484
  12.7 47.3 %collective-permute-start.2 = (f32[6,4,4,128]{3,2,1,0:T(4,128)S(1)}, f32[6,4,4,128]{3,2,1,0:T(4,128)S(1)}, u32[]{:S(2)}, u32[]{:S(2)}) collective-permute-start(f32[6,4,4,128]{3,2,1,0:T(4,128)S(1)} %get-tuple-element.14), channel_id=1, source_target_pairs={{0,28},{4,8},{8,4},{12,16},{16,12},{20,24},{24,20},{28,0},{1,29},{... | collective-permute-start | bytes 147464 | tf_op jit(solution)/shard_map/ppermute | solution.py:58
  43.6 16.4 %collective-permute-start.3 = (f32[6,4,4,128]{3,2,1,0:T(4,128)S(1)}, f32[6,4,4,128]{3,2,1,0:T(4,128)S(1)}, u32[]{:S(2)}, u32[]{:S(2)}) collective-permute-start(f32[6,4,4,128]{3,2,1,0:T(4,128)S(1)} %get-tuple-element.15), channel_id=1, source_target_pairs={{0,4},{4,0},{8,12},{12,8},{16,20},{20,16},{24,28},{28,24},{1,5},{5... | collective-permute-start | bytes 147464 | tf_op jit(solution)/shard_map/ppermute | solution.py:59
  60.2 37.9 %copy-start.1 = (f32[6,4,16,128]{3,2,1,0:T(8,128)}, f32[6,4,16,128]{3,2,1,0:T(8,128)S(1)}, u32[]{:S(2)}) copy-start(f32[6,4,16,128]{3,2,1,0:T(8,128)S(1)} %pad_maximum_fusion.own_ref) | copy-start | bytes 589828
  60.2 37.1 %collective-permute-start.5 = (f32[6,4,16,128]{3,2,1,0:T(8,128)S(1)}, f32[6,4,16,128]{3,2,1,0:T(8,128)S(1)}, u32[]{:S(2)}, u32[]{:S(2)}) collective-permute-start(f32[6,4,16,128]{3,2,1,0:T(8,128)S(1)} %pad_maximum_fusion.own_ref), channel_id=1, source_target_pairs={{0,992},{32,64},{64,32},{96,128},{128,96},{160,192},{192,160},{224... | collective-permute-start | bytes 589832 | tf_op jit(solution)/shard_map/ppermute | solution.py:58
  63.5 33.8 %collective-permute-start.4 = (f32[6,4,16,128]{3,2,1,0:T(8,128)S(1)}, f32[6,4,16,128]{3,2,1,0:T(8,128)S(1)}, u32[]{:S(2)}, u32[]{:S(2)}) collective-permute-start(f32[6,4,16,128]{3,2,1,0:T(8,128)S(1)} %pad_maximum_fusion.own_ref), channel_id=1, source_target_pairs={{0,32},{32,0},{64,96},{96,64},{128,160},{160,128},{192,224},{224,1... | collective-permute-start | bytes 589832 | tf_op jit(solution)/shard_map/ppermute | solution.py:59
  72.8 23.1 %all-to-all-start.1 = ((f32[32,1,1]{2,1,0:T(1,128)}), f32[32,1,1]{2,1,0:T(1,128)S(1)}, u32[]{:S(2)}, u32[]{:S(2)}) async-start(f32[32,1,1]{2,1,0:T(1,128)} %broadcast_in_dim.13), calls=%async_computation.1 | async-start | bytes 32768 | tf_op jit(solution)/shard_map/all_to_all | solution.py:38

commit v5 on v4

--- a/solution.py
+++ b/solution.py
@@ -47,7 +47,7 @@
     return even, odd
 
 
-def ghosts(block, axes, parity, dim, width):
+def swapped(block, axes, parity, dim, width):
     even, odd = swaps(lax.axis_size(axes))
     first = lax.slice_in_dim(block, 0, width, axis=dim)
     last = lax.slice_in_dim(block, block.shape[dim] - width, None, axis=dim)
@@ -57,11 +57,12 @@
         to_even, to_odd = jnp.where(parity, first, last), jnp.where(parity, last, first)
     by_odd = lax.ppermute(to_odd, axes, odd)
     by_even = lax.ppermute(to_even, axes, even)
-    return jnp.where(parity, by_even, by_odd), jnp.where(parity, by_odd, by_even)
+    return by_even, by_odd
 
 
 def padded(block, axes, parity, dim, width):
-    low, high = ghosts(block, axes, parity, dim, width)
+    by_even, by_odd = swapped(block, axes, parity, dim, width)
+    low, high = jnp.where(parity, by_even, by_odd), jnp.where(parity, by_odd, by_even)
     return jnp.concatenate([block, high, low], axis=dim)
 
 
@@ -156,10 +157,11 @@
     return [flux[c] + weight * (star[c] - state[c]) for c in range(6)]
 
 
-def kernel(step_ref, low_ref, own_ref, high_ref, out_ref, signal_ref, prim, lower, upper, fluxes, gx):
+def kernel(parity_ref, step_ref, even_ref, own_ref, odd_ref, out_ref, signal_ref, prim, lower, upper, fluxes, gx):
     step = step_ref[0]
     half = 0.5 * step
-    for source, start in ((low_ref, 0), (own_ref, 4), (high_ref, 8)):
+    even_start = 8 - 8 * parity_ref[0]
+    for source, start in ((even_ref, even_start), (own_ref, 4), (odd_ref, 8 - even_start)):
         for layer in range(4):
             values = primitive_of([source[c, layer] for c in range(6)])
             for c in range(6):
@@ -251,12 +253,13 @@
     signal_ref[0] = jnp.max(fastest)
 
 
-def hydro_step(low, own, high, time_step):
+def hydro_step(parity, time_step, by_even, own, by_odd):
     vmem = pl.BlockSpec(memory_space=pltpu.VMEM)
     smem = pl.BlockSpec(memory_space=pltpu.SMEM)
+    blocks = [pltpu.with_memory_space_constraint(item, pltpu.VMEM) for item in (by_even, own, by_odd)]
     return pl.pallas_call(
         kernel,
-        in_specs=[smem, vmem, vmem, vmem],
+        in_specs=[smem, smem, vmem, vmem, vmem],
         out_specs=[vmem, smem],
         out_shape=[
             jax.ShapeDtypeStruct((6, 4, 8, 120), jnp.float32),
@@ -270,18 +273,21 @@
             pltpu.VMEM((6, 5, 8, 128), jnp.float32),
         ],
         name="hydro",
-    )(time_step.reshape(1), low, own, high)
+    )(parity.reshape(1), time_step.reshape(1), *blocks)
 
 
 def step(conserved_state):
     signal_now = jnp.max(fastest_signal([conserved_state[component] for component in range(6)]))
     block = padded(conserved_state, GZ, lax.axis_index("y") % 2 == 1, 3, GHOST)
-    signal_now = over_group(signal_now, PLANE)
+    to_plane = jnp.broadcast_to(signal_now, (lax.axis_size(PLANE), 1, 1))
+    block, to_plane = lax.optimization_barrier((block, to_plane))
+    signal_now = jnp.max(lax.all_to_all(to_plane, PLANE, 0, 0, tiled=True))
     block = padded(block, GY, lax.axis_index("x") % 2 == 1, 2, GHOST)
     block, _ = lax.optimization_barrier((block, signal_now))
-    signal_now = over_column(signal_now, 20)
-    low, high = ghosts(block, GX, lax.axis_index("c") == 1, 1, GHOST)
-    updated, signal_next = hydro_step(low, block, high, courant / signal_now)
+    signal_now = over_column(signal_now, 8)
+    parity = lax.axis_index("c")
+    by_even, by_odd = swapped(block, GX, parity == 1, 1, GHOST)
+    updated, signal_next = hydro_step(parity, courant / signal_now, by_even, block, by_odd)
     signal_next = over_group(signal_next[0], PLANE)
     signal_next = over_group(signal_next, COLUMN)
     return (updated, courant / signal_next)

time: 159 us -> 155 us (0.975)
  blocking collectives: 62.1 us -> 57.5 us
  waiting for transfers between devices: 10.1 us -> 14.3 us
  starting transfers between devices: 67.9 us -> 66.3 us
    all_to_all x3 -> x2, blocking collectives: 62.1 us -> 44.9 us  [over_group(): lax.all_to_all(jnp.broadcast_to(value, (lax.axis_size(axes),)), axes, 0,...]
    all_to_all x0 -> x1, blocking collectives: none -> 12.6 us  [step(): signal_now = jnp.max(lax.all_to_all(to_plane, PLANE, 0, 0, tiled=True))]
    all_to_all x1, waiting for transfers between devices: 6.7 us -> 11.5 us  [over_column(): lax.all_to_all(jnp.broadcast_to(value, (deep,)), ALL, 0, 0, axis_index_gr...]
    all_to_all x1, starting transfers between devices: 16.4 us -> 14.8 us  [over_column(): lax.all_to_all(jnp.broadcast_to(value, (deep,)), ALL, 0, 0, axis_index_gr...]
where the time goes in v5:
time: 155 us; the launch traced here: 154 us
  starting transfers between devices  66.3 us (43%)
  blocking collectives  57.5 us (37%)
  waiting for transfers between devices  14.3 us (9%)
  Pallas kernels  5.34 us (3%)
  other arithmetic  4.48 us (3%)
  between operations  3.32 us (2%)
  local copies, waits for them, and re-layouts  3.14 us (2%)
    all_to_all x2, blocking collectives, over_group(): lax.all_to_all(jnp.broadcast_to(value, (lax.axis_size(axes),)), axes, 0,...  44.9 us
    ppermute x3, starting transfers between devices, swapped(): by_odd = lax.ppermute(to_odd, axes, odd)  39.6 us
    all_to_all x1, starting transfers between devices, over_column(): lax.all_to_all(jnp.broadcast_to(value, (deep,)), ALL, 0, 0, axis_index_gr...  14.8 us
    all_to_all x1, blocking collectives, step(): signal_now = jnp.max(lax.all_to_all(to_plane, PLANE, 0, 0, tiled=True))  12.6 us
    ppermute x3, starting transfers between devices, swapped(): by_even = lax.ppermute(to_even, axes, even)  11.9 us
    all_to_all x1, waiting for transfers between devices, over_column(): lax.all_to_all(jnp.broadcast_to(value, (deep,)), ALL, 0, 0, axis_index_gr...  11.5 us
    pallas_call x1, Pallas kernels, hydro_step(): pl.pallas_call(kernel, in_specs=[smem, smem, vmem, vmem, vmem], out_specs...  5.34 us
  transfers between devices with their start and end apart: 7, of which 2 were waited for; matrix products, arithmetic and copies ran while one was open for 2% of the time, Pallas kernels for 0%

profile of v5, /device:TPU:1, one launch (start us, length us, event | category | flops | bytes accessed | tf_op | source)
XLA Modules:
  0.0 154.4 jit_solution(657042569690154474)
XLA Ops:
  0.6 0.0 copy-start
  0.7 1.1 slice_select_fusion.1
  1.8 5.5 %collective-permute-start = (f32[6,4,8,4]{3,2,1,0:T(8,128)S(1)}, f32[6,4,8,4]{3,2,1,0:T(8,128)S(1)}, u32[]{:S(2)}, u32[]{:S(2)}) collective-permute-start(f32[6,4,8,4]{3,2,1,0:T(8,128)S(1)} %get-tuple-element.18), channel_id=1, source_target_pairs={{0,3},{1,2},{2,1},{3,0},{4,7},{5,6},{6,5},{7,4},{8,11},{9,10},{10,... | collective-permute-start | bytes 9224 | tf_op jit(solution)/shard_map/ppermute | solution.py:58
  7.3 1.9 %collective-permute-start.1 = (f32[6,4,8,4]{3,2,1,0:T(8,128)S(1)}, f32[6,4,8,4]{3,2,1,0:T(8,128)S(1)}, u32[]{:S(2)}, u32[]{:S(2)}) collective-permute-start(f32[6,4,8,4]{3,2,1,0:T(8,128)S(1)} %get-tuple-element.19), channel_id=1, source_target_pairs={{0,1},{1,0},{2,3},{3,2},{4,5},{5,4},{6,7},{7,6},{8,9},{9,8},{10,11... | collective-permute-start | bytes 9224 | tf_op jit(solution)/shard_map/ppermute | solution.py:59
  9.2 0.0 copy-done
  9.2 0.6 fusion.7
  9.8 0.0 collective-permute-done
  9.8 2.8 %collective-permute-done.1 = f32[6,4,8,4]{3,2,1,0:T(8,128)S(1)} collective-permute-done((f32[6,4,8,4]{3,2,1,0:T(8,128)S(1)}, f32[6,4,8,4]{3,2,1,0:T(8,128)S(1)}, u32[]{:S(2)}, u32[]{:S(2)}) %collective-permute-start.1) | collective-permute-done | bytes 3104 | tf_op jit(solution)/shard_map/ppermute | solution.py:59
  12.6 0.1 pad_maximum_fusion.1
  12.8 0.7 broadcast_in_dim.12
  13.4 30.9 %collective-permute-start.2 = (f32[6,4,4,128]{3,2,1,0:T(4,128)S(1)}, f32[6,4,4,128]{3,2,1,0:T(4,128)S(1)}, u32[]{:S(2)}, u32[]{:S(2)}) collective-permute-start(f32[6,4,4,128]{3,2,1,0:T(4,128)S(1)} %get-tuple-element.16), channel_id=1, source_target_pairs={{0,28},{4,8},{8,4},{12,16},{16,12},{20,24},{24,20},{28,0},{1,29},{... | collective-permute-start | bytes 147464 | tf_op jit(solution)/shard_map/ppermute | solution.py:58
  44.3 1.9 %collective-permute-start.3 = (f32[6,4,4,128]{3,2,1,0:T(4,128)S(1)}, f32[6,4,4,128]{3,2,1,0:T(4,128)S(1)}, u32[]{:S(2)}, u32[]{:S(2)}) collective-permute-start(f32[6,4,4,128]{3,2,1,0:T(4,128)S(1)} %get-tuple-element.17), channel_id=1, source_target_pairs={{0,4},{4,0},{8,12},{12,8},{16,20},{20,16},{24,28},{28,24},{1,5},{5... | collective-permute-start | bytes 147464 | tf_op jit(solution)/shard_map/ppermute | solution.py:59
  46.3 12.6 %all_to_all.23 = f32[32,1,1]{2,1,0:T(1,128)S(1)} all-to-all(f32[32,1,1]{2,1,0:T(1,128)S(1)} %broadcast_in_dim.12), channel_id=1, replica_groups=mesh['zl'=16,'c'=2,'zh'=2,'x'=4,'y'=4] {'c','x','y'}, dimensions={0} | all-to-all | bytes 256 | tf_op jit(solution)/shard_map/all_to_all | solution.py:284
  58.9 0.6 reduce_max.46
  59.5 0.0 collective-permute-done.2
  59.5 0.0 collective-permute-done.3
  59.6 3.2 %collective-permute-start.5 = (f32[6,4,16,128]{3,2,1,0:T(8,128)S(1)}, f32[6,4,16,128]{3,2,1,0:T(8,128)S(1)}, u32[]{:S(2)}, u32[]{:S(2)}) collective-permute-start(f32[6,4,16,128]{3,2,1,0:T(8,128)S(1)} %pad_maximum_fusion.own_ref), channel_id=1, source_target_pairs={{0,992},{32,64},{64,32},{96,128},{128,96},{160,192},{192,160},{224... | collective-permute-start | bytes 589832 | tf_op jit(solution)/shard_map/ppermute | solution.py:58
  62.8 8.1 %collective-permute-start.4 = (f32[6,4,16,128]{3,2,1,0:T(8,128)S(1)}, f32[6,4,16,128]{3,2,1,0:T(8,128)S(1)}, u32[]{:S(2)}, u32[]{:S(2)}) collective-permute-start(f32[6,4,16,128]{3,2,1,0:T(8,128)S(1)} %pad_maximum_fusion.own_ref), channel_id=1, source_target_pairs={{0,32},{32,0},{64,96},{96,64},{128,160},{160,128},{192,224},{224,1... | collective-permute-start | bytes 589832 | tf_op jit(solution)/shard_map/ppermute | solution.py:59
  70.9 1.3 broadcast_in_dim.13
  72.1 14.8 %all-to-all-start.1 = ((f32[32,1,1]{2,1,0:T(1,128)}), f32[32,1,1]{2,1,0:T(1,128)S(1)}, u32[]{:S(2)}, u32[]{:S(2)}) async-start(f32[32,1,1]{2,1,0:T(1,128)} %broadcast_in_dim.13), calls=%async_computation.1 | async-start | bytes 32768 | tf_op jit(solution)/shard_map/all_to_all | solution.py:38
  87.0 11.5 %all-to-all-done.1 = f32[32,1,1]{2,1,0:T(1,128)S(1)} async-done(((f32[32,1,1]{2,1,0:T(1,128)}), f32[32,1,1]{2,1,0:T(1,128)S(1)}, u32[]{:S(2)}, u32[]{:S(2)}) %all-to-all-start.1) | async-done | bytes 160 | tf_op jit(solution)/shard_map/all_to_all | solution.py:38
  98.5 0.6 reduce_max.47
  99.8 0.0 collective-permute-done.5.odd_ref
  99.8 0.0 collective-permute-done.4.even_ref
  99.8 5.3 %hydro.1 = (f32[6,4,8,120]{3,2,1,0:T(8,128)}, f32[1]{0:T(128)}) custom-call(s32[1]{0:T(128)} %bitcast.parity_ref, f32[1]{0:T(128)} %bitcast.6.step_ref, f32[6,4,16,128]{3,2,1,0:T(8,128)S(1)} %collective-permute-done.4.even_ref, f32[6,4,16,128]{3,2,1,0:T(8,128)S(1)} %pad_maximum_fusion.own_ref, f32[6,4,16,128]{3,2,1,0:T(8,128)S(1)} %collective-permute-done.5.odd_ref), custom_call_target="tpu_custom_call" | custom-call | tf_op jit(solution)/shard_map/hydro/pallas_call | solution.py:260
  105.2 0.6 broadcast_in_dim.14
  105.8 12.8 %all_to_all.24 = f32[32,1,1]{2,1,0:T(1,128)S(1)} all-to-all(f32[32,1,1]{2,1,0:T(1,128)S(1)} %broadcast_in_dim.14), channel_id=1, replica_groups=mesh['zl'=16,'c'=2,'zh'=2,'x'=4,'y'=4] {'c','x','y'}, dimensions={0} | all-to-all | bytes 256 | tf_op jit(solution)/shard_map/all_to_all | solution.py:22
  118.5 0.6 reduce_max.48
  119.2 0.7 broadcast_in_dim.15
  119.8 32.1 %all_to_all.25 = f32[32,1,1]{2,1,0:T(1,128)S(1)} all-to-all(f32[32,1,1]{2,1,0:T(1,128)S(1)} %broadcast_in_dim.15), channel_id=1, replica_groups=mesh['zl'=16,'c'=2,'zh'=2,'x'=4,'y'=4] {'zl','zh'}, dimensions={0} | all-to-all | bytes 256 | tf_op jit(solution)/shard_map/all_to_all | solution.py:22
  152.0 0.6 reduce_max.49
  (4 shorter events, 0.1 us)
Async XLA Ops:
  0.6 8.5 %copy-start = (f32[6,4,8,120]{3,2,1,0:T(8,128)S(1)}, f32[6,4,8,120]{3,2,1,0:T(8,128)}, u32[]{:S(2)}) copy-start(f32[6,4,8,120]{3,2,1,0:T(8,128)} %param.1) | copy-start | bytes 276484
  1.8 8.0 %collective-permute-start = (f32[6,4,8,4]{3,2,1,0:T(8,128)S(1)}, f32[6,4,8,4]{3,2,1,0:T(8,128)S(1)}, u32[]{:S(2)}, u32[]{:S(2)}) collective-permute-start(f32[6,4,8,4]{3,2,1,0:T(8,128)S(1)} %get-tuple-element.18), channel_id=1, source_target_pairs={{0,3},{1,2},{2,1},{3,0},{4,7},{5,6},{6,5},{7,4},{8,11},{9,10},{10,... | collective-permute-start | bytes 9224 | tf_op jit(solution)/shard_map/ppermute | solution.py:58
  7.3 5.4 %collective-permute-start.1 = (f32[6,4,8,4]{3,2,1,0:T(8,128)S(1)}, f32[6,4,8,4]{3,2,1,0:T(8,128)S(1)}, u32[]{:S(2)}, u32[]{:S(2)}) collective-permute-start(f32[6,4,8,4]{3,2,1,0:T(8,128)S(1)} %get-tuple-element.19), channel_id=1, source_target_pairs={{0,1},{1,0},{2,3},{3,2},{4,5},{5,4},{6,7},{7,6},{8,9},{9,8},{10,11... | collective-permute-start | bytes 9224 | tf_op jit(solution)/shard_map/ppermute | solution.py:59
  13.4 46.0 %collective-permute-start.2 = (f32[6,4,4,128]{3,2,1,0:T(4,128)S(1)}, f32[6,4,4,128]{3,2,1,0:T(4,128)S(1)}, u32[]{:S(2)}, u32[]{:S(2)}) collective-permute-start(f32[6,4,4,128]{3,2,1,0:T(4,128)S(1)} %get-tuple-element.16), channel_id=1, source_target_pairs={{0,28},{4,8},{8,4},{12,16},{16,12},{20,24},{24,20},{28,0},{1,29},{... | collective-permute-start | bytes 147464 | tf_op jit(solution)/shard_map/ppermute | solution.py:58
  44.3 15.2 %collective-permute-start.3 = (f32[6,4,4,128]{3,2,1,0:T(4,128)S(1)}, f32[6,4,4,128]{3,2,1,0:T(4,128)S(1)}, u32[]{:S(2)}, u32[]{:S(2)}) collective-permute-start(f32[6,4,4,128]{3,2,1,0:T(4,128)S(1)} %get-tuple-element.17), channel_id=1, source_target_pairs={{0,4},{4,0},{8,12},{12,8},{16,20},{20,16},{24,28},{28,24},{1,5},{5... | collective-permute-start | bytes 147464 | tf_op jit(solution)/shard_map/ppermute | solution.py:59
  59.6 40.3 %collective-permute-start.5 = (f32[6,4,16,128]{3,2,1,0:T(8,128)S(1)}, f32[6,4,16,128]{3,2,1,0:T(8,128)S(1)}, u32[]{:S(2)}, u32[]{:S(2)}) collective-permute-start(f32[6,4,16,128]{3,2,1,0:T(8,128)S(1)} %pad_maximum_fusion.own_ref), channel_id=1, source_target_pairs={{0,992},{32,64},{64,32},{96,128},{128,96},{160,192},{192,160},{224... | collective-permute-start | bytes 589832 | tf_op jit(solution)/shard_map/ppermute | solution.py:58
  62.8 37.0 %collective-permute-start.4 = (f32[6,4,16,128]{3,2,1,0:T(8,128)S(1)}, f32[6,4,16,128]{3,2,1,0:T(8,128)S(1)}, u32[]{:S(2)}, u32[]{:S(2)}) collective-permute-start(f32[6,4,16,128]{3,2,1,0:T(8,128)S(1)} %pad_maximum_fusion.own_ref), channel_id=1, source_target_pairs={{0,32},{32,0},{64,96},{96,64},{128,160},{160,128},{192,224},{224,1... | collective-permute-start | bytes 589832 | tf_op jit(solution)/shard_map/ppermute | solution.py:59
  72.1 26.3 %all-to-all-start.1 = ((f32[32,1,1]{2,1,0:T(1,128)}), f32[32,1,1]{2,1,0:T(1,128)S(1)}, u32[]{:S(2)}, u32[]{:S(2)}) async-start(f32[32,1,1]{2,1,0:T(1,128)} %broadcast_in_dim.13), calls=%async_computation.1 | async-start | bytes 32768 | tf_op jit(solution)/shard_map/all_to_all | solution.py:38

commit v6 on v5

--- a/solution.py
+++ b/solution.py
@@ -16,13 +16,6 @@
 
 adiabatic = 5.0 / 3.0
 courant = 0.3
-
-
-def over_group(value, axes):
-    everyone = lax.all_to_all(
-        jnp.broadcast_to(value, (lax.axis_size(axes),)), axes, 0, 0, tiled=True
-    )
-    return jnp.max(everyone)
 
 
 def over_column(value, first):
@@ -35,10 +28,8 @@
         for c in range(columns)
         for place in range(width)
     ]
-    everyone = lax.all_to_all(
-        jnp.broadcast_to(value, (deep,)), ALL, 0, 0, axis_index_groups=groups, tiled=True
-    )
-    return jnp.max(everyone)
+    value = jnp.broadcast_to(value, (deep, 1, 1))
+    return lax.all_to_all(value, ALL, 0, 0, axis_index_groups=groups, tiled=True)
 
 
 def swaps(count):
@@ -157,10 +148,32 @@
     return [flux[c] + weight * (star[c] - state[c]) for c in range(6)]
 
 
-def kernel(parity_ref, step_ref, even_ref, own_ref, odd_ref, out_ref, signal_ref, prim, lower, upper, fluxes, gx):
-    step = step_ref[0]
+def maximum_of(everyone_ref):
+    fastest = everyone_ref[0]
+    for device in range(1, everyone_ref.shape[0]):
+        fastest = jnp.maximum(fastest, everyone_ref[device])
+    return fastest
+
+
+def spread_kernel(everyone_ref, out_ref):
+    out_ref[...] = jnp.broadcast_to(maximum_of(everyone_ref)[None], out_ref.shape)
+
+
+def spread(everyone, count):
+    vmem = pl.BlockSpec(memory_space=pltpu.VMEM)
+    return pl.pallas_call(
+        spread_kernel,
+        in_specs=[vmem],
+        out_specs=vmem,
+        out_shape=jax.ShapeDtypeStruct((count, 1, 1), jnp.float32),
+        name="spread",
+    )(pltpu.with_memory_space_constraint(everyone, pltpu.VMEM))
+
+
+def kernel(column_ref, even_ref, own_ref, odd_ref, out_ref, signal_ref, prim, lower, upper, fluxes, gx):
+    step = jnp.max(courant / maximum_of(column_ref))
     half = 0.5 * step
-    even_start = 8 - 8 * parity_ref[0]
+    even_start = 8 - 8 * lax.axis_index("c")
     for source, start in ((even_ref, even_start), (own_ref, 4), (odd_ref, 8 - even_start)):
         for layer in range(4):
             values = primitive_of([source[c, layer] for c in range(6)])
@@ -250,20 +263,22 @@
         return jnp.maximum(fastest, jnp.where(lanes, fastest_signal(total), 0.0))
 
     fastest = lax.fori_loop(0, 4, final, jnp.zeros((8, 128), jnp.float32))
-    signal_ref[0] = jnp.max(fastest)
-
-
-def hydro_step(parity, time_step, by_even, own, by_odd):
+    signal_ref[...] = jnp.full(signal_ref.shape, jnp.max(fastest))
+
+
+def hydro_step(column, by_even, own, by_odd, count):
     vmem = pl.BlockSpec(memory_space=pltpu.VMEM)
-    smem = pl.BlockSpec(memory_space=pltpu.SMEM)
-    blocks = [pltpu.with_memory_space_constraint(item, pltpu.VMEM) for item in (by_even, own, by_odd)]
+    blocks = [
+        pltpu.with_memory_space_constraint(item, pltpu.VMEM)
+        for item in (column, by_even, own, by_odd)
+    ]
     return pl.pallas_call(
         kernel,
-        in_specs=[smem, smem, vmem, vmem, vmem],
-        out_specs=[vmem, smem],
+        in_specs=[vmem] * 4,
+        out_specs=[vmem, vmem],
         out_shape=[
             jax.ShapeDtypeStruct((6, 4, 8, 120), jnp.float32),
-            jax.ShapeDtypeStruct((1,), jnp.float32),
+            jax.ShapeDtypeStruct((count, 1, 1), jnp.float32),
         ],
         scratch_shapes=[
             pltpu.VMEM((6, 12, 16, 128), jnp.float32),
@@ -273,7 +288,7 @@
             pltpu.VMEM((6, 5, 8, 128), jnp.float32),
         ],
         name="hydro",
-    )(parity.reshape(1), time_step.reshape(1), *blocks)
+    )(*blocks)
 
 
 def step(conserved_state):
@@ -284,13 +299,13 @@
     signal_now = jnp.max(lax.all_to_all(to_plane, PLANE, 0, 0, tiled=True))
     block = padded(block, GY, lax.axis_index("x") % 2 == 1, 2, GHOST)
     block, _ = lax.optimization_barrier((block, signal_now))
-    signal_now = over_column(signal_now, 8)
-    parity = lax.axis_index("c")
-    by_even, by_odd = swapped(block, GX, parity == 1, 1, GHOST)
-    updated, signal_next = hydro_step(parity, courant / signal_now, by_even, block, by_odd)
-    signal_next = over_group(signal_next[0], PLANE)
-    signal_next = over_group(signal_next, COLUMN)
-    return (updated, courant / signal_next)
+    column = over_column(signal_now, 8)
+    by_even, by_odd = swapped(block, GX, lax.axis_index("c") == 1, 1, GHOST)
+    updated, to_plane = hydro_step(column, by_even, block, by_odd, lax.axis_size(PLANE))
+    plane = lax.all_to_all(to_plane, PLANE, 0, 0, tiled=True)
+    to_column = spread(plane, lax.axis_size(COLUMN))
+    column = lax.all_to_all(to_column, COLUMN, 0, 0, tiled=True)
+    return (updated, courant / jnp.max(column))
 
 
 def solution(mesh):

time: 155 us -> 152 us (0.981)
  blocking collectives: 57.5 us -> 84.1 us
  starting transfers between devices: 66.3 us -> 51.5 us
  waiting for transfers between devices: 14.3 us -> 2.81 us
  local copies, waits for them, and re-layouts: 3.14 us -> 1.32 us
    all_to_all x2 -> x3, blocking collectives: 44.9 us -> 71.5 us  [the longest x1 32.3 us: step(): column = lax.all_to_all(to_column, COLUMN, 0, 0, tiled=True)]
    all_to_all x1 -> x0, starting transfers between devices: 14.8 us -> none  [over_column(): lax.all_to_all(jnp.broadcast_to(value, (deep,)), ALL, 0, 0, axis_index_gr...]
    all_to_all x1 -> x0, waiting for transfers between devices: 11.5 us -> none  [over_column(): lax.all_to_all(jnp.broadcast_to(value, (deep,)), ALL, 0, 0, axis_index_gr...]
    broadcast_in_dim x3 -> x1, local copies, waits for them, and re-layouts: 2.48 us -> 0.66 us  [over_column(): value = jnp.broadcast_to(value, (deep, 1, 1))]
    pallas_call x1 -> x2, Pallas kernels: 5.34 us -> 6.09 us  [the longest x1 5.45 us: hydro_step(): pl.pallas_call(kernel, in_specs=[vmem] * 4, out_specs=[vmem, vmem], out_s...]
  transfers between devices with their start and end apart: 7 -> 6, of which waited for: 2 -> 1; matrix products, arithmetic and copies ran while one was open for 2% -> 1% of each run, Pallas kernels for 0% -> 0%
where the time goes in v6:
time: 152 us
  blocking collectives  84.1 us (55%)
  starting transfers between devices  51.5 us (34%)
  Pallas kernels  6.09 us (4%)
  other arithmetic  3.21 us (2%)
  waiting for transfers between devices  2.81 us (2%)
  between operations  2.58 us (2%)
    ppermute x3, starting transfers between devices, swapped(): by_odd = lax.ppermute(to_odd, axes, odd)  39.6 us
    all_to_all x1, blocking collectives, step(): column = lax.all_to_all(to_column, COLUMN, 0, 0, tiled=True)  32.3 us
    all_to_all x1, blocking collectives, over_column(): lax.all_to_all(value, ALL, 0, 0, axis_index_groups=groups, tiled=True)  26.2 us
    all_to_all x1, blocking collectives, step(): plane = lax.all_to_all(to_plane, PLANE, 0, 0, tiled=True)  13 us
    all_to_all x1, blocking collectives, step(): signal_now = jnp.max(lax.all_to_all(to_plane, PLANE, 0, 0, tiled=True))  12.6 us
    ppermute x3, starting transfers between devices, swapped(): by_even = lax.ppermute(to_even, axes, even)  11.9 us
    pallas_call x1, Pallas kernels, hydro_step(): pl.pallas_call(kernel, in_specs=[vmem] * 4, out_specs=[vmem, vmem], out_s...  5.45 us
  transfers between devices with their start and end apart: 6, of which 1 were waited for; matrix products, arithmetic and copies ran while one was open for 1% of the time, Pallas kernels for 0%

profile of v6, /device:TPU:1, one launch (start us, length us, event | category | flops | bytes accessed | tf_op | source)
XLA Modules:
  0.0 151.6 jit_solution(14329232080492194451)
XLA Ops:
  0.6 0.0 copy-start
  0.7 1.1 slice_select_fusion.1
  1.8 5.5 %collective-permute-start = (f32[6,4,8,4]{3,2,1,0:T(8,128)S(1)}, f32[6,4,8,4]{3,2,1,0:T(8,128)S(1)}, u32[]{:S(2)}, u32[]{:S(2)}) collective-permute-start(f32[6,4,8,4]{3,2,1,0:T(8,128)S(1)} %get-tuple-element.18), channel_id=1, source_target_pairs={{0,3},{1,2},{2,1},{3,0},{4,7},{5,6},{6,5},{7,4},{8,11},{9,10},{10,... | collective-permute-start | bytes 9224 | tf_op jit(solution)/shard_map/ppermute | solution.py:49
  7.3 1.9 %collective-permute-start.1 = (f32[6,4,8,4]{3,2,1,0:T(8,128)S(1)}, f32[6,4,8,4]{3,2,1,0:T(8,128)S(1)}, u32[]{:S(2)}, u32[]{:S(2)}) collective-permute-start(f32[6,4,8,4]{3,2,1,0:T(8,128)S(1)} %get-tuple-element.19), channel_id=1, source_target_pairs={{0,1},{1,0},{2,3},{3,2},{4,5},{5,4},{6,7},{7,6},{8,9},{9,8},{10,11... | collective-permute-start | bytes 9224 | tf_op jit(solution)/shard_map/ppermute | solution.py:50
  9.2 0.0 copy-done
  9.2 0.6 fusion.7
  9.8 0.0 collective-permute-done
  9.8 2.8 %collective-permute-done.1 = f32[6,4,8,4]{3,2,1,0:T(8,128)S(1)} collective-permute-done((f32[6,4,8,4]{3,2,1,0:T(8,128)S(1)}, f32[6,4,8,4]{3,2,1,0:T(8,128)S(1)}, u32[]{:S(2)}, u32[]{:S(2)}) %collective-permute-start.1) | collective-permute-done | bytes 3104 | tf_op jit(solution)/shard_map/ppermute | solution.py:50
  12.6 0.1 pad_maximum_fusion.1
  12.8 0.7 broadcast_in_dim.6
  13.5 30.9 %collective-permute-start.2 = (f32[6,4,4,128]{3,2,1,0:T(4,128)S(1)}, f32[6,4,4,128]{3,2,1,0:T(4,128)S(1)}, u32[]{:S(2)}, u32[]{:S(2)}) collective-permute-start(f32[6,4,4,128]{3,2,1,0:T(4,128)S(1)} %get-tuple-element.16), channel_id=1, source_target_pairs={{0,28},{4,8},{8,4},{12,16},{16,12},{20,24},{24,20},{28,0},{1,29},{... | collective-permute-start | bytes 147464 | tf_op jit(solution)/shard_map/ppermute | solution.py:49
  44.3 1.9 %collective-permute-start.3 = (f32[6,4,4,128]{3,2,1,0:T(4,128)S(1)}, f32[6,4,4,128]{3,2,1,0:T(4,128)S(1)}, u32[]{:S(2)}, u32[]{:S(2)}) collective-permute-start(f32[6,4,4,128]{3,2,1,0:T(4,128)S(1)} %get-tuple-element.17), channel_id=1, source_target_pairs={{0,4},{4,0},{8,12},{12,8},{16,20},{20,16},{24,28},{28,24},{1,5},{5... | collective-permute-start | bytes 147464 | tf_op jit(solution)/shard_map/ppermute | solution.py:50
  46.3 12.6 %all_to_all.20 = f32[32,1,1]{2,1,0:T(1,128)S(1)} all-to-all(f32[32,1,1]{2,1,0:T(1,128)S(1)} %broadcast_in_dim.6), channel_id=1, replica_groups=mesh['zl'=16,'c'=2,'zh'=2,'x'=4,'y'=4] {'c','x','y'}, dimensions={0} | all-to-all | bytes 256 | tf_op jit(solution)/shard_map/all_to_all | solution.py:299
  58.9 0.6 reduce_max.28
  59.5 0.0 collective-permute-done.2
  59.5 0.0 collective-permute-done.3
  59.6 3.2 %collective-permute-start.5 = (f32[6,4,16,128]{3,2,1,0:T(8,128)S(1)}, f32[6,4,16,128]{3,2,1,0:T(8,128)S(1)}, u32[]{:S(2)}, u32[]{:S(2)}) collective-permute-start(f32[6,4,16,128]{3,2,1,0:T(8,128)S(1)} %pad_maximum_fusion.own_ref), channel_id=1, source_target_pairs={{0,992},{32,64},{64,32},{96,128},{128,96},{160,192},{192,160},{224... | collective-permute-start | bytes 589832 | tf_op jit(solution)/shard_map/ppermute | solution.py:49
  62.8 8.1 %collective-permute-start.4 = (f32[6,4,16,128]{3,2,1,0:T(8,128)S(1)}, f32[6,4,16,128]{3,2,1,0:T(8,128)S(1)}, u32[]{:S(2)}, u32[]{:S(2)}) collective-permute-start(f32[6,4,16,128]{3,2,1,0:T(8,128)S(1)} %pad_maximum_fusion.own_ref), channel_id=1, source_target_pairs={{0,32},{32,0},{64,96},{96,64},{128,160},{160,128},{192,224},{224,1... | collective-permute-start | bytes 589832 | tf_op jit(solution)/shard_map/ppermute | solution.py:50
  70.9 0.7 broadcast_in_dim.7
  71.6 26.2 %all_to_all.21.column_ref = f32[32,1,1]{2,1,0:T(1,128)S(1)} all-to-all(f32[32,1,1]{2,1,0:T(1,128)S(1)} %broadcast_in_dim.7), channel_id=1, replica_groups={{512,576,640,704,768,832,896,960,16,80,144,208,272,336,400,464,528,592,..., dimensions={0} | all-to-all | bytes 256 | tf_op jit(solution)/shard_map/all_to_all | solution.py:32
  97.8 0.0 collective-permute-done.5.odd_ref
  97.8 0.0 collective-permute-done.4.even_ref
  97.8 5.4 %hydro.1 = (f32[6,4,8,120]{3,2,1,0:T(8,128)}, f32[32,1,1]{2,1,0:T(1,128)}) custom-call(f32[32,1,1]{2,1,0:T(1,128)S(1)} %all_to_all.21.column_ref, f32[6,4,16,128]{3,2,1,0:T(8,128)S(1)} %collective-permute-done.4.even_ref, f32[6,4,16,128]{3,2,1,0:T(8,128)S(1)} %pad_maximum_fusion.own_ref, f32[6,4,16,128]{3,2,1,0:T(8,128)S(1)} %collective-permute-done.5.odd_ref), custom_call_target="tpu_custom_call" | custom-call | tf_op jit(solution)/shard_map/hydro/pallas_call | solution.py:275
  103.2 13.0 %all_to_all.22.everyone_ref = f32[32,1,1]{2,1,0:T(1,128)S(1)} all-to-all(f32[32,1,1]{2,1,0:T(1,128)} %get-tuple-element.11), channel_id=1, replica_groups=mesh['zl'=16,'c'=2,'zh'=2,'x'=4,'y'=4] {'c','x','y'}, dimensions={0} | all-to-all | bytes 256 | tf_op jit(solution)/shard_map/all_to_all | solution.py:305
  116.2 0.6 spread.1
  116.8 32.3 %all_to_all.23 = f32[32,1,1]{2,1,0:T(1,128)S(1)} all-to-all(f32[32,1,1]{2,1,0:T(1,128)} %spread.1), channel_id=1, replica_groups=mesh['zl'=16,'c'=2,'zh'=2,'x'=4,'y'=4] {'zl','zh'}, dimensions={0} | all-to-all | bytes 256 | tf_op jit(solution)/shard_map/all_to_all | solution.py:307
  149.2 0.6 reduce_max.29
  (4 shorter events, 0.1 us)
Async XLA Ops:
  0.6 8.5 %copy-start = (f32[6,4,8,120]{3,2,1,0:T(8,128)S(1)}, f32[6,4,8,120]{3,2,1,0:T(8,128)}, u32[]{:S(2)}) copy-start(f32[6,4,8,120]{3,2,1,0:T(8,128)} %param.1) | copy-start | bytes 276484
  1.8 8.0 %collective-permute-start = (f32[6,4,8,4]{3,2,1,0:T(8,128)S(1)}, f32[6,4,8,4]{3,2,1,0:T(8,128)S(1)}, u32[]{:S(2)}, u32[]{:S(2)}) collective-permute-start(f32[6,4,8,4]{3,2,1,0:T(8,128)S(1)} %get-tuple-element.18), channel_id=1, source_target_pairs={{0,3},{1,2},{2,1},{3,0},{4,7},{5,6},{6,5},{7,4},{8,11},{9,10},{10,... | collective-permute-start | bytes 9224 | tf_op jit(solution)/shard_map/ppermute | solution.py:49
  7.3 5.4 %collective-permute-start.1 = (f32[6,4,8,4]{3,2,1,0:T(8,128)S(1)}, f32[6,4,8,4]{3,2,1,0:T(8,128)S(1)}, u32[]{:S(2)}, u32[]{:S(2)}) collective-permute-start(f32[6,4,8,4]{3,2,1,0:T(8,128)S(1)} %get-tuple-element.19), channel_id=1, source_target_pairs={{0,1},{1,0},{2,3},{3,2},{4,5},{5,4},{6,7},{7,6},{8,9},{9,8},{10,11... | collective-permute-start | bytes 9224 | tf_op jit(solution)/shard_map/ppermute | solution.py:50
  13.5 46.0 %collective-permute-start.2 = (f32[6,4,4,128]{3,2,1,0:T(4,128)S(1)}, f32[6,4,4,128]{3,2,1,0:T(4,128)S(1)}, u32[]{:S(2)}, u32[]{:S(2)}) collective-permute-start(f32[6,4,4,128]{3,2,1,0:T(4,128)S(1)} %get-tuple-element.16), channel_id=1, source_target_pairs={{0,28},{4,8},{8,4},{12,16},{16,12},{20,24},{24,20},{28,0},{1,29},{... | collective-permute-start | bytes 147464 | tf_op jit(solution)/shard_map/ppermute | solution.py:49
  44.3 15.2 %collective-permute-start.3 = (f32[6,4,4,128]{3,2,1,0:T(4,128)S(1)}, f32[6,4,4,128]{3,2,1,0:T(4,128)S(1)}, u32[]{:S(2)}, u32[]{:S(2)}) collective-permute-start(f32[6,4,4,128]{3,2,1,0:T(4,128)S(1)} %get-tuple-element.17), channel_id=1, source_target_pairs={{0,4},{4,0},{8,12},{12,8},{16,20},{20,16},{24,28},{28,24},{1,5},{5... | collective-permute-start | bytes 147464 | tf_op jit(solution)/shard_map/ppermute | solution.py:50
  59.6 38.2 %collective-permute-start.5 = (f32[6,4,16,128]{3,2,1,0:T(8,128)S(1)}, f32[6,4,16,128]{3,2,1,0:T(8,128)S(1)}, u32[]{:S(2)}, u32[]{:S(2)}) collective-permute-start(f32[6,4,16,128]{3,2,1,0:T(8,128)S(1)} %pad_maximum_fusion.own_ref), channel_id=1, source_target_pairs={{0,992},{32,64},{64,32},{96,128},{128,96},{160,192},{192,160},{224... | collective-permute-start | bytes 589832 | tf_op jit(solution)/shard_map/ppermute | solution.py:49
  62.8 35.0 %collective-permute-start.4 = (f32[6,4,16,128]{3,2,1,0:T(8,128)S(1)}, f32[6,4,16,128]{3,2,1,0:T(8,128)S(1)}, u32[]{:S(2)}, u32[]{:S(2)}) collective-permute-start(f32[6,4,16,128]{3,2,1,0:T(8,128)S(1)} %pad_maximum_fusion.own_ref), channel_id=1, source_target_pairs={{0,32},{32,0},{64,96},{96,64},{128,160},{160,128},{192,224},{224,1... | collective-permute-start | bytes 589832 | tf_op jit(solution)/shard_map/ppermute | solution.py:50

commit v7 on v6

--- a/solution.py
+++ b/solution.py
@@ -28,7 +28,6 @@
         for c in range(columns)
         for place in range(width)
     ]
-    value = jnp.broadcast_to(value, (deep, 1, 1))
     return lax.all_to_all(value, ALL, 0, 0, axis_index_groups=groups, tiled=True)
 
 
@@ -170,6 +169,82 @@
     )(pltpu.with_memory_space_constraint(everyone, pltpu.VMEM))
 
 
+def lane_ids():
+    return lax.broadcasted_iota(jnp.int32, (8, 128), 1)
+
+
+def pack_kernel(state_ref, out_ref, wide):
+    lanes = lane_ids()
+    for c in range(6):
+        for layer in range(4):
+            wide[c, layer, :, 0:120] = state_ref[c, layer]
+    fastest = jnp.zeros((8, 128), jnp.float32)
+    for layer in range(4):
+        signal = fastest_signal([wide[c, layer] for c in range(6)])
+        fastest = jnp.maximum(fastest, jnp.where(lanes < 120, signal, 0.0))
+    first = last = jnp.full((8, 128), jnp.max(fastest))
+    for c in range(6):
+        for layer in range(4):
+            spot = 4 * (4 * c + layer)
+            here = (lanes >= spot) & (lanes < spot + 4)
+            first = jnp.where(here, roll(wide[c, layer], spot, 1), first)
+            last = jnp.where(here, roll(wide[c, layer], spot - 116, 1), last)
+    above = lax.rem(lax.axis_index("y") + 1, 4)
+    for y in range(4):
+        tile = jnp.where(above == y, last, first)
+        for place in range(y, 32, 4):
+            out_ref[place] = tile
+
+
+def unpack_kernel(state_ref, tiles_ref, block_ref, column_ref):
+    lanes = lane_ids()
+    fastest = tiles_ref[0]
+    for place in range(1, 32):
+        fastest = jnp.maximum(fastest, tiles_ref[place])
+    fastest = jnp.max(jnp.where(lanes >= 96, fastest, 0.0))
+    column_ref[...] = jnp.full(column_ref.shape, fastest)
+    y = lax.axis_index("y")
+    base = 16 * lax.axis_index("c") + 4 * lax.axis_index("x")
+    below = tiles_ref[base + lax.rem(y + 3, 4)]
+    above = tiles_ref[base + lax.rem(y + 1, 4)]
+    for c in range(6):
+        for layer in range(4):
+            spot = 4 * (4 * c + layer)
+            ghosts = jnp.where(lanes < 124, roll(above, 120 - spot, 1), roll(below, 124 - spot, 1))
+            block_ref[c, layer] = ghosts
+            block_ref[c, layer, :, 0:120] = state_ref[c, layer]
+
+
+def in_vmem(*arrays):
+    return [pltpu.with_memory_space_constraint(item, pltpu.VMEM) for item in arrays]
+
+
+def packed(state):
+    vmem = pl.BlockSpec(memory_space=pltpu.VMEM)
+    return pl.pallas_call(
+        pack_kernel,
+        in_specs=[vmem],
+        out_specs=vmem,
+        out_shape=jax.ShapeDtypeStruct((32, 8, 128), jnp.float32),
+        scratch_shapes=[pltpu.VMEM((6, 4, 8, 128), jnp.float32)],
+        name="pack",
+    )(*in_vmem(state))
+
+
+def unpacked(state, tiles, count):
+    vmem = pl.BlockSpec(memory_space=pltpu.VMEM)
+    return pl.pallas_call(
+        unpack_kernel,
+        in_specs=[vmem, vmem],
+        out_specs=[vmem, vmem],
+        out_shape=[
+            jax.ShapeDtypeStruct((6, 4, 8, 128), jnp.float32),
+            jax.ShapeDtypeStruct((count, 1, 1), jnp.float32),
+        ],
+        name="unpack",
+    )(*in_vmem(state, tiles))
+
+
 def kernel(column_ref, even_ref, own_ref, odd_ref, out_ref, signal_ref, prim, lower, upper, fluxes, gx):
     step = jnp.max(courant / maximum_of(column_ref))
     half = 0.5 * step
@@ -242,7 +317,7 @@
     first = tuple(corrected([upper[0, c, 0, 0:8] for c in range(6)], change))
     lax.fori_loop(0, 5, final_first, first)
 
-    lanes = lax.broadcasted_iota(jnp.int32, (8, 128), 1) < 120
+    lanes = lane_ids() < 120
 
     def final(index, fastest):
         here = index + 1
@@ -292,14 +367,10 @@
 
 
 def step(conserved_state):
-    signal_now = jnp.max(fastest_signal([conserved_state[component] for component in range(6)]))
-    block = padded(conserved_state, GZ, lax.axis_index("y") % 2 == 1, 3, GHOST)
-    to_plane = jnp.broadcast_to(signal_now, (lax.axis_size(PLANE), 1, 1))
-    block, to_plane = lax.optimization_barrier((block, to_plane))
-    signal_now = jnp.max(lax.all_to_all(to_plane, PLANE, 0, 0, tiled=True))
+    tiles = lax.all_to_all(packed(conserved_state), PLANE, 0, 0, tiled=True)
+    block, to_column = unpacked(conserved_state, tiles, lax.axis_size(COLUMN))
+    column = over_column(to_column, 8)
     block = padded(block, GY, lax.axis_index("x") % 2 == 1, 2, GHOST)
-    block, _ = lax.optimization_barrier((block, signal_now))
-    column = over_column(signal_now, 8)
     by_even, by_odd = swapped(block, GX, lax.axis_index("c") == 1, 1, GHOST)
     updated, to_plane = hydro_step(column, by_even, block, by_odd, lax.axis_size(PLANE))
     plane = lax.all_to_all(to_plane, PLANE, 0, 0, tiled=True)

time: 152 us -> 158 us (1.039)
  blocking collectives: 84.1 us -> 73.4 us
  waiting for transfers between devices: 2.81 us -> 10.8 us
  starting transfers between devices: 51.5 us -> 59.1 us
  Pallas kernels: 6.09 us -> 7.72 us
    all_to_all x0 -> x1, starting transfers between devices: none -> 17.7 us  [step(): tiles = lax.all_to_all(packed(conserved_state), PLANE, 0, 0, tiled=True)]
    ppermute x3 -> x2, starting transfers between devices: 39.6 us -> 24.3 us  [swapped(): by_odd = lax.ppermute(to_odd, axes, odd)]
    all_to_all x1 -> x0, blocking collectives: 12.6 us -> none  [step(): signal_now = jnp.max(lax.all_to_all(to_plane, PLANE, 0, 0, tiled=True))]
    all_to_all x0 -> x1, waiting for transfers between devices: none -> 7.55 us  [step(): tiles = lax.all_to_all(packed(conserved_state), PLANE, 0, 0, tiled=True)]
    ppermute x3 -> x2, starting transfers between devices: 11.9 us -> 17.1 us  [swapped(): by_even = lax.ppermute(to_even, axes, even)]
    ppermute x3 -> x2, waiting for transfers between devices: 0.01 us -> 3.13 us  [swapped(): by_odd = lax.ppermute(to_odd, axes, odd)]
    all_to_all x1, blocking collectives: 26.2 us -> 29 us  [over_column(): lax.all_to_all(value, ALL, 0, 0, axis_index_groups=groups, tiled=True)]
    ppermute x3 -> x2, waiting for transfers between devices: 2.8 us -> 0.07 us  [swapped(): by_even = lax.ppermute(to_even, axes, even)]
  transfers between devices with their start and end apart: 6 -> 5, of which waited for: 1 -> 3; matrix products, arithmetic and copies ran while one was open for 1% -> 0% of each run, Pallas kernels for 0% -> 0%
where the time goes in v7:
time: 158 us; the launch traced here: 157 us
  blocking collectives  73.4 us (46%)
  starting transfers between devices  59.1 us (37%)
  waiting for transfers between devices  10.8 us (7%)
  Pallas kernels  7.72 us (5%)
  between operations  2.53 us (2%)
  local copies, waits for them, and re-layouts  1.77 us (1%)
  other arithmetic  1.66 us (1%)
    all_to_all x1, blocking collectives, step(): column = lax.all_to_all(to_column, COLUMN, 0, 0, tiled=True)  32.3 us
    all_to_all x1, blocking collectives, over_column(): lax.all_to_all(value, ALL, 0, 0, axis_index_groups=groups, tiled=True)  29 us
    ppermute x2, starting transfers between devices, swapped(): by_odd = lax.ppermute(to_odd, axes, odd)  24.3 us
    all_to_all x1, starting transfers between devices, step(): tiles = lax.all_to_all(packed(conserved_state), PLANE, 0, 0, tiled=True)  17.7 us
    ppermute x2, starting transfers between devices, swapped(): by_even = lax.ppermute(to_even, axes, even)  17.1 us
    all_to_all x1, blocking collectives, step(): plane = lax.all_to_all(to_plane, PLANE, 0, 0, tiled=True)  12.1 us
    all_to_all x1, waiting for transfers between devices, step(): tiles = lax.all_to_all(packed(conserved_state), PLANE, 0, 0, tiled=True)  7.55 us
    pallas_call x1, Pallas kernels, hydro_step(): pl.pallas_call(kernel, in_specs=[vmem] * 4, out_specs=[vmem, vmem], out_s...  5.45 us
  transfers between devices with their start and end apart: 5, of which 3 were waited for; matrix products, arithmetic and copies ran while one was open for 0% of the time, Pallas kernels for 0%

profile of v7, /device:TPU:1, one launch (start us, length us, event | category | flops | bytes accessed | tf_op | source)
XLA Modules:
  0.0 156.9 jit_solution(9402817663436801692)
XLA Ops:
  0.6 0.0 copy-start
  0.6 0.9 copy-done
  1.5 0.8 pack.1
  2.3 17.7 %all-to-all-start = ((f32[32,8,128]{2,1,0:T(8,128)}), f32[32,8,128]{2,1,0:T(8,128)S(1)}, u32[]{:S(2)}, u32[]{:S(2)}) async-start(f32[32,8,128]{2,1,0:T(8,128)} %pack.1), calls=%async_computation | async-start | bytes 262144 | tf_op jit(solution)/shard_map/all_to_all | solution.py:370
  20.1 7.6 %all-to-all-done.tiles_ref = f32[32,8,128]{2,1,0:T(8,128)S(1)} async-done(((f32[32,8,128]{2,1,0:T(8,128)}), f32[32,8,128]{2,1,0:T(8,128)S(1)}, u32[]{:S(2)}, u32[]{:S(2)}) %all-to-all-start) | async-done | bytes 131104 | tf_op jit(solution)/shard_map/all_to_all | solution.py:370
  27.6 0.8 unpack.1
  28.4 1.0 slice_select_fusion.1
  29.4 20.2 %collective-permute-start = (f32[6,4,4,128]{3,2,1,0:T(4,128)S(1)}, f32[6,4,4,128]{3,2,1,0:T(4,128)S(1)}, u32[]{:S(2)}, u32[]{:S(2)}) collective-permute-start(f32[6,4,4,128]{3,2,1,0:T(4,128)S(1)} %get-tuple-element.12), channel_id=1, source_target_pairs={{0,28},{4,8},{8,4},{12,16},{16,12},{20,24},{24,20},{28,0},{1,29},{... | collective-permute-start | bytes 147464 | tf_op jit(solution)/shard_map/ppermute | solution.py:48
  49.6 1.9 %collective-permute-start.1 = (f32[6,4,4,128]{3,2,1,0:T(4,128)S(1)}, f32[6,4,4,128]{3,2,1,0:T(4,128)S(1)}, u32[]{:S(2)}, u32[]{:S(2)}) collective-permute-start(f32[6,4,4,128]{3,2,1,0:T(4,128)S(1)} %get-tuple-element.13), channel_id=1, source_target_pairs={{0,4},{4,0},{8,12},{12,8},{16,20},{20,16},{24,28},{28,24},{1,5},{5... | collective-permute-start | bytes 147464 | tf_op jit(solution)/shard_map/ppermute | solution.py:49
  51.6 3.1 %collective-permute-done = f32[6,4,4,128]{3,2,1,0:T(4,128)S(1)} collective-permute-done((f32[6,4,4,128]{3,2,1,0:T(4,128)S(1)}, f32[6,4,4,128]{3,2,1,0:T(4,128)S(1)}, u32[]{:S(2)}, u32[]{:S(2)}) %collective-permute-start) | collective-permute-done | bytes 49184 | tf_op jit(solution)/shard_map/ppermute | solution.py:48
  54.7 0.1 collective-permute-done.1
  54.8 0.0 copy-start.1
  54.8 0.9 copy-done.1
  55.7 0.0 copy-start.2
  55.7 4.1 %collective-permute-start.3 = (f32[6,4,16,128]{3,2,1,0:T(8,128)S(1)}, f32[6,4,16,128]{3,2,1,0:T(8,128)S(1)}, u32[]{:S(2)}, u32[]{:S(2)}) collective-permute-start(f32[6,4,16,128]{3,2,1,0:T(8,128)S(1)} %pad_maximum_fusion.own_ref), channel_id=1, source_target_pairs={{0,992},{32,64},{64,32},{96,128},{128,96},{160,192},{192,160},{224... | collective-permute-start | bytes 589832 | tf_op jit(solution)/shard_map/ppermute | solution.py:48
  59.8 15.2 %collective-permute-start.2 = (f32[6,4,16,128]{3,2,1,0:T(8,128)S(1)}, f32[6,4,16,128]{3,2,1,0:T(8,128)S(1)}, u32[]{:S(2)}, u32[]{:S(2)}) collective-permute-start(f32[6,4,16,128]{3,2,1,0:T(8,128)S(1)} %pad_maximum_fusion.own_ref), channel_id=1, source_target_pairs={{0,32},{32,0},{64,96},{96,64},{128,160},{160,128},{192,224},{224,1... | collective-permute-start | bytes 589832 | tf_op jit(solution)/shard_map/ppermute | solution.py:49
  74.9 0.0 copy-done.2
  75.0 29.0 %all_to_all.20.column_ref = f32[32,1,1]{2,1,0:T(1,128)S(1)} all-to-all(f32[32,1,1]{2,1,0:T(1,128)S(1)} %copy-done.2), channel_id=1, replica_groups={{512,576,640,704,768,832,896,960,16,80,144,208,272,336,400,464,528,592,..., dimensions={0} | all-to-all | bytes 256 | tf_op jit(solution)/shard_map/all_to_all | solution.py:31
  103.9 0.0 collective-permute-done.3.odd_ref
  103.9 0.0 collective-permute-done.2.even_ref
  103.9 5.5 %hydro.1 = (f32[6,4,8,120]{3,2,1,0:T(8,128)}, f32[32,1,1]{2,1,0:T(1,128)}) custom-call(f32[32,1,1]{2,1,0:T(1,128)S(1)} %all_to_all.20.column_ref, f32[6,4,16,128]{3,2,1,0:T(8,128)S(1)} %collective-permute-done.2.even_ref, f32[6,4,16,128]{3,2,1,0:T(8,128)S(1)} %pad_maximum_fusion.own_ref, f32[6,4,16,128]{3,2,1,0:T(8,128)S(1)} %collective-permute-done.3.odd_ref), custom_call_target="tpu_custom_call" | custom-call | tf_op jit(solution)/shard_map/hydro/pallas_call | solution.py:350
  109.4 12.1 %all_to_all.21.everyone_ref = f32[32,1,1]{2,1,0:T(1,128)S(1)} all-to-all(f32[32,1,1]{2,1,0:T(1,128)} %get-tuple-element.9), channel_id=1, replica_groups=mesh['zl'=16,'c'=2,'zh'=2,'x'=4,'y'=4] {'c','x','y'}, dimensions={0} | all-to-all | bytes 256 | tf_op jit(solution)/shard_map/all_to_all | solution.py:376
  121.5 0.6 spread.1
  122.1 32.3 %all_to_all.22 = f32[32,1,1]{2,1,0:T(1,128)S(1)} all-to-all(f32[32,1,1]{2,1,0:T(1,128)} %spread.1), channel_id=1, replica_groups=mesh['zl'=16,'c'=2,'zh'=2,'x'=4,'y'=4] {'zl','zh'}, dimensions={0} | all-to-all | bytes 256 | tf_op jit(solution)/shard_map/all_to_all | solution.py:378
  154.5 0.6 reduce_max.9
  (2 shorter events, 0.0 us)
Async XLA Ops:
  0.6 0.9 copy-start
  2.3 25.3 %all-to-all-start = ((f32[32,8,128]{2,1,0:T(8,128)}), f32[32,8,128]{2,1,0:T(8,128)S(1)}, u32[]{:S(2)}, u32[]{:S(2)}) async-start(f32[32,8,128]{2,1,0:T(8,128)} %pack.1), calls=%async_computation | async-start | bytes 262144 | tf_op jit(solution)/shard_map/all_to_all | solution.py:370
  29.4 25.3 %collective-permute-start = (f32[6,4,4,128]{3,2,1,0:T(4,128)S(1)}, f32[6,4,4,128]{3,2,1,0:T(4,128)S(1)}, u32[]{:S(2)}, u32[]{:S(2)}) collective-permute-start(f32[6,4,4,128]{3,2,1,0:T(4,128)S(1)} %get-tuple-element.12), channel_id=1, source_target_pairs={{0,28},{4,8},{8,4},{12,16},{16,12},{20,24},{24,20},{28,0},{1,29},{... | collective-permute-start | bytes 147464 | tf_op jit(solution)/shard_map/ppermute | solution.py:48
  49.6 5.1 %collective-permute-start.1 = (f32[6,4,4,128]{3,2,1,0:T(4,128)S(1)}, f32[6,4,4,128]{3,2,1,0:T(4,128)S(1)}, u32[]{:S(2)}, u32[]{:S(2)}) collective-permute-start(f32[6,4,4,128]{3,2,1,0:T(4,128)S(1)} %get-tuple-element.13), channel_id=1, source_target_pairs={{0,4},{4,0},{8,12},{12,8},{16,20},{20,16},{24,28},{28,24},{1,5},{5... | collective-permute-start | bytes 147464 | tf_op jit(solution)/shard_map/ppermute | solution.py:49
  54.8 0.9 copy-start.1
  55.7 19.3 %copy-start.2 = (f32[32,1,1]{2,1,0:T(1,128)S(1)}, f32[32,1,1]{2,1,0:T(1,128)}, u32[]{:S(2)}) copy-start(f32[32,1,1]{2,1,0:T(1,128)} %get-tuple-element.6) | copy-start | bytes 388
  55.7 48.2 %collective-permute-start.3 = (f32[6,4,16,128]{3,2,1,0:T(8,128)S(1)}, f32[6,4,16,128]{3,2,1,0:T(8,128)S(1)}, u32[]{:S(2)}, u32[]{:S(2)}) collective-permute-start(f32[6,4,16,128]{3,2,1,0:T(8,128)S(1)} %pad_maximum_fusion.own_ref), channel_id=1, source_target_pairs={{0,992},{32,64},{64,32},{96,128},{128,96},{160,192},{192,160},{224... | collective-permute-start | bytes 589832 | tf_op jit(solution)/shard_map/ppermute | solution.py:48
  59.8 44.2 %collective-permute-start.2 = (f32[6,4,16,128]{3,2,1,0:T(8,128)S(1)}, f32[6,4,16,128]{3,2,1,0:T(8,128)S(1)}, u32[]{:S(2)}, u32[]{:S(2)}) collective-permute-start(f32[6,4,16,128]{3,2,1,0:T(8,128)S(1)} %pad_maximum_fusion.own_ref), channel_id=1, source_target_pairs={{0,32},{32,0},{64,96},{96,64},{128,160},{160,128},{192,224},{224,1... | collective-permute-start | bytes 589832 | tf_op jit(solution)/shard_map/ppermute | solution.py:49

commit v8 on v7

--- a/solution.py
+++ b/solution.py
@@ -37,23 +37,28 @@
     return even, odd
 
 
-def swapped(block, axes, parity, dim, width):
-    even, odd = swaps(lax.axis_size(axes))
-    first = lax.slice_in_dim(block, 0, width, axis=dim)
-    last = lax.slice_in_dim(block, block.shape[dim] - width, None, axis=dim)
-    if block.shape[dim] == width:
-        to_even, to_odd = block, block
-    else:
-        to_even, to_odd = jnp.where(parity, first, last), jnp.where(parity, last, first)
-    by_odd = lax.ppermute(to_odd, axes, odd)
-    by_even = lax.ppermute(to_even, axes, even)
-    return by_even, by_odd
-
-
-def padded(block, axes, parity, dim, width):
-    by_even, by_odd = swapped(block, axes, parity, dim, width)
-    low, high = jnp.where(parity, by_even, by_odd), jnp.where(parity, by_odd, by_even)
-    return jnp.concatenate([block, high, low], axis=dim)
+def swap(block, axes, odd):
+    return lax.ppermute(block, axes, swaps(lax.axis_size(axes))[odd])
+
+
+def corner_swap():
+    sizes = [lax.axis_size(axis) for axis in ALL]
+    rows, cores, halves, columns, width = sizes
+    _, odd_first = swaps(rows * cores)
+    _, odd_second = swaps(halves * columns)
+    pairs = []
+    for first in range(rows * cores):
+        for second in range(halves * columns):
+            far_first, far_second = first in (0, rows * cores - 1), second % columns in (0, columns - 1)
+            to_first = odd_first[first][1] if far_second else first
+            to_second = second if far_second and not far_first else odd_second[second][1]
+            if far_first and not far_second:
+                to_first = first
+            for y in range(width):
+                here = (first * halves * columns + second) * width + y
+                there = (to_first * halves * columns + to_second) * width + y
+                pairs.append((here, there))
+    return pairs
 
 
 def roll(value, shift, axis):
@@ -196,7 +201,7 @@
             out_ref[place] = tile
 
 
-def unpack_kernel(state_ref, tiles_ref, block_ref, column_ref):
+def unpack_kernel(state_ref, tiles_ref, block_ref, even_ref, odd_ref, column_ref):
     lanes = lane_ids()
     fastest = tiles_ref[0]
     for place in range(1, 32):
@@ -205,6 +210,7 @@
     column_ref[...] = jnp.full(column_ref.shape, fastest)
     y = lax.axis_index("y")
     base = 16 * lax.axis_index("c") + 4 * lax.axis_index("x")
+    odd = lax.rem(lax.axis_index("x"), 2) == 1
     below = tiles_ref[base + lax.rem(y + 3, 4)]
     above = tiles_ref[base + lax.rem(y + 1, 4)]
     for c in range(6):
@@ -213,6 +219,10 @@
             ghosts = jnp.where(lanes < 124, roll(above, 120 - spot, 1), roll(below, 124 - spot, 1))
             block_ref[c, layer] = ghosts
             block_ref[c, layer, :, 0:120] = state_ref[c, layer]
+            whole = block_ref[c, layer]
+            first, last = whole[0:4], whole[4:8]
+            even_ref[c, layer] = jnp.where(odd, first, last)
+            odd_ref[c, layer] = jnp.where(odd, last, first)
 
 
 def in_vmem(*arrays):
@@ -235,10 +245,12 @@
     vmem = pl.BlockSpec(memory_space=pltpu.VMEM)
     return pl.pallas_call(
         unpack_kernel,
-        in_specs=[vmem, vmem],
-        out_specs=[vmem, vmem],
+        in_specs=[vmem] * 2,
+        out_specs=[vmem] * 4,
         out_shape=[
             jax.ShapeDtypeStruct((6, 4, 8, 128), jnp.float32),
+            jax.ShapeDtypeStruct((6, 4, 4, 128), jnp.float32),
+            jax.ShapeDtypeStruct((6, 4, 4, 128), jnp.float32),
             jax.ShapeDtypeStruct((count, 1, 1), jnp.float32),
         ],
         name="unpack",
@@ -366,13 +378,34 @@
     )(*blocks)
 
 
+def cyclic(block, by_even, by_odd, odd):
+    above, below = jnp.where(odd, by_odd, by_even), jnp.where(odd, by_even, by_odd)
+    return jnp.concatenate([block, above, below], axis=2)
+
+
 def step(conserved_state):
     tiles = lax.all_to_all(packed(conserved_state), PLANE, 0, 0, tiled=True)
-    block, to_column = unpacked(conserved_state, tiles, lax.axis_size(COLUMN))
+    block, to_even, to_odd, to_column = unpacked(
+        conserved_state, tiles, lax.axis_size(COLUMN)
+    )
+    x, chip_row, core = (lax.axis_index(axis) for axis in ("x", "zl", "c"))
+    odd = x % 2 == 1
+    far_second = (x == 0) | (x == lax.axis_size("x") - 1)
+    far_first = ((core == 0) & (chip_row == 0)) | ((core == 1) & (chip_row == lax.axis_size("zl") - 1))
+    beside_odd = swap(to_odd, GY, 1)
+    ahead_odd = swap(block, GX, 1)
+    beside_even = swap(to_even, GY, 0)
     column = over_column(to_column, 8)
-    block = padded(block, GY, lax.axis_index("x") % 2 == 1, 2, GHOST)
-    by_even, by_odd = swapped(block, GX, lax.axis_index("c") == 1, 1, GHOST)
-    updated, to_plane = hydro_step(column, by_even, block, by_odd, lax.axis_size(PLANE))
+    own = cyclic(block, beside_even, beside_odd, odd)
+    by_even = swap(own, GX, 0)
+    low, high = ahead_odd[:, :, :GHOST], ahead_odd[:, :, GHOST:]
+    corner_even = swap(jnp.where(odd, low, high), GY, 0)
+    kept = jnp.where(far_first, to_odd, beside_odd)
+    corner_odd = lax.ppermute(
+        jnp.where(far_second, kept, jnp.where(odd, high, low)), ALL, corner_swap()
+    )
+    by_odd = cyclic(ahead_odd, corner_even, corner_odd, odd)
+    updated, to_plane = hydro_step(column, by_even, own, by_odd, lax.axis_size(PLANE))
     plane = lax.all_to_all(to_plane, PLANE, 0, 0, tiled=True)
     to_column = spread(plane, lax.axis_size(COLUMN))
     column = lax.all_to_all(to_column, COLUMN, 0, 0, tiled=True)

time: 158 us -> 138 us (0.87)
  waiting for transfers between devices: 10.8 us -> 1.26 us
  starting transfers between devices: 59.1 us -> 55 us
  blocking collectives: 73.4 us -> 69.4 us
    all_to_all x1, waiting for transfers between devices: 7.55 us -> 1.25 us  [over_column(): lax.all_to_all(value, ALL, 0, 0, axis_index_groups=groups, tiled=True)]
    ppermute x4 -> x6, starting transfers between devices: 41.4 us -> 36.3 us  [the longest x5 33.9 us: swap(): return lax.ppermute(block, axes, swaps(lax.axis_size(axes))[odd])]
    all_to_all x1, blocking collectives: 29 us -> 25.3 us  [step(): tiles = lax.all_to_all(packed(conserved_state), PLANE, 0, 0, tiled=True)]
    ppermute x4 -> x6, waiting for transfers between devices: 3.21 us -> 0.02 us  [the longest x5 0.01 us: swap(): return lax.ppermute(block, axes, swaps(lax.axis_size(axes))[odd])]
  transfers between devices with their start and end apart: 5 -> 7, of which waited for: 3 -> 1; matrix products, arithmetic and copies ran while one was open for 0% -> 0% of each run, Pallas kernels for 0% -> 0%
where the time goes in v8:
time: 138 us
  blocking collectives  69.4 us (50%)
  starting transfers between devices  55 us (40%)
  Pallas kernels  7.74 us (6%)
  between operations  2.64 us (2%)
    ppermute x5, starting transfers between devices, swap(): return lax.ppermute(block, axes, swaps(lax.axis_size(axes))[odd])  33.9 us
    all_to_all x1, blocking collectives, step(): column = lax.all_to_all(to_column, COLUMN, 0, 0, tiled=True)  31.7 us
    all_to_all x1, blocking collectives, step(): tiles = lax.all_to_all(packed(conserved_state), PLANE, 0, 0, tiled=True)  25.3 us
    all_to_all x1, starting transfers between devices, over_column(): lax.all_to_all(value, ALL, 0, 0, axis_index_groups=groups, tiled=True)  18.7 us
    all_to_all x1, blocking collectives, step(): plane = lax.all_to_all(to_plane, PLANE, 0, 0, tiled=True)  12.4 us
    pallas_call x1, Pallas kernels, hydro_step(): pl.pallas_call(kernel, in_specs=[vmem] * 4, out_specs=[vmem, vmem], out_s...  5.44 us
  transfers between devices with their start and end apart: 7, of which 1 were waited for; matrix products, arithmetic and copies ran while one was open for 0% of the time, Pallas kernels for 0%

profile of v8, /device:TPU:1, one launch (start us, length us, event | category | flops | bytes accessed | tf_op | source)
XLA Modules:
  0.0 137.7 jit_solution(1160821794364916958)
XLA Ops:
  0.6 0.0 copy-start
  0.6 0.9 copy-done
  1.5 0.8 pack.1
  2.3 25.3 %all_to_all.20.tiles_ref = f32[32,8,128]{2,1,0:T(8,128)S(1)} all-to-all(f32[32,8,128]{2,1,0:T(8,128)} %pack.1), channel_id=1, replica_groups=mesh['zl'=16,'c'=2,'zh'=2,'x'=4,'y'=4] {'c','x','y'}, dimensions={0} | all-to-all | bytes 262144 | tf_op jit(solution)/shard_map/all_to_all | solution.py:387
  27.6 0.8 unpack.1
  28.5 1.9 %collective-permute-start.3 = (f32[6,4,8,128]{3,2,1,0:T(8,128)}, f32[6,4,8,128]{3,2,1,0:T(8,128)S(1)}, u32[]{:S(2)}, u32[]{:S(2)}) collective-permute-start(f32[6,4,8,128]{3,2,1,0:T(8,128)} %get-tuple-element.9), channel_id=1, source_target_pairs={{0,992},{32,64},{64,32},{96,128},{128,96},{160,192},{192,160},{224... | collective-permute-start | bytes 294920 | tf_op jit(solution)/shard_map/ppermute | solution.py:41
  30.4 0.0 copy-start.2
  30.4 2.4 %collective-permute-start.1 = (f32[6,4,4,128]{3,2,1,0:T(4,128)}, f32[6,4,4,128]{3,2,1,0:T(4,128)S(1)}, u32[]{:S(2)}, u32[]{:S(2)}) collective-permute-start(f32[6,4,4,128]{3,2,1,0:T(4,128)} %get-tuple-element.11), channel_id=1, source_target_pairs={{0,4},{4,0},{8,12},{12,8},{16,20},{20,16},{24,28},{28,24},{1,5},{5... | collective-permute-start | bytes 147464 | tf_op jit(solution)/shard_map/ppermute | solution.py:41
  32.8 21.5 %collective-permute-start = (f32[6,4,4,128]{3,2,1,0:T(4,128)}, f32[6,4,4,128]{3,2,1,0:T(4,128)S(1)}, u32[]{:S(2)}, u32[]{:S(2)}) collective-permute-start(f32[6,4,4,128]{3,2,1,0:T(4,128)} %get-tuple-element.10), channel_id=1, source_target_pairs={{0,28},{4,8},{8,4},{12,16},{16,12},{20,24},{24,20},{28,0},{1,29},{... | collective-permute-start | bytes 147464 | tf_op jit(solution)/shard_map/ppermute | solution.py:41
  54.4 18.7 %all-to-all-start.1 = ((f32[32,1,1]{2,1,0:T(1,128)}), f32[32,1,1]{2,1,0:T(1,128)S(1)}, u32[]{:S(2)}, u32[]{:S(2)}) async-start(f32[32,1,1]{2,1,0:T(1,128)} %get-tuple-element.8), calls=%async_computation.1 | async-start | bytes 32768 | tf_op jit(solution)/shard_map/all_to_all | solution.py:31
  73.1 0.0 copy-start.1
  73.1 0.0 collective-permute-done.1
  73.2 0.0 collective-permute-done
  73.2 0.0 collective-permute-done.3
  73.2 0.0 copy-done.2
  73.2 2.4 %collective-permute-start.4 = (f32[6,4,4,128]{3,2,1,0:T(4,128)S(1)}, f32[6,4,4,128]{3,2,1,0:T(4,128)S(1)}, u32[]{:S(2)}, u32[]{:S(2)}) collective-permute-start(f32[6,4,4,128]{3,2,1,0:T(4,128)S(1)} %get-tuple-element.16), channel_id=1, source_target_pairs={{0,1020},{1,1021},{2,1022},{3,1023},{4,8},{5,9},{6,10},{7,11},{8,4... | collective-permute-start | bytes 147464 | tf_op jit(solution)/shard_map/ppermute | solution.py:404
  75.7 1.9 %collective-permute-start.5 = (f32[6,4,4,128]{3,2,1,0:T(4,128)S(1)}, f32[6,4,4,128]{3,2,1,0:T(4,128)S(1)}, u32[]{:S(2)}, u32[]{:S(2)}) collective-permute-start(f32[6,4,4,128]{3,2,1,0:T(4,128)S(1)} %get-tuple-element.17), channel_id=1, source_target_pairs={{0,4},{4,0},{8,12},{12,8},{16,20},{20,16},{24,28},{28,24},{1,5},{5... | collective-permute-start | bytes 147464 | tf_op jit(solution)/shard_map/ppermute | solution.py:41
  77.6 0.0 copy-done.1
  77.7 6.1 %collective-permute-start.2 = (f32[6,4,16,128]{3,2,1,0:T(8,128)S(1)}, f32[6,4,16,128]{3,2,1,0:T(8,128)S(1)}, u32[]{:S(2)}, u32[]{:S(2)}) collective-permute-start(f32[6,4,16,128]{3,2,1,0:T(8,128)S(1)} %pad_maximum_fusion.own_ref), channel_id=1, source_target_pairs={{0,32},{32,0},{64,96},{96,64},{128,160},{160,128},{192,224},{224,1... | collective-permute-start | bytes 589832 | tf_op jit(solution)/shard_map/ppermute | solution.py:41
  83.7 0.0 collective-permute-done.4
  83.8 0.0 collective-permute-done.5
  83.8 1.2 all-to-all-done.1.column_ref
  85.1 0.0 collective-permute-done.2.even_ref
  85.1 5.4 %hydro.1 = (f32[6,4,8,120]{3,2,1,0:T(8,128)}, f32[32,1,1]{2,1,0:T(1,128)}) custom-call(f32[32,1,1]{2,1,0:T(1,128)S(1)} %all-to-all-done.1.column_ref, f32[6,4,16,128]{3,2,1,0:T(8,128)S(1)} %collective-permute-done.2.even_ref, f32[6,4,16,128]{3,2,1,0:T(8,128)S(1)} %pad_maximum_fusion.own_ref, f32[6,4,16,128]{3,2,1,0:T(8,128)S(1)} %pad_maximum_fusion.1.odd_ref), custom_call_target="tpu_custom_call" | custom-call | tf_op jit(solution)/shard_map/hydro/pallas_call | solution.py:362
  90.5 12.4 %all_to_all.21.everyone_ref = f32[32,1,1]{2,1,0:T(1,128)S(1)} all-to-all(f32[32,1,1]{2,1,0:T(1,128)} %get-tuple-element.13), channel_id=1, replica_groups=mesh['zl'=16,'c'=2,'zh'=2,'x'=4,'y'=4] {'c','x','y'}, dimensions={0} | all-to-all | bytes 256 | tf_op jit(solution)/shard_map/all_to_all | solution.py:409
  102.9 0.6 spread.1
  103.5 31.7 %all_to_all.22 = f32[32,1,1]{2,1,0:T(1,128)S(1)} all-to-all(f32[32,1,1]{2,1,0:T(1,128)} %spread.1), channel_id=1, replica_groups=mesh['zl'=16,'c'=2,'zh'=2,'x'=4,'y'=4] {'zl','zh'}, dimensions={0} | all-to-all | bytes 256 | tf_op jit(solution)/shard_map/all_to_all | solution.py:411
  135.3 0.6 reduce_max.9
  (4 shorter events, 0.1 us)
Async XLA Ops:
  0.6 0.9 copy-start
  28.5 44.7 %collective-permute-start.3 = (f32[6,4,8,128]{3,2,1,0:T(8,128)}, f32[6,4,8,128]{3,2,1,0:T(8,128)S(1)}, u32[]{:S(2)}, u32[]{:S(2)}) collective-permute-start(f32[6,4,8,128]{3,2,1,0:T(8,128)} %get-tuple-element.9), channel_id=1, source_target_pairs={{0,992},{32,64},{64,32},{96,128},{128,96},{160,192},{192,160},{224... | collective-permute-start | bytes 294920 | tf_op jit(solution)/shard_map/ppermute | solution.py:41
  30.4 42.8 %copy-start.2 = (f32[6,4,4,128]{3,2,1,0:T(4,128)S(1)}, f32[6,4,4,128]{3,2,1,0:T(4,128)}, u32[]{:S(2)}) copy-start(f32[6,4,4,128]{3,2,1,0:T(4,128)} %get-tuple-element.10) | copy-start | bytes 147460
  30.4 42.8 %collective-permute-start.1 = (f32[6,4,4,128]{3,2,1,0:T(4,128)}, f32[6,4,4,128]{3,2,1,0:T(4,128)S(1)}, u32[]{:S(2)}, u32[]{:S(2)}) collective-permute-start(f32[6,4,4,128]{3,2,1,0:T(4,128)} %get-tuple-element.11), channel_id=1, source_target_pairs={{0,4},{4,0},{8,12},{12,8},{16,20},{20,16},{24,28},{28,24},{1,5},{5... | collective-permute-start | bytes 147464 | tf_op jit(solution)/shard_map/ppermute | solution.py:41
  32.8 40.3 %collective-permute-start = (f32[6,4,4,128]{3,2,1,0:T(4,128)}, f32[6,4,4,128]{3,2,1,0:T(4,128)S(1)}, u32[]{:S(2)}, u32[]{:S(2)}) collective-permute-start(f32[6,4,4,128]{3,2,1,0:T(4,128)} %get-tuple-element.10), channel_id=1, source_target_pairs={{0,28},{4,8},{8,4},{12,16},{16,12},{20,24},{24,20},{28,0},{1,29},{... | collective-permute-start | bytes 147464 | tf_op jit(solution)/shard_map/ppermute | solution.py:41
  54.4 30.7 %all-to-all-start.1 = ((f32[32,1,1]{2,1,0:T(1,128)}), f32[32,1,1]{2,1,0:T(1,128)S(1)}, u32[]{:S(2)}, u32[]{:S(2)}) async-start(f32[32,1,1]{2,1,0:T(1,128)} %get-tuple-element.8), calls=%async_computation.1 | async-start | bytes 32768 | tf_op jit(solution)/shard_map/all_to_all | solution.py:31
  73.1 4.5 %copy-start.1 = (f32[6,4,8,128]{3,2,1,0:T(8,128)S(1)}, f32[6,4,8,128]{3,2,1,0:T(8,128)}, u32[]{:S(2)}) copy-start(f32[6,4,8,128]{3,2,1,0:T(8,128)} %get-tuple-element.9) | copy-start | bytes 294916
  73.2 10.5 %collective-permute-start.4 = (f32[6,4,4,128]{3,2,1,0:T(4,128)S(1)}, f32[6,4,4,128]{3,2,1,0:T(4,128)S(1)}, u32[]{:S(2)}, u32[]{:S(2)}) collective-permute-start(f32[6,4,4,128]{3,2,1,0:T(4,128)S(1)} %get-tuple-element.16), channel_id=1, source_target_pairs={{0,1020},{1,1021},{2,1022},{3,1023},{4,8},{5,9},{6,10},{7,11},{8,4... | collective-permute-start | bytes 147464 | tf_op jit(solution)/shard_map/ppermute | solution.py:404
  75.7 8.1 %collective-permute-start.5 = (f32[6,4,4,128]{3,2,1,0:T(4,128)S(1)}, f32[6,4,4,128]{3,2,1,0:T(4,128)S(1)}, u32[]{:S(2)}, u32[]{:S(2)}) collective-permute-start(f32[6,4,4,128]{3,2,1,0:T(4,128)S(1)} %get-tuple-element.17), channel_id=1, source_target_pairs={{0,4},{4,0},{8,12},{12,8},{16,20},{20,16},{24,28},{28,24},{1,5},{5... | collective-permute-start | bytes 147464 | tf_op jit(solution)/shard_map/ppermute | solution.py:41
  77.7 7.4 %collective-permute-start.2 = (f32[6,4,16,128]{3,2,1,0:T(8,128)S(1)}, f32[6,4,16,128]{3,2,1,0:T(8,128)S(1)}, u32[]{:S(2)}, u32[]{:S(2)}) collective-permute-start(f32[6,4,16,128]{3,2,1,0:T(8,128)S(1)} %pad_maximum_fusion.own_ref), channel_id=1, source_target_pairs={{0,32},{32,0},{64,96},{96,64},{128,160},{160,128},{192,224},{224,1... | collective-permute-start | bytes 589832 | tf_op jit(solution)/shard_map/ppermute | solution.py:41

commit v9 on v8

--- a/solution.py
+++ b/solution.py
@@ -169,7 +169,7 @@
         spread_kernel,
         in_specs=[vmem],
         out_specs=vmem,
-        out_shape=jax.ShapeDtypeStruct((count, 1, 1), jnp.float32),
+        out_shape=pltpu.VMEM((count, 1, 1), jnp.float32),
         name="spread",
     )(pltpu.with_memory_space_constraint(everyone, pltpu.VMEM))
 
@@ -248,9 +248,9 @@
         in_specs=[vmem] * 2,
         out_specs=[vmem] * 4,
         out_shape=[
-            jax.ShapeDtypeStruct((6, 4, 8, 128), jnp.float32),
-            jax.ShapeDtypeStruct((6, 4, 4, 128), jnp.float32),
-            jax.ShapeDtypeStruct((6, 4, 4, 128), jnp.float32),
+            pltpu.VMEM((6, 4, 8, 128), jnp.float32),
+            pltpu.VMEM((6, 4, 4, 128), jnp.float32),
+            pltpu.VMEM((6, 4, 4, 128), jnp.float32),
             jax.ShapeDtypeStruct((count, 1, 1), jnp.float32),
         ],
         name="unpack",
@@ -364,8 +364,8 @@
         in_specs=[vmem] * 4,
         out_specs=[vmem, vmem],
         out_shape=[
-            jax.ShapeDtypeStruct((6, 4, 8, 120), jnp.float32),
-            jax.ShapeDtypeStruct((count, 1, 1), jnp.float32),
+            pltpu.VMEM((6, 4, 8, 120), jnp.float32),
+            pltpu.VMEM((count, 1, 1), jnp.float32),
         ],
         scratch_shapes=[
             pltpu.VMEM((6, 12, 16, 128), jnp.float32),

time: 138 us -> 137 us (level)
  blocking collectives: 69.4 us -> 37.4 us
  waiting for transfers between devices: 1.26 us -> 21.5 us
  starting transfers between devices: 55 us -> 65.9 us
    all_to_all x1 -> x0, blocking collectives: 31.7 us -> none  [step(): column = lax.all_to_all(to_column, COLUMN, 0, 0, tiled=True)]
    all_to_all x0 -> x1, waiting for transfers between devices: none -> 20 us  [step(): column = lax.all_to_all(to_column, COLUMN, 0, 0, tiled=True)]
    all_to_all x0 -> x1, starting transfers between devices: none -> 11.2 us  [step(): column = lax.all_to_all(to_column, COLUMN, 0, 0, tiled=True)]
  transfers between devices with their start and end apart: 7 -> 8, of which waited for: 1 -> 2; matrix products, arithmetic and copies ran while one was open for 0% -> 1% of each run, Pallas kernels for 0% -> 0%
where the time goes in v9:
time: 137 us
  starting transfers between devices  65.9 us (48%)
  blocking collectives  37.4 us (27%)
  waiting for transfers between devices  21.5 us (16%)
  Pallas kernels  7.1 us (5%)
  between operations  2.63 us (2%)
  local copies, waits for them, and re-layouts  1.53 us (1%)
    ppermute x5, starting transfers between devices, swap(): return lax.ppermute(block, axes, swaps(lax.axis_size(axes))[odd])  33.6 us
    all_to_all x1, blocking collectives, step(): tiles = lax.all_to_all(packed(conserved_state), PLANE, 0, 0, tiled=True)  25.3 us
    all_to_all x1, waiting for transfers between devices, step(): column = lax.all_to_all(to_column, COLUMN, 0, 0, tiled=True)  20 us
    all_to_all x1, starting transfers between devices, over_column(): lax.all_to_all(value, ALL, 0, 0, axis_index_groups=groups, tiled=True)  18.7 us
    all_to_all x1, blocking collectives, step(): plane = lax.all_to_all(to_plane, PLANE, 0, 0, tiled=True)  12.2 us
    all_to_all x1, starting transfers between devices, step(): column = lax.all_to_all(to_column, COLUMN, 0, 0, tiled=True)  11.2 us
    pallas_call x1, Pallas kernels, hydro_step(): pl.pallas_call(kernel, in_specs=[vmem] * 4, out_specs=[vmem, vmem], out_s...  4.85 us
  transfers between devices with their start and end apart: 8, of which 2 were waited for; matrix products, arithmetic and copies ran while one was open for 1% of the time, Pallas kernels for 0%

profile of v9, /device:TPU:1, one launch (start us, length us, event | category | flops | bytes accessed | tf_op | source)
XLA Modules:
  0.0 136.9 jit_solution(1517789361916796637)
XLA Ops:
  0.6 0.0 copy-start
  0.6 0.9 copy-done
  1.5 0.8 pack.1
  2.3 25.3 %all_to_all.20.tiles_ref = f32[32,8,128]{2,1,0:T(8,128)S(1)} all-to-all(f32[32,8,128]{2,1,0:T(8,128)} %pack.1), channel_id=1, replica_groups=mesh['zl'=16,'c'=2,'zh'=2,'x'=4,'y'=4] {'c','x','y'}, dimensions={0} | all-to-all | bytes 262144 | tf_op jit(solution)/shard_map/all_to_all | solution.py:387
  27.6 0.8 unpack.1
  28.4 1.9 %collective-permute-start.3 = (f32[6,4,8,128]{3,2,1,0:T(8,128)S(1)}, f32[6,4,8,128]{3,2,1,0:T(8,128)S(1)}, u32[]{:S(2)}, u32[]{:S(2)}) collective-permute-start(f32[6,4,8,128]{3,2,1,0:T(8,128)S(1)} %get-tuple-element.9), channel_id=1, source_target_pairs={{0,992},{32,64},{64,32},{96,128},{128,96},{160,192},{192,160},{224... | collective-permute-start | bytes 294920 | tf_op jit(solution)/shard_map/ppermute | solution.py:41
  30.3 2.3 %collective-permute-start.1 = (f32[6,4,4,128]{3,2,1,0:T(4,128)S(1)}, f32[6,4,4,128]{3,2,1,0:T(4,128)S(1)}, u32[]{:S(2)}, u32[]{:S(2)}) collective-permute-start(f32[6,4,4,128]{3,2,1,0:T(4,128)S(1)} %get-tuple-element.11), channel_id=1, source_target_pairs={{0,4},{4,0},{8,12},{12,8},{16,20},{20,16},{24,28},{28,24},{1,5},{5... | collective-permute-start | bytes 147464 | tf_op jit(solution)/shard_map/ppermute | solution.py:41
  32.6 21.5 %collective-permute-start = (f32[6,4,4,128]{3,2,1,0:T(4,128)S(1)}, f32[6,4,4,128]{3,2,1,0:T(4,128)S(1)}, u32[]{:S(2)}, u32[]{:S(2)}) collective-permute-start(f32[6,4,4,128]{3,2,1,0:T(4,128)S(1)} %get-tuple-element.10), channel_id=1, source_target_pairs={{0,28},{4,8},{8,4},{12,16},{16,12},{20,24},{24,20},{28,0},{1,29},{... | collective-permute-start | bytes 147464 | tf_op jit(solution)/shard_map/ppermute | solution.py:41
  54.2 18.7 %all-to-all-start.1 = ((f32[32,1,1]{2,1,0:T(1,128)}), f32[32,1,1]{2,1,0:T(1,128)S(1)}, u32[]{:S(2)}, u32[]{:S(2)}) async-start(f32[32,1,1]{2,1,0:T(1,128)} %get-tuple-element.8), calls=%async_computation.1 | async-start | bytes 32768 | tf_op jit(solution)/shard_map/all_to_all | solution.py:31
  72.9 0.0 collective-permute-done.1
  73.0 0.0 collective-permute-done
  73.0 0.0 collective-permute-done.3
  73.0 2.4 %collective-permute-start.4 = (f32[6,4,4,128]{3,2,1,0:T(4,128)S(1)}, f32[6,4,4,128]{3,2,1,0:T(4,128)S(1)}, u32[]{:S(2)}, u32[]{:S(2)}) collective-permute-start(f32[6,4,4,128]{3,2,1,0:T(4,128)S(1)} %get-tuple-element.16), channel_id=1, source_target_pairs={{0,1020},{1,1021},{2,1022},{3,1023},{4,8},{5,9},{6,10},{7,11},{8,4... | collective-permute-start | bytes 147464 | tf_op jit(solution)/shard_map/ppermute | solution.py:404
  75.5 1.9 %collective-permute-start.5 = (f32[6,4,4,128]{3,2,1,0:T(4,128)S(1)}, f32[6,4,4,128]{3,2,1,0:T(4,128)S(1)}, u32[]{:S(2)}, u32[]{:S(2)}) collective-permute-start(f32[6,4,4,128]{3,2,1,0:T(4,128)S(1)} %get-tuple-element.17), channel_id=1, source_target_pairs={{0,4},{4,0},{8,12},{12,8},{16,20},{20,16},{24,28},{28,24},{1,5},{5... | collective-permute-start | bytes 147464 | tf_op jit(solution)/shard_map/ppermute | solution.py:41
  77.4 5.9 %collective-permute-start.2 = (f32[6,4,16,128]{3,2,1,0:T(8,128)S(1)}, f32[6,4,16,128]{3,2,1,0:T(8,128)S(1)}, u32[]{:S(2)}, u32[]{:S(2)}) collective-permute-start(f32[6,4,16,128]{3,2,1,0:T(8,128)S(1)} %pad_maximum_fusion.own_ref), channel_id=1, source_target_pairs={{0,32},{32,0},{64,96},{96,64},{128,160},{160,128},{192,224},{224,1... | collective-permute-start | bytes 589832 | tf_op jit(solution)/shard_map/ppermute | solution.py:41
  83.3 0.0 collective-permute-done.4
  83.3 0.0 collective-permute-done.5
  83.4 1.4 %all-to-all-done.1.column_ref = f32[32,1,1]{2,1,0:T(1,128)S(1)} async-done(((f32[32,1,1]{2,1,0:T(1,128)}), f32[32,1,1]{2,1,0:T(1,128)S(1)}, u32[]{:S(2)}, u32[]{:S(2)}) %all-to-all-start.1) | async-done | bytes 160 | tf_op jit(solution)/shard_map/all_to_all | solution.py:31
  84.8 0.0 collective-permute-done.2.even_ref
  84.8 4.8 %hydro.1 = (f32[6,4,8,120]{3,2,1,0:T(8,128)S(1)}, f32[32,1,1]{2,1,0:T(1,128)S(1)}) custom-call(f32[32,1,1]{2,1,0:T(1,128)S(1)} %all-to-all-done.1.column_ref, f32[6,4,16,128]{3,2,1,0:T(8,128)S(1)} %collective-permute-done.2.even_ref, f32[6,4,16,128]{3,2,1,0:T(8,128)S(1)} %pad_maximum_fusion.own_ref, f32[6,4,16,128]{3,2,1,0:T(8,128)S(1)} %pad_maximum_fusion.1.odd_ref), custom_call_target="tpu_custom_call" | custom-call | tf_op jit(solution)/shard_map/hydro/pallas_call | solution.py:362
  89.7 12.2 %all_to_all.21.everyone_ref = f32[32,1,1]{2,1,0:T(1,128)S(1)} all-to-all(f32[32,1,1]{2,1,0:T(1,128)S(1)} %get-tuple-element.13), channel_id=1, replica_groups=mesh['zl'=16,'c'=2,'zh'=2,'x'=4,'y'=4] {'c','x','y'}, dimensions={0} | all-to-all | bytes 256 | tf_op jit(solution)/shard_map/all_to_all | solution.py:409
  101.8 0.6 spread.1
  102.5 11.2 %all-to-all-start.3 = ((f32[32,1,1]{2,1,0:T(1,128)}), f32[32,1,1]{2,1,0:T(1,128)S(1)}, u32[]{:S(2)}, u32[]{:S(2)}) async-start(f32[32,1,1]{2,1,0:T(1,128)} %spread.1), calls=%async_computation.3 | async-start | bytes 32768 | tf_op jit(solution)/shard_map/all_to_all | solution.py:411
  113.7 0.6 copy.3
  114.4 20.0 %all-to-all-done.3 = f32[32,1,1]{2,1,0:T(1,128)S(1)} async-done(((f32[32,1,1]{2,1,0:T(1,128)}), f32[32,1,1]{2,1,0:T(1,128)S(1)}, u32[]{:S(2)}, u32[]{:S(2)}) %all-to-all-start.3) | async-done | bytes 160 | tf_op jit(solution)/shard_map/all_to_all | solution.py:411
  134.4 0.6 reduce_max.9
  (4 shorter events, 0.1 us)
Async XLA Ops:
  0.6 0.9 copy-start
  28.4 44.6 %collective-permute-start.3 = (f32[6,4,8,128]{3,2,1,0:T(8,128)S(1)}, f32[6,4,8,128]{3,2,1,0:T(8,128)S(1)}, u32[]{:S(2)}, u32[]{:S(2)}) collective-permute-start(f32[6,4,8,128]{3,2,1,0:T(8,128)S(1)} %get-tuple-element.9), channel_id=1, source_target_pairs={{0,992},{32,64},{64,32},{96,128},{128,96},{160,192},{192,160},{224... | collective-permute-start | bytes 294920 | tf_op jit(solution)/shard_map/ppermute | solution.py:41
  30.3 42.6 %collective-permute-start.1 = (f32[6,4,4,128]{3,2,1,0:T(4,128)S(1)}, f32[6,4,4,128]{3,2,1,0:T(4,128)S(1)}, u32[]{:S(2)}, u32[]{:S(2)}) collective-permute-start(f32[6,4,4,128]{3,2,1,0:T(4,128)S(1)} %get-tuple-element.11), channel_id=1, source_target_pairs={{0,4},{4,0},{8,12},{12,8},{16,20},{20,16},{24,28},{28,24},{1,5},{5... | collective-permute-start | bytes 147464 | tf_op jit(solution)/shard_map/ppermute | solution.py:41
  32.6 40.3 %collective-permute-start = (f32[6,4,4,128]{3,2,1,0:T(4,128)S(1)}, f32[6,4,4,128]{3,2,1,0:T(4,128)S(1)}, u32[]{:S(2)}, u32[]{:S(2)}) collective-permute-start(f32[6,4,4,128]{3,2,1,0:T(4,128)S(1)} %get-tuple-element.10), channel_id=1, source_target_pairs={{0,28},{4,8},{8,4},{12,16},{16,12},{20,24},{24,20},{28,0},{1,29},{... | collective-permute-start | bytes 147464 | tf_op jit(solution)/shard_map/ppermute | solution.py:41
  54.2 30.6 %all-to-all-start.1 = ((f32[32,1,1]{2,1,0:T(1,128)}), f32[32,1,1]{2,1,0:T(1,128)S(1)}, u32[]{:S(2)}, u32[]{:S(2)}) async-start(f32[32,1,1]{2,1,0:T(1,128)} %get-tuple-element.8), calls=%async_computation.1 | async-start | bytes 32768 | tf_op jit(solution)/shard_map/all_to_all | solution.py:31
  73.0 10.3 %collective-permute-start.4 = (f32[6,4,4,128]{3,2,1,0:T(4,128)S(1)}, f32[6,4,4,128]{3,2,1,0:T(4,128)S(1)}, u32[]{:S(2)}, u32[]{:S(2)}) collective-permute-start(f32[6,4,4,128]{3,2,1,0:T(4,128)S(1)} %get-tuple-element.16), channel_id=1, source_target_pairs={{0,1020},{1,1021},{2,1022},{3,1023},{4,8},{5,9},{6,10},{7,11},{8,4... | collective-permute-start | bytes 147464 | tf_op jit(solution)/shard_map/ppermute | solution.py:404
  75.5 7.9 %collective-permute-start.5 = (f32[6,4,4,128]{3,2,1,0:T(4,128)S(1)}, f32[6,4,4,128]{3,2,1,0:T(4,128)S(1)}, u32[]{:S(2)}, u32[]{:S(2)}) collective-permute-start(f32[6,4,4,128]{3,2,1,0:T(4,128)S(1)} %get-tuple-element.17), channel_id=1, source_target_pairs={{0,4},{4,0},{8,12},{12,8},{16,20},{20,16},{24,28},{28,24},{1,5},{5... | collective-permute-start | bytes 147464 | tf_op jit(solution)/shard_map/ppermute | solution.py:41
  77.4 7.4 %collective-permute-start.2 = (f32[6,4,16,128]{3,2,1,0:T(8,128)S(1)}, f32[6,4,16,128]{3,2,1,0:T(8,128)S(1)}, u32[]{:S(2)}, u32[]{:S(2)}) collective-permute-start(f32[6,4,16,128]{3,2,1,0:T(8,128)S(1)} %pad_maximum_fusion.own_ref), channel_id=1, source_target_pairs={{0,32},{32,0},{64,96},{96,64},{128,160},{160,128},{192,224},{224,1... | collective-permute-start | bytes 589832 | tf_op jit(solution)/shard_map/ppermute | solution.py:41
  102.5 31.9 %all-to-all-start.3 = ((f32[32,1,1]{2,1,0:T(1,128)}), f32[32,1,1]{2,1,0:T(1,128)S(1)}, u32[]{:S(2)}, u32[]{:S(2)}) async-start(f32[32,1,1]{2,1,0:T(1,128)} %spread.1), calls=%async_computation.3 | async-start | bytes 32768 | tf_op jit(solution)/shard_map/all_to_all | solution.py:411

commit v10 on v9

--- a/solution.py
+++ b/solution.py
@@ -394,16 +394,18 @@
     far_first = ((core == 0) & (chip_row == 0)) | ((core == 1) & (chip_row == lax.axis_size("zl") - 1))
     beside_odd = swap(to_odd, GY, 1)
     ahead_odd = swap(block, GX, 1)
-    beside_even = swap(to_even, GY, 0)
-    column = over_column(to_column, 8)
-    own = cyclic(block, beside_even, beside_odd, odd)
-    by_even = swap(own, GX, 0)
+    column = over_column(to_column, 6)
     low, high = ahead_odd[:, :, :GHOST], ahead_odd[:, :, GHOST:]
-    corner_even = swap(jnp.where(odd, low, high), GY, 0)
+    both = jnp.concatenate([to_even, jnp.where(odd, low, high)], axis=1)
+    both = swap(both, GY, 0)
+    beside_even, corner_even = both[:, :GHOST], both[:, GHOST:]
     kept = jnp.where(far_first, to_odd, beside_odd)
     corner_odd = lax.ppermute(
         jnp.where(far_second, kept, jnp.where(odd, high, low)), ALL, corner_swap()
     )
+    own = cyclic(block, beside_even, beside_odd, odd)
+    by_even = swap(own, GX, 0)
+    corner_even, corner_odd, _ = lax.optimization_barrier((corner_even, corner_odd, own))
     by_odd = cyclic(ahead_odd, corner_even, corner_odd, odd)
     updated, to_plane = hydro_step(column, by_even, own, by_odd, lax.axis_size(PLANE))
     plane = lax.all_to_all(to_plane, PLANE, 0, 0, tiled=True)

time: 137 us -> 153 us (1.12)
  waiting for transfers between devices: 21.5 us -> 30.4 us
  blocking collectives: 37.4 us -> 41.4 us
  starting transfers between devices: 65.9 us -> 68.5 us
    all_to_all x1, starting transfers between devices: 18.7 us -> 26.7 us  [over_column(): lax.all_to_all(value, ALL, 0, 0, axis_index_groups=groups, tiled=True)]
    ppermute x5 -> x4, starting transfers between devices: 33.6 us -> 27 us  [swap(): return lax.ppermute(block, axes, swaps(lax.axis_size(axes))[odd])]
    all_to_all x1, waiting for transfers between devices: 1.42 us -> 6.21 us  [over_column(): lax.all_to_all(value, ALL, 0, 0, axis_index_groups=groups, tiled=True)]
    ppermute x5 -> x4, waiting for transfers between devices: 0.01 us -> 4.1 us  [swap(): return lax.ppermute(block, axes, swaps(lax.axis_size(axes))[odd])]
    all_to_all x1, blocking collectives: 12.2 us -> 16.2 us  [step(): plane = lax.all_to_all(to_plane, PLANE, 0, 0, tiled=True)]
    ppermute x1, starting transfers between devices: 2.44 us -> 6.24 us  [step(): lax.ppermute(jnp.where(far_second, kept, jnp.where(odd, high, low)), ALL,...]
    all_to_all x1, starting transfers between devices: 11.2 us -> 8.57 us  [step(): column = lax.all_to_all(to_column, COLUMN, 0, 0, tiled=True)]
  transfers between devices with their start and end apart: 8 -> 7, of which waited for: 2 -> 3; matrix products, arithmetic and copies ran while one was open for 1% -> 0% of each run, Pallas kernels for 0% -> 0%
where the time goes in v10:
time: 153 us; the launch traced here: 152 us
  starting transfers between devices  68.5 us (45%)
  blocking collectives  41.4 us (27%)
  waiting for transfers between devices  30.4 us (20%)
  Pallas kernels  7.1 us (5%)
  between operations  2.6 us (2%)
  local copies, waits for them, and re-layouts  1.53 us (1%)
    ppermute x4, starting transfers between devices, swap(): return lax.ppermute(block, axes, swaps(lax.axis_size(axes))[odd])  27 us
    all_to_all x1, starting transfers between devices, over_column(): lax.all_to_all(value, ALL, 0, 0, axis_index_groups=groups, tiled=True)  26.7 us
    all_to_all x1, blocking collectives, step(): tiles = lax.all_to_all(packed(conserved_state), PLANE, 0, 0, tiled=True)  25.3 us
    all_to_all x1, waiting for transfers between devices, step(): column = lax.all_to_all(to_column, COLUMN, 0, 0, tiled=True)  20 us
    all_to_all x1, blocking collectives, step(): plane = lax.all_to_all(to_plane, PLANE, 0, 0, tiled=True)  16.2 us
    all_to_all x1, starting transfers between devices, step(): column = lax.all_to_all(to_column, COLUMN, 0, 0, tiled=True)  8.57 us
    ppermute x1, starting transfers between devices, step(): lax.ppermute(jnp.where(far_second, kept, jnp.where(odd, high, low)), ALL,...  6.24 us
    all_to_all x1, waiting for transfers between devices, over_column(): lax.all_to_all(value, ALL, 0, 0, axis_index_groups=groups, tiled=True)  6.21 us
  transfers between devices with their start and end apart: 7, of which 3 were waited for; matrix products, arithmetic and copies ran while one was open for 0% of the time, Pallas kernels for 0%

profile of v10, /device:TPU:1, one launch (start us, length us, event | category | flops | bytes accessed | tf_op | source)
XLA Modules:
  0.0 152.3 jit_solution(4930879217047727407)
XLA Ops:
  0.6 0.0 copy-start
  0.6 0.9 copy-done
  1.5 0.8 pack.1
  2.3 25.3 %all_to_all.20.tiles_ref = f32[32,8,128]{2,1,0:T(8,128)S(1)} all-to-all(f32[32,8,128]{2,1,0:T(8,128)} %pack.1), channel_id=1, replica_groups=mesh['zl'=16,'c'=2,'zh'=2,'x'=4,'y'=4] {'c','x','y'}, dimensions={0} | all-to-all | bytes 262144 | tf_op jit(solution)/shard_map/all_to_all | solution.py:387
  27.6 0.8 unpack.1
  28.4 1.9 %collective-permute-start.1 = (f32[6,4,8,128]{3,2,1,0:T(8,128)S(1)}, f32[6,4,8,128]{3,2,1,0:T(8,128)S(1)}, u32[]{:S(2)}, u32[]{:S(2)}) collective-permute-start(f32[6,4,8,128]{3,2,1,0:T(8,128)S(1)} %get-tuple-element.11), channel_id=1, source_target_pairs={{0,992},{32,64},{64,32},{96,128},{128,96},{160,192},{192,160},{224... | collective-permute-start | bytes 294920 | tf_op jit(solution)/shard_map/ppermute | solution.py:41
  30.3 21.2 %collective-permute-start = (f32[6,4,4,128]{3,2,1,0:T(4,128)S(1)}, f32[6,4,4,128]{3,2,1,0:T(4,128)S(1)}, u32[]{:S(2)}, u32[]{:S(2)}) collective-permute-start(f32[6,4,4,128]{3,2,1,0:T(4,128)S(1)} %get-tuple-element.12), channel_id=1, source_target_pairs={{0,28},{4,8},{8,4},{12,16},{16,12},{20,24},{24,20},{28,0},{1,29},{... | collective-permute-start | bytes 147464 | tf_op jit(solution)/shard_map/ppermute | solution.py:41
  51.6 4.1 %collective-permute-done = f32[6,4,4,128]{3,2,1,0:T(4,128)S(1)} collective-permute-done((f32[6,4,4,128]{3,2,1,0:T(4,128)S(1)}, f32[6,4,4,128]{3,2,1,0:T(4,128)S(1)}, u32[]{:S(2)}, u32[]{:S(2)}) %collective-permute-start) | collective-permute-done | bytes 49184 | tf_op jit(solution)/shard_map/ppermute | solution.py:41
  55.7 0.0 collective-permute-done.1
  55.8 1.9 %collective-permute-start.2 = (f32[6,8,4,128]{3,2,1,0:T(4,128)S(1)}, f32[6,8,4,128]{3,2,1,0:T(4,128)S(1)}, u32[]{:S(2)}, u32[]{:S(2)}) collective-permute-start(f32[6,8,4,128]{3,2,1,0:T(4,128)S(1)} %pad_maximum_fusion.2), channel_id=1, source_target_pairs={{0,4},{4,0},{8,12},{12,8},{16,20},{20,16},{24,28},{28,24},{1,5},{5... | collective-permute-start | bytes 294920 | tf_op jit(solution)/shard_map/ppermute | solution.py:41
  57.7 26.7 %all-to-all-start.1 = ((f32[32,1,1]{2,1,0:T(1,128)}), f32[32,1,1]{2,1,0:T(1,128)S(1)}, u32[]{:S(2)}, u32[]{:S(2)}) async-start(f32[32,1,1]{2,1,0:T(1,128)} %get-tuple-element.10), calls=%async_computation.1 | async-start | bytes 32768 | tf_op jit(solution)/shard_map/all_to_all | solution.py:31
  84.4 6.2 %collective-permute-start.4 = (f32[6,4,4,128]{3,2,1,0:T(4,128)S(1)}, f32[6,4,4,128]{3,2,1,0:T(4,128)S(1)}, u32[]{:S(2)}, u32[]{:S(2)}) collective-permute-start(f32[6,4,4,128]{3,2,1,0:T(4,128)S(1)} %get-tuple-element.22), channel_id=1, source_target_pairs={{0,1020},{1,1021},{2,1022},{3,1023},{4,8},{5,9},{6,10},{7,11},{8,4... | collective-permute-start | bytes 147464 | tf_op jit(solution)/shard_map/ppermute | solution.py:403
  90.6 0.0 collective-permute-done.2
  90.7 1.9 %collective-permute-start.3 = (f32[6,4,16,128]{3,2,1,0:T(8,128)S(1)}, f32[6,4,16,128]{3,2,1,0:T(8,128)S(1)}, u32[]{:S(2)}, u32[]{:S(2)}) collective-permute-start(f32[6,4,16,128]{3,2,1,0:T(8,128)S(1)} %pad_maximum_fusion.own_ref), channel_id=1, source_target_pairs={{0,32},{32,0},{64,96},{96,64},{128,160},{160,128},{192,224},{224,1... | collective-permute-start | bytes 589832 | tf_op jit(solution)/shard_map/ppermute | solution.py:41
  92.6 0.0 collective-permute-done.4
  92.7 6.2 %all-to-all-done.1.column_ref = f32[32,1,1]{2,1,0:T(1,128)S(1)} async-done(((f32[32,1,1]{2,1,0:T(1,128)}), f32[32,1,1]{2,1,0:T(1,128)S(1)}, u32[]{:S(2)}, u32[]{:S(2)}) %all-to-all-start.1) | async-done | bytes 160 | tf_op jit(solution)/shard_map/all_to_all | solution.py:31
  98.9 0.0 collective-permute-done.3.even_ref
  98.9 4.8 %hydro.1 = (f32[6,4,8,120]{3,2,1,0:T(8,128)S(1)}, f32[32,1,1]{2,1,0:T(1,128)S(1)}) custom-call(f32[32,1,1]{2,1,0:T(1,128)S(1)} %all-to-all-done.1.column_ref, f32[6,4,16,128]{3,2,1,0:T(8,128)S(1)} %collective-permute-done.3.even_ref, f32[6,4,16,128]{3,2,1,0:T(8,128)S(1)} %pad_maximum_fusion.own_ref, f32[6,4,16,128]{3,2,1,0:T(8,128)S(1)} %pad_maximum_fusion.1.odd_ref), custom_call_target="tpu_custom_call" | custom-call | tf_op jit(solution)/shard_map/hydro/pallas_call | solution.py:362
  103.8 16.2 %all_to_all.21.everyone_ref = f32[32,1,1]{2,1,0:T(1,128)S(1)} all-to-all(f32[32,1,1]{2,1,0:T(1,128)S(1)} %get-tuple-element.17), channel_id=1, replica_groups=mesh['zl'=16,'c'=2,'zh'=2,'x'=4,'y'=4] {'c','x','y'}, dimensions={0} | all-to-all | bytes 256 | tf_op jit(solution)/shard_map/all_to_all | solution.py:411
  120.0 0.6 spread.1
  120.6 8.6 %all-to-all-start.3 = ((f32[32,1,1]{2,1,0:T(1,128)}), f32[32,1,1]{2,1,0:T(1,128)S(1)}, u32[]{:S(2)}, u32[]{:S(2)}) async-start(f32[32,1,1]{2,1,0:T(1,128)} %spread.1), calls=%async_computation.3 | async-start | bytes 32768 | tf_op jit(solution)/shard_map/all_to_all | solution.py:413
  129.2 0.6 copy.3
  129.8 20.0 %all-to-all-done.3 = f32[32,1,1]{2,1,0:T(1,128)S(1)} async-done(((f32[32,1,1]{2,1,0:T(1,128)}), f32[32,1,1]{2,1,0:T(1,128)S(1)}, u32[]{:S(2)}, u32[]{:S(2)}) %all-to-all-start.3) | async-done | bytes 160 | tf_op jit(solution)/shard_map/all_to_all | solution.py:413
  149.9 0.6 reduce_max.9
  (6 shorter events, 0.1 us)
Async XLA Ops:
  0.6 0.9 copy-start
  28.4 27.3 %collective-permute-start.1 = (f32[6,4,8,128]{3,2,1,0:T(8,128)S(1)}, f32[6,4,8,128]{3,2,1,0:T(8,128)S(1)}, u32[]{:S(2)}, u32[]{:S(2)}) collective-permute-start(f32[6,4,8,128]{3,2,1,0:T(8,128)S(1)} %get-tuple-element.11), channel_id=1, source_target_pairs={{0,992},{32,64},{64,32},{96,128},{128,96},{160,192},{192,160},{224... | collective-permute-start | bytes 294920 | tf_op jit(solution)/shard_map/ppermute | solution.py:41
  30.3 25.4 %collective-permute-start = (f32[6,4,4,128]{3,2,1,0:T(4,128)S(1)}, f32[6,4,4,128]{3,2,1,0:T(4,128)S(1)}, u32[]{:S(2)}, u32[]{:S(2)}) collective-permute-start(f32[6,4,4,128]{3,2,1,0:T(4,128)S(1)} %get-tuple-element.12), channel_id=1, source_target_pairs={{0,28},{4,8},{8,4},{12,16},{16,12},{20,24},{24,20},{28,0},{1,29},{... | collective-permute-start | bytes 147464 | tf_op jit(solution)/shard_map/ppermute | solution.py:41
  55.8 34.9 %collective-permute-start.2 = (f32[6,8,4,128]{3,2,1,0:T(4,128)S(1)}, f32[6,8,4,128]{3,2,1,0:T(4,128)S(1)}, u32[]{:S(2)}, u32[]{:S(2)}) collective-permute-start(f32[6,8,4,128]{3,2,1,0:T(4,128)S(1)} %pad_maximum_fusion.2), channel_id=1, source_target_pairs={{0,4},{4,0},{8,12},{12,8},{16,20},{20,16},{24,28},{28,24},{1,5},{5... | collective-permute-start | bytes 294920 | tf_op jit(solution)/shard_map/ppermute | solution.py:41
  57.7 41.2 %all-to-all-start.1 = ((f32[32,1,1]{2,1,0:T(1,128)}), f32[32,1,1]{2,1,0:T(1,128)S(1)}, u32[]{:S(2)}, u32[]{:S(2)}) async-start(f32[32,1,1]{2,1,0:T(1,128)} %get-tuple-element.10), calls=%async_computation.1 | async-start | bytes 32768 | tf_op jit(solution)/shard_map/all_to_all | solution.py:31
  84.4 8.3 %collective-permute-start.4 = (f32[6,4,4,128]{3,2,1,0:T(4,128)S(1)}, f32[6,4,4,128]{3,2,1,0:T(4,128)S(1)}, u32[]{:S(2)}, u32[]{:S(2)}) collective-permute-start(f32[6,4,4,128]{3,2,1,0:T(4,128)S(1)} %get-tuple-element.22), channel_id=1, source_target_pairs={{0,1020},{1,1021},{2,1022},{3,1023},{4,8},{5,9},{6,10},{7,11},{8,4... | collective-permute-start | bytes 147464 | tf_op jit(solution)/shard_map/ppermute | solution.py:403
  90.7 8.2 %collective-permute-start.3 = (f32[6,4,16,128]{3,2,1,0:T(8,128)S(1)}, f32[6,4,16,128]{3,2,1,0:T(8,128)S(1)}, u32[]{:S(2)}, u32[]{:S(2)}) collective-permute-start(f32[6,4,16,128]{3,2,1,0:T(8,128)S(1)} %pad_maximum_fusion.own_ref), channel_id=1, source_target_pairs={{0,32},{32,0},{64,96},{96,64},{128,160},{160,128},{192,224},{224,1... | collective-permute-start | bytes 589832 | tf_op jit(solution)/shard_map/ppermute | solution.py:41
  120.6 29.3 %all-to-all-start.3 = ((f32[32,1,1]{2,1,0:T(1,128)}), f32[32,1,1]{2,1,0:T(1,128)S(1)}, u32[]{:S(2)}, u32[]{:S(2)}) async-start(f32[32,1,1]{2,1,0:T(1,128)} %spread.1), calls=%async_computation.3 | async-start | bytes 32768 | tf_op jit(solution)/shard_map/all_to_all | solution.py:413

commit v11 on v10

--- a/solution.py
+++ b/solution.py
@@ -163,6 +163,21 @@
     out_ref[...] = jnp.broadcast_to(maximum_of(everyone_ref)[None], out_ref.shape)
 
 
+def timestep_kernel(everyone_ref, out_ref):
+    out_ref[...] = courant / maximum_of(everyone_ref)
+
+
+def timestep(everyone):
+    vmem = pl.BlockSpec(memory_space=pltpu.VMEM)
+    return pl.pallas_call(
+        timestep_kernel,
+        in_specs=[vmem],
+        out_specs=vmem,
+        out_shape=jax.ShapeDtypeStruct((1, 1), jnp.float32),
+        name="timestep",
+    )(*in_vmem(everyone)).reshape(())
+
+
 def spread(everyone, count):
     vmem = pl.BlockSpec(memory_space=pltpu.VMEM)
     return pl.pallas_call(
@@ -394,7 +409,7 @@
     far_first = ((core == 0) & (chip_row == 0)) | ((core == 1) & (chip_row == lax.axis_size("zl") - 1))
     beside_odd = swap(to_odd, GY, 1)
     ahead_odd = swap(block, GX, 1)
-    column = over_column(to_column, 6)
+    column = over_column(to_column, 8)
     low, high = ahead_odd[:, :, :GHOST], ahead_odd[:, :, GHOST:]
     both = jnp.concatenate([to_even, jnp.where(odd, low, high)], axis=1)
     both = swap(both, GY, 0)
@@ -411,7 +426,7 @@
     plane = lax.all_to_all(to_plane, PLANE, 0, 0, tiled=True)
     to_column = spread(plane, lax.axis_size(COLUMN))
     column = lax.all_to_all(to_column, COLUMN, 0, 0, tiled=True)
-    return (updated, courant / jnp.max(column))
+    return (updated, timestep(column))
 
 
 def solution(mesh):

time: 153 us -> 151 us (0.987)
  starting transfers between devices: 68.5 us -> 73.5 us
  blocking collectives: 41.4 us -> 38.4 us
  waiting for transfers between devices: 30.4 us -> 28.5 us
  between operations: 2.6 us -> 0.79 us
    all_to_all x1, starting transfers between devices: 8.57 us -> 11.6 us  [step(): column = lax.all_to_all(to_column, COLUMN, 0, 0, tiled=True)]
    all_to_all x1, blocking collectives: 16.2 us -> 13.1 us  [step(): plane = lax.all_to_all(to_plane, PLANE, 0, 0, tiled=True)]
    ppermute x1, starting transfers between devices: 6.24 us -> 3.24 us  [step(): lax.ppermute(jnp.where(far_second, kept, jnp.where(odd, high, low)), ALL,...]
    all_to_all x1, starting transfers between devices: 26.7 us -> 29.6 us  [over_column(): lax.all_to_all(value, ALL, 0, 0, axis_index_groups=groups, tiled=True)]
    ppermute x4, starting transfers between devices: 27 us -> 28.9 us  [swap(): return lax.ppermute(block, axes, swaps(lax.axis_size(axes))[odd])]
    all_to_all x1, waiting for transfers between devices: 6.21 us -> 4.3 us  [over_column(): lax.all_to_all(value, ALL, 0, 0, axis_index_groups=groups, tiled=True)]
where the time goes in v11:
time: 151 us; the launch traced here: 150 us
  starting transfers between devices  73.5 us (49%)
  blocking collectives  38.4 us (25%)
  waiting for transfers between devices  28.5 us (19%)
  Pallas kernels  7.66 us (5%)
  local copies, waits for them, and re-layouts  1.53 us (1%)
    all_to_all x1, starting transfers between devices, over_column(): lax.all_to_all(value, ALL, 0, 0, axis_index_groups=groups, tiled=True)  29.6 us
    ppermute x4, starting transfers between devices, swap(): return lax.ppermute(block, axes, swaps(lax.axis_size(axes))[odd])  28.9 us
    all_to_all x1, blocking collectives, step(): tiles = lax.all_to_all(packed(conserved_state), PLANE, 0, 0, tiled=True)  25.3 us
    all_to_all x1, waiting for transfers between devices, step(): column = lax.all_to_all(to_column, COLUMN, 0, 0, tiled=True)  20 us
    all_to_all x1, blocking collectives, step(): plane = lax.all_to_all(to_plane, PLANE, 0, 0, tiled=True)  13.1 us
    all_to_all x1, starting transfers between devices, step(): column = lax.all_to_all(to_column, COLUMN, 0, 0, tiled=True)  11.6 us
    pallas_call x1, Pallas kernels, hydro_step(): pl.pallas_call(kernel, in_specs=[vmem] * 4, out_specs=[vmem, vmem], out_s...  4.85 us
    all_to_all x1, waiting for transfers between devices, over_column(): lax.all_to_all(value, ALL, 0, 0, axis_index_groups=groups, tiled=True)  4.3 us
  transfers between devices with their start and end apart: 7, of which 3 were waited for; matrix products, arithmetic and copies ran while one was open for 0% of the time, Pallas kernels for 0%

profile of v11, /device:TPU:1, one launch (start us, length us, event | category | flops | bytes accessed | tf_op | source)
XLA Modules:
  0.0 150.5 jit_solution(648457674271309231)
XLA Ops:
  0.6 0.0 copy-start
  0.6 0.9 copy-done
  1.5 0.8 pack.1
  2.3 25.3 %all_to_all.20.tiles_ref = f32[32,8,128]{2,1,0:T(8,128)S(1)} all-to-all(f32[32,8,128]{2,1,0:T(8,128)} %pack.1), channel_id=1, replica_groups=mesh['zl'=16,'c'=2,'zh'=2,'x'=4,'y'=4] {'c','x','y'}, dimensions={0} | all-to-all | bytes 262144 | tf_op jit(solution)/shard_map/all_to_all | solution.py:402
  27.6 0.8 unpack.1
  28.4 1.9 %collective-permute-start.1 = (f32[6,4,8,128]{3,2,1,0:T(8,128)S(1)}, f32[6,4,8,128]{3,2,1,0:T(8,128)S(1)}, u32[]{:S(2)}, u32[]{:S(2)}) collective-permute-start(f32[6,4,8,128]{3,2,1,0:T(8,128)S(1)} %get-tuple-element.11), channel_id=1, source_target_pairs={{0,992},{32,64},{64,32},{96,128},{128,96},{160,192},{192,160},{224... | collective-permute-start | bytes 294920 | tf_op jit(solution)/shard_map/ppermute | solution.py:41
  30.3 21.2 %collective-permute-start = (f32[6,4,4,128]{3,2,1,0:T(4,128)S(1)}, f32[6,4,4,128]{3,2,1,0:T(4,128)S(1)}, u32[]{:S(2)}, u32[]{:S(2)}) collective-permute-start(f32[6,4,4,128]{3,2,1,0:T(4,128)S(1)} %get-tuple-element.12), channel_id=1, source_target_pairs={{0,28},{4,8},{8,4},{12,16},{16,12},{20,24},{24,20},{28,0},{1,29},{... | collective-permute-start | bytes 147464 | tf_op jit(solution)/shard_map/ppermute | solution.py:41
  51.6 4.1 %collective-permute-done = f32[6,4,4,128]{3,2,1,0:T(4,128)S(1)} collective-permute-done((f32[6,4,4,128]{3,2,1,0:T(4,128)S(1)}, f32[6,4,4,128]{3,2,1,0:T(4,128)S(1)}, u32[]{:S(2)}, u32[]{:S(2)}) %collective-permute-start) | collective-permute-done | bytes 49184 | tf_op jit(solution)/shard_map/ppermute | solution.py:41
  55.7 0.0 collective-permute-done.1
  55.8 1.9 %collective-permute-start.2 = (f32[6,8,4,128]{3,2,1,0:T(4,128)S(1)}, f32[6,8,4,128]{3,2,1,0:T(4,128)S(1)}, u32[]{:S(2)}, u32[]{:S(2)}) collective-permute-start(f32[6,8,4,128]{3,2,1,0:T(4,128)S(1)} %pad_maximum_fusion.2), channel_id=1, source_target_pairs={{0,4},{4,0},{8,12},{12,8},{16,20},{20,16},{24,28},{28,24},{1,5},{5... | collective-permute-start | bytes 294920 | tf_op jit(solution)/shard_map/ppermute | solution.py:41
  57.7 29.6 %all-to-all-start.1 = ((f32[32,1,1]{2,1,0:T(1,128)}), f32[32,1,1]{2,1,0:T(1,128)S(1)}, u32[]{:S(2)}, u32[]{:S(2)}) async-start(f32[32,1,1]{2,1,0:T(1,128)} %get-tuple-element.10), calls=%async_computation.1 | async-start | bytes 32768 | tf_op jit(solution)/shard_map/all_to_all | solution.py:31
  87.4 3.2 %collective-permute-start.4 = (f32[6,4,4,128]{3,2,1,0:T(4,128)S(1)}, f32[6,4,4,128]{3,2,1,0:T(4,128)S(1)}, u32[]{:S(2)}, u32[]{:S(2)}) collective-permute-start(f32[6,4,4,128]{3,2,1,0:T(4,128)S(1)} %get-tuple-element.22), channel_id=1, source_target_pairs={{0,1020},{1,1021},{2,1022},{3,1023},{4,8},{5,9},{6,10},{7,11},{8,4... | collective-permute-start | bytes 147464 | tf_op jit(solution)/shard_map/ppermute | solution.py:418
  90.6 0.0 collective-permute-done.2
  90.7 3.9 %collective-permute-start.3 = (f32[6,4,16,128]{3,2,1,0:T(8,128)S(1)}, f32[6,4,16,128]{3,2,1,0:T(8,128)S(1)}, u32[]{:S(2)}, u32[]{:S(2)}) collective-permute-start(f32[6,4,16,128]{3,2,1,0:T(8,128)S(1)} %pad_maximum_fusion.own_ref), channel_id=1, source_target_pairs={{0,32},{32,0},{64,96},{96,64},{128,160},{160,128},{192,224},{224,1... | collective-permute-start | bytes 589832 | tf_op jit(solution)/shard_map/ppermute | solution.py:41
  94.6 0.0 collective-permute-done.4
  94.6 4.3 %all-to-all-done.1.column_ref = f32[32,1,1]{2,1,0:T(1,128)S(1)} async-done(((f32[32,1,1]{2,1,0:T(1,128)}), f32[32,1,1]{2,1,0:T(1,128)S(1)}, u32[]{:S(2)}, u32[]{:S(2)}) %all-to-all-start.1) | async-done | bytes 160 | tf_op jit(solution)/shard_map/all_to_all | solution.py:31
  98.9 0.0 collective-permute-done.3.even_ref
  98.9 4.8 %hydro.1 = (f32[6,4,8,120]{3,2,1,0:T(8,128)S(1)}, f32[32,1,1]{2,1,0:T(1,128)S(1)}) custom-call(f32[32,1,1]{2,1,0:T(1,128)S(1)} %all-to-all-done.1.column_ref, f32[6,4,16,128]{3,2,1,0:T(8,128)S(1)} %collective-permute-done.3.even_ref, f32[6,4,16,128]{3,2,1,0:T(8,128)S(1)} %pad_maximum_fusion.own_ref, f32[6,4,16,128]{3,2,1,0:T(8,128)S(1)} %pad_maximum_fusion.1.odd_ref), custom_call_target="tpu_custom_call" | custom-call | tf_op jit(solution)/shard_map/hydro/pallas_call | solution.py:377
  103.8 13.1 %all_to_all.21.everyone_ref = f32[32,1,1]{2,1,0:T(1,128)S(1)} all-to-all(f32[32,1,1]{2,1,0:T(1,128)S(1)} %get-tuple-element.17), channel_id=1, replica_groups=mesh['zl'=16,'c'=2,'zh'=2,'x'=4,'y'=4] {'c','x','y'}, dimensions={0} | all-to-all | bytes 256 | tf_op jit(solution)/shard_map/all_to_all | solution.py:426
  116.9 0.6 spread.1
  117.6 11.6 %all-to-all-start.3 = ((f32[32,1,1]{2,1,0:T(1,128)}), f32[32,1,1]{2,1,0:T(1,128)S(1)}, u32[]{:S(2)}, u32[]{:S(2)}) async-start(f32[32,1,1]{2,1,0:T(1,128)} %spread.1), calls=%async_computation.3 | async-start | bytes 32768 | tf_op jit(solution)/shard_map/all_to_all | solution.py:428
  129.2 0.6 copy.3
  129.9 20.0 %all-to-all-done.3.everyone_ref = f32[32,1,1]{2,1,0:T(1,128)S(1)} async-done(((f32[32,1,1]{2,1,0:T(1,128)}), f32[32,1,1]{2,1,0:T(1,128)S(1)}, u32[]{:S(2)}, u32[]{:S(2)}) %all-to-all-start.3) | async-done | bytes 160 | tf_op jit(solution)/shard_map/all_to_all | solution.py:428
  149.9 0.6 timestep.1
  (6 shorter events, 0.1 us)
Async XLA Ops:
  0.6 0.9 copy-start
  28.4 27.3 %collective-permute-start.1 = (f32[6,4,8,128]{3,2,1,0:T(8,128)S(1)}, f32[6,4,8,128]{3,2,1,0:T(8,128)S(1)}, u32[]{:S(2)}, u32[]{:S(2)}) collective-permute-start(f32[6,4,8,128]{3,2,1,0:T(8,128)S(1)} %get-tuple-element.11), channel_id=1, source_target_pairs={{0,992},{32,64},{64,32},{96,128},{128,96},{160,192},{192,160},{224... | collective-permute-start | bytes 294920 | tf_op jit(solution)/shard_map/ppermute | solution.py:41
  30.3 25.4 %collective-permute-start = (f32[6,4,4,128]{3,2,1,0:T(4,128)S(1)}, f32[6,4,4,128]{3,2,1,0:T(4,128)S(1)}, u32[]{:S(2)}, u32[]{:S(2)}) collective-permute-start(f32[6,4,4,128]{3,2,1,0:T(4,128)S(1)} %get-tuple-element.12), channel_id=1, source_target_pairs={{0,28},{4,8},{8,4},{12,16},{16,12},{20,24},{24,20},{28,0},{1,29},{... | collective-permute-start | bytes 147464 | tf_op jit(solution)/shard_map/ppermute | solution.py:41
  55.8 34.8 %collective-permute-start.2 = (f32[6,8,4,128]{3,2,1,0:T(4,128)S(1)}, f32[6,8,4,128]{3,2,1,0:T(4,128)S(1)}, u32[]{:S(2)}, u32[]{:S(2)}) collective-permute-start(f32[6,8,4,128]{3,2,1,0:T(4,128)S(1)} %pad_maximum_fusion.2), channel_id=1, source_target_pairs={{0,4},{4,0},{8,12},{12,8},{16,20},{20,16},{24,28},{28,24},{1,5},{5... | collective-permute-start | bytes 294920 | tf_op jit(solution)/shard_map/ppermute | solution.py:41
  57.7 41.2 %all-to-all-start.1 = ((f32[32,1,1]{2,1,0:T(1,128)}), f32[32,1,1]{2,1,0:T(1,128)S(1)}, u32[]{:S(2)}, u32[]{:S(2)}) async-start(f32[32,1,1]{2,1,0:T(1,128)} %get-tuple-element.10), calls=%async_computation.1 | async-start | bytes 32768 | tf_op jit(solution)/shard_map/all_to_all | solution.py:31
  87.4 7.2 %collective-permute-start.4 = (f32[6,4,4,128]{3,2,1,0:T(4,128)S(1)}, f32[6,4,4,128]{3,2,1,0:T(4,128)S(1)}, u32[]{:S(2)}, u32[]{:S(2)}) collective-permute-start(f32[6,4,4,128]{3,2,1,0:T(4,128)S(1)} %get-tuple-element.22), channel_id=1, source_target_pairs={{0,1020},{1,1021},{2,1022},{3,1023},{4,8},{5,9},{6,10},{7,11},{8,4... | collective-permute-start | bytes 147464 | tf_op jit(solution)/shard_map/ppermute | solution.py:418
  90.7 8.2 %collective-permute-start.3 = (f32[6,4,16,128]{3,2,1,0:T(8,128)S(1)}, f32[6,4,16,128]{3,2,1,0:T(8,128)S(1)}, u32[]{:S(2)}, u32[]{:S(2)}) collective-permute-start(f32[6,4,16,128]{3,2,1,0:T(8,128)S(1)} %pad_maximum_fusion.own_ref), channel_id=1, source_target_pairs={{0,32},{32,0},{64,96},{96,64},{128,160},{160,128},{192,224},{224,1... | collective-permute-start | bytes 589832 | tf_op jit(solution)/shard_map/ppermute | solution.py:41
  117.6 32.3 %all-to-all-start.3 = ((f32[32,1,1]{2,1,0:T(1,128)}), f32[32,1,1]{2,1,0:T(1,128)S(1)}, u32[]{:S(2)}, u32[]{:S(2)}) async-start(f32[32,1,1]{2,1,0:T(1,128)} %spread.1), calls=%async_computation.3 | async-start | bytes 32768 | tf_op jit(solution)/shard_map/all_to_all | solution.py:428
